TPU v7x, 32 devices: a whole 2x2x4 slice. The times are simulated.
32 devices in a mesh: head: 4 (over x, core), blk: 8 (over z, y).
Axes of the slice: x: 2, y: 2, z: 4, core: 2. Of those that a mesh axis runs over, the one named last changes fastest.
Arguments:
- tokens: bfloat16 [4096, 2048], P(('head', 'blk')), may hold values from -6 to 6
- norm1_gain: float32 [2048], replicated, may hold values from 0.5 to 1.5
- norm1_bias: float32 [2048], replicated, may hold values from -3 to 3
- w_qkv: bfloat16 [2048, 3, 2048], P('blk', None, 'head'), may hold values from -0.125 to 0.125
- qkv_bias: float32 [3, 2048], P(None, 'head'), may hold values from -3 to 3
- w_out: bfloat16 [2048, 2048], P('head', 'blk'), may hold values from -0.5 to 0.5
- norm2_gain: float32 [2048], replicated, may hold values from 0.5 to 1.5
- norm2_bias: float32 [2048], replicated, may hold values from -3 to 3
- w_gate: bfloat16 [2048, 5632], P('blk', 'head'), may hold values from -0.125 to 0.125
- w_up: bfloat16 [2048, 5632], P('blk', 'head'), may hold values from -0.125 to 0.125
- w_down: bfloat16 [5632, 2048], P('head', 'blk'), may hold values from -0.078125 to 0.078125
- cotangent: bfloat16 [4096, 2048], P(('head', 'blk')), may hold values from -6 to 6
- seq_lengths: int32 [8], replicated, may hold values from 1 to 2048, 4096 in all
- block_order: int32 [32], replicated, may hold values from 0 to 31, each once
Outputs:
- output: bfloat16 [4096, 2048], P(('head', 'blk'))
- input_grad: float32 [4096, 2048], P(('head', 'blk'))
- norm1_gain_grad: float32 [2048], P(('head', 'blk'))
- norm1_bias_grad: float32 [2048], P(('head', 'blk'))
- w_qkv_grad: float32 [2048, 3, 2048], P('blk', None, 'head')
- qkv_bias_grad: float32 [3, 2048], P(None, ('head', 'blk'))
- w_out_grad: float32 [2048, 2048], P('head', 'blk')
- norm2_gain_grad: float32 [2048], P(('head', 'blk'))
- norm2_bias_grad: float32 [2048], P(('head', 'blk'))
- w_gate_grad: float32 [2048, 5632], P('blk', 'head')
- w_up_grad: float32 [2048, 5632], P('blk', 'head')
- w_down_grad: float32 [5632, 2048], P('head', 'blk')
Inputs may be any that keep to these rules, and one draw needn't show every extreme that they name: `seq_lengths`: 8 sequences lie end to end over the packed positions 0 to 4095 in this order; the longest has exactly 2048 tokens. Each block number appears once; rows j * 128 to j * 128 + 127 of tokens and cotangent are packed block block_order[j].
All inputs are finite; a program needn't handle non-finite values.
Results may differ from a plain program's by a relative error of at most 0.019.
Values may be sent and summed in bfloat16 or wider, within the bound.
A program may use at most 320 MiB of HBM per device.

v0:
```python
import jax
import jax.numpy as jnp
from jax import lax
from jax.sharding import PartitionSpec as P

HD = 64
ROT = 16
BLOCK = 128


EPSILON = 1e-05
MASKED = -1000000000.0


def contract_rows(left, right):
    return lax.dot_general(
        left, right, (((0,), (0,)), ((), ())), preferred_element_type=jnp.float32
    )


def times_transpose(left, right):
    return lax.dot_general(
        left, right, (((1,), (1,)), ((), ())), preferred_element_type=jnp.float32
    )


def packed_positions(row_ids, block_order):
    block_ids = jnp.arange(block_order.shape[0], dtype=jnp.int32)
    matches = (row_ids // BLOCK)[:, None] == block_ids[None, :]
    block_start = jnp.sum(jnp.where(matches, block_order[None, :], 0), axis=1)
    return block_start * BLOCK + row_ids % BLOCK


def sequence_start(position, seq_lengths):
    seq_ends = jnp.cumsum(seq_lengths)
    ends_before = seq_ends[None, :] <= position[:, None]
    return jnp.sum(jnp.where(ends_before, seq_lengths[None, :], 0), axis=1)


def rotate(values, cosine, sine_table):
    half_rot = ROT // 2
    lead_part = values[..., :half_rot]
    tail_part = values[..., half_rot:ROT]
    cos_rows = cosine[:, None, :]
    sin_rows = sine_table[:, None, :]
    return jnp.concatenate(
        [
            lead_part * cos_rows - tail_part * sin_rows,
            tail_part * cos_rows + lead_part * sin_rows,
            values[..., ROT:],
        ],
        axis=-1,
    )


def normalize(values, norm_gain, norm_shift):
    centre = values - jnp.mean(values, axis=-1, keepdims=True)
    inv_scale = lax.rsqrt(jnp.mean(centre * centre, axis=-1, keepdims=True) + EPSILON)
    unit_rows = centre * inv_scale
    return (unit_rows * norm_gain + norm_shift, unit_rows, inv_scale)


def normalize_back(grad_norm, unit_rows, inv_scale, norm_gain):
    grad_unit = grad_norm * norm_gain
    mean_grad = jnp.mean(grad_unit, axis=-1, keepdims=True)
    mean_proj = jnp.mean(grad_unit * unit_rows, axis=-1, keepdims=True)
    return inv_scale * (grad_unit - mean_grad - unit_rows * mean_proj)


def gather_keys(keys_flat, values_flat):
    return (
        lax.all_gather(keys_flat, "blk", axis=0, tiled=True),
        lax.all_gather(values_flat, "blk", axis=0, tiled=True),
    )


def tile_count_of(total_rows):
    tile_rows = min(1024, total_rows)
    return (total_rows // tile_rows, tile_rows)


def key_tiles(keys_all, values_all, key_pos, heads_local):
    tile_count, tile_rows = tile_count_of(keys_all.shape[0])
    return (
        keys_all.reshape(tile_count, tile_rows, heads_local, HD),
        values_all.reshape(tile_count, tile_rows, heads_local, HD),
        key_pos.reshape(tile_count, tile_rows),
    )


def masked_scores(queries, key_tile, pos_tile, query_pos, query_start):
    raw_scores = jnp.einsum(
        "qhd,khd->hqk", queries, key_tile, preferred_element_type=jnp.float32
    ) * HD ** (-0.5)
    allowed = (pos_tile[None, :] <= query_pos[:, None]) & (
        pos_tile[None, :] >= query_start[:, None]
    )
    return jnp.where(allowed[None], raw_scores, MASKED)


def attend(queries, tiles, query_pos, query_start):
    group_rows = queries.shape[0]
    heads_local = queries.shape[1]

    def first_pass(run_state, tile):
        run_max, run_sum = run_state
        scores = masked_scores(queries, tile[0], tile[2], query_pos, query_start)
        new_max = jnp.maximum(run_max, jnp.max(scores, axis=-1))
        new_sum = run_sum * jnp.exp(run_max - new_max) + jnp.sum(
            jnp.exp(scores - new_max[..., None]), axis=-1
        )
        return ((new_max, new_sum), None)

    start_state = (
        jnp.full((heads_local, group_rows), -3e38, jnp.float32),
        jnp.zeros((heads_local, group_rows), jnp.float32),
    )
    (run_max, run_sum), unused = lax.scan(first_pass, start_state, tiles)
    log_norm = run_max + jnp.log(run_sum)

    def second_pass(totals, tile):
        total_out, total_rest = totals
        scores = masked_scores(queries, tile[0], tile[2], query_pos, query_start)
        probs_f32 = jnp.exp(scores - log_norm[..., None])
        probs_b = probs_f32.astype(jnp.bfloat16)
        rest_b = (probs_f32 - probs_b.astype(jnp.float32)).astype(jnp.bfloat16)
        total_out = total_out + jnp.einsum(
            "hqk,khd->qhd", probs_b, tile[1], preferred_element_type=jnp.float32
        )
        total_rest = total_rest + jnp.einsum(
            "hqk,khd->qhd", rest_b, tile[1], preferred_element_type=jnp.float32
        )
        return ((total_out, total_rest), None)

    empty = jnp.zeros((group_rows, heads_local, HD), jnp.float32)
    (attended, leftover), unused = lax.scan(second_pass, (empty, empty), tiles)
    return (attended, attended + leftover, log_norm)


def attend_back(queries, tiles, query_pos, query_start, log_norm, grad_attn, delta_rows):
    scale = HD ** (-0.5)

    def step_back(grad_query, tile):
        key_tile, value_tile, pos_tile = tile
        scores = masked_scores(queries, key_tile, pos_tile, query_pos, query_start)
        probs_f32 = jnp.exp(scores - log_norm[..., None])
        grad_probs = jnp.einsum(
            "qhd,khd->hqk", grad_attn, value_tile, preferred_element_type=jnp.float32
        )
        grad_scores = (probs_f32 * (grad_probs - delta_rows[..., None])).astype(jnp.bfloat16)
        probs_b = probs_f32.astype(jnp.bfloat16)
        grad_query = grad_query + scale * jnp.einsum(
            "hqk,khd->qhd", grad_scores, key_tile, preferred_element_type=jnp.float32
        )
        grad_key = scale * jnp.einsum(
            "hqk,qhd->khd", grad_scores, queries, preferred_element_type=jnp.float32
        )
        grad_value = jnp.einsum(
            "hqk,qhd->khd", probs_b, grad_attn, preferred_element_type=jnp.float32
        )
        return (grad_query, (grad_key, grad_value))

    grad_query, (grad_keys, grad_values) = lax.scan(
        step_back, jnp.zeros(queries.shape, jnp.float32), tiles
    )
    return (grad_query, grad_keys, grad_values)


def on_device(
    tokens,
    norm1_gain,
    norm1_bias,
    w_qkv,
    qkv_bias,
    w_out,
    norm2_gain,
    norm2_bias,
    w_gate,
    w_up,
    w_down,
    cotangent,
    seq_lengths,
    block_order,
):
    team_count = lax.axis_size("head")
    span_count = lax.axis_size("blk")
    span_index = lax.axis_index("blk")
    tok_rows = tokens.shape[0]
    model_width = tokens.shape[1]
    group_rows = tok_rows * team_count
    local_width = w_out.shape[0]
    heads_local = local_width // HD
    offsets = jnp.arange(tok_rows, dtype=jnp.int32)
    member = jnp.arange(team_count, dtype=jnp.int32)
    owner_index = jnp.arange(span_count, dtype=jnp.int32)
    query_ids = ((member[:, None] * span_count + span_index) * tok_rows + offsets[None, :]).reshape(
        -1
    )
    key_ids = (
        (member[None, :, None] * span_count + owner_index[:, None, None]) * tok_rows
        + offsets[None, None, :]
    ).reshape(-1)
    query_pos = packed_positions(query_ids, block_order)
    query_start = sequence_start(query_pos, seq_lengths)
    key_pos = packed_positions(key_ids, block_order)
    half_rot = ROT // 2
    freq_table = jnp.power(10000.0, -2.0 * jnp.arange(half_rot, dtype=jnp.float32) / ROT)
    angles = (query_pos - query_start).astype(jnp.float32)[:, None] * freq_table[None, :]
    cosine = jnp.cos(angles)
    sine_table = jnp.sin(angles)
    x_own = tokens.astype(jnp.float32)
    norm1_out, unit_one, inv_one = normalize(x_own, norm1_gain, norm1_bias)
    norm1_group = lax.all_gather(norm1_out.astype(jnp.bfloat16), "head", axis=0, tiled=True)
    qkv_full, out_full = (
        lax.all_gather(w_qkv, "blk", axis=0, tiled=True),
        lax.all_gather(w_out, "blk", axis=1, tiled=True),
    )
    qkv_matrix = qkv_full.reshape(model_width, 3 * local_width)
    projected = jnp.dot(
        norm1_group, qkv_matrix, preferred_element_type=jnp.float32
    ) + qkv_bias.reshape(1, -1)
    projected = projected.reshape(group_rows, 3, heads_local, HD)
    queries = rotate(projected[:, 0], cosine, sine_table).astype(jnp.bfloat16)
    keys_flat = (
        rotate(projected[:, 1], cosine, sine_table)
        .astype(jnp.bfloat16)
        .reshape(group_rows, local_width)
    )
    values_flat = projected[:, 2].astype(jnp.bfloat16).reshape(group_rows, local_width)
    keys_all, values_all = gather_keys(keys_flat, values_flat)
    attn_out, attn_exact, log_norm = attend(
        queries, key_tiles(keys_all, values_all, key_pos, heads_local), query_pos, query_start
    )
    attn_b = attn_out.reshape(group_rows, local_width).astype(jnp.bfloat16)
    attn_own = lax.psum_scatter(
        jnp.dot(attn_b, out_full, preferred_element_type=jnp.float32),
        "head",
        scatter_dimension=0,
        tiled=True,
    )
    hidden = x_own + attn_own
    norm2_out, unit_two, inv_two = normalize(hidden, norm2_gain, norm2_bias)
    norm2_group = lax.all_gather(norm2_out.astype(jnp.bfloat16), "head", axis=0, tiled=True)
    gate_full, up_full, down_full = (
        lax.all_gather(w_gate, "blk", axis=0, tiled=True),
        lax.all_gather(w_up, "blk", axis=0, tiled=True),
        lax.all_gather(w_down, "blk", axis=1, tiled=True),
    )
    gate_val = jnp.dot(norm2_group, gate_full, preferred_element_type=jnp.float32)
    up_val = jnp.dot(norm2_group, up_full, preferred_element_type=jnp.float32)
    sigmoid_gate = jax.nn.sigmoid(gate_val)
    swish_val = gate_val * sigmoid_gate
    activ_b = (swish_val * up_val).astype(jnp.bfloat16)
    mlp_own = lax.psum_scatter(
        jnp.dot(activ_b, down_full, preferred_element_type=jnp.float32).astype(jnp.bfloat16),
        "head",
        scatter_dimension=0,
        tiled=True,
    ).astype(jnp.float32)
    output = (hidden + mlp_own).astype(jnp.bfloat16)
    grad_out = cotangent.astype(jnp.float32)
    grad_group = lax.all_gather(cotangent, "head", axis=0, tiled=True)
    grad_activ = times_transpose(grad_group, down_full)
    grad_w_down = contract_rows(activ_b, grad_group)
    grad_up_b = (grad_activ * swish_val).astype(jnp.bfloat16)
    grad_gate_b = (
        grad_activ * up_val * sigmoid_gate * (1.0 + gate_val * (1.0 - sigmoid_gate))
    ).astype(jnp.bfloat16)
    grad_w_gate = contract_rows(norm2_group, grad_gate_b)
    grad_w_up = contract_rows(norm2_group, grad_up_b)
    grad_norm2 = lax.psum_scatter(
        times_transpose(grad_gate_b, gate_full) + times_transpose(grad_up_b, up_full),
        "head",
        scatter_dimension=0,
        tiled=True,
    )
    grad_hidden = grad_out + normalize_back(grad_norm2, unit_two, inv_two, norm2_gain)
    gain_two_grad = jnp.sum(grad_norm2 * unit_two, axis=0)
    shift_two_grad = jnp.sum(grad_norm2, axis=0)
    branch_group = lax.all_gather(grad_hidden.astype(jnp.bfloat16), "head", axis=0, tiled=True)
    grad_w_out = contract_rows(attn_b, branch_group)
    grad_attn = (
        times_transpose(branch_group, out_full)
        .astype(jnp.bfloat16)
        .reshape(group_rows, heads_local, HD)
    )
    delta_rows = jnp.sum(grad_attn.astype(jnp.float32) * attn_exact, axis=-1).T
    keys_back_all, values_back_all = gather_keys(keys_flat, values_flat)
    tiles_back = key_tiles(keys_back_all, values_back_all, key_pos, heads_local)
    grad_query, grad_keys, grad_values = attend_back(
        queries, tiles_back, query_pos, query_start, log_norm, grad_attn, delta_rows
    )
    key_terms = grad_keys.reshape(-1, local_width)
    value_terms = grad_values.reshape(-1, local_width)
    grad_key_own, grad_value_own = (
        lax.psum_scatter(
            key_terms.astype(jnp.bfloat16), "blk", scatter_dimension=0, tiled=True
        ).astype(jnp.float32),
        lax.psum_scatter(
            value_terms.astype(jnp.bfloat16), "blk", scatter_dimension=0, tiled=True
        ).astype(jnp.float32),
    )
    grad_query_pre = rotate(grad_query, cosine, -sine_table).reshape(group_rows, local_width)
    grad_key_pre = rotate(
        grad_key_own.reshape(group_rows, heads_local, HD), cosine, -sine_table
    ).reshape(group_rows, local_width)
    grad_proj_b = jnp.stack([grad_query_pre, grad_key_pre, grad_value_own], axis=1).astype(
        jnp.bfloat16
    )
    bias_grad = jnp.sum(grad_proj_b.astype(jnp.float32), axis=0)
    grad_proj_flat = grad_proj_b.reshape(group_rows, 3 * local_width)
    grad_w_qkv = contract_rows(norm1_group, grad_proj_flat).reshape(model_width, 3, local_width)
    grad_norm1 = lax.psum_scatter(
        times_transpose(grad_proj_flat, qkv_matrix).astype(jnp.bfloat16),
        "head",
        scatter_dimension=0,
        tiled=True,
    ).astype(jnp.float32)
    input_grad = grad_hidden + normalize_back(grad_norm1, unit_one, inv_one, norm1_gain)
    gain_one_grad = jnp.sum(grad_norm1 * unit_one, axis=0)
    shift_one_grad = jnp.sum(grad_norm1, axis=0)
    norm_sums = (
        lax.psum_scatter(gain_one_grad, ("head", "blk"), scatter_dimension=0, tiled=True),
        lax.psum_scatter(shift_one_grad, ("head", "blk"), scatter_dimension=0, tiled=True),
        lax.psum_scatter(gain_two_grad, ("head", "blk"), scatter_dimension=0, tiled=True),
        lax.psum_scatter(shift_two_grad, ("head", "blk"), scatter_dimension=0, tiled=True),
    )
    grad_shards = (
        lax.psum_scatter(
            grad_w_qkv.astype(jnp.bfloat16), "blk", scatter_dimension=0, tiled=True
        ).astype(jnp.float32),
        lax.psum_scatter(
            bias_grad.astype(jnp.bfloat16), "blk", scatter_dimension=1, tiled=True
        ).astype(jnp.float32),
        lax.psum_scatter(
            grad_w_out.astype(jnp.bfloat16), "blk", scatter_dimension=1, tiled=True
        ).astype(jnp.float32),
        lax.psum_scatter(
            grad_w_gate.astype(jnp.bfloat16), "blk", scatter_dimension=0, tiled=True
        ).astype(jnp.float32),
        lax.psum_scatter(
            grad_w_up.astype(jnp.bfloat16), "blk", scatter_dimension=0, tiled=True
        ).astype(jnp.float32),
        lax.psum_scatter(
            grad_w_down.astype(jnp.bfloat16), "blk", scatter_dimension=1, tiled=True
        ).astype(jnp.float32),
    )
    return (
        output,
        input_grad,
        norm_sums[0],
        norm_sums[1],
        grad_shards[0],
        grad_shards[1],
        grad_shards[2],
        norm_sums[2],
        norm_sums[3],
        grad_shards[3],
        grad_shards[4],
        grad_shards[5],
    )


def solution(mesh):
    placed = (
        P(("head", "blk"), None),
        P(),
        P(),
        P("blk", None, "head"),
        P(None, "head"),
        P("head", "blk"),
        P(),
        P(),
        P("blk", "head"),
        P("blk", "head"),
        P("head", "blk"),
        P(("head", "blk"), None),
        P(),
        P(),
    )
    return jax.shard_map(
        on_device,
        mesh=mesh,
        in_specs=placed,
        out_specs=(
            P(("head", "blk"), None),
            P(("head", "blk"), None),
            P(("head", "blk")),
            P(("head", "blk")),
            P("blk", None, "head"),
            P(None, ("head", "blk")),
            P("head", "blk"),
            P(("head", "blk")),
            P(("head", "blk")),
            P("blk", "head"),
            P("blk", "head"),
            P("head", "blk"),
        ),
        check_vma=False,
    )
```

profile of v0, /device:TPU:0, one launch (start us, length us, event | category | flops | bytes accessed | tf_op | source)
XLA Modules:
  0.0 1931.6 jit_solution(8082596680562907784)
XLA Ops:
  14.1 97.6 %all-gather.14.cloned.1.call-done = bf16[2048,3,512]{2,0,1:T(8,128)(2,1)} async-done(((bf16[256,3,512]{2,0,1:T(8,128)(2,1)}), bf16[2048,3,512]{2,0,1:T(8,128)(2,1)}) %all-gather.14.cloned.1.call-update) | async-done | bytes 6291472 | tf_op jit(solution)/shard_map/all_gather | solution.py:215
  111.6 8.9 copy.80
  120.5 14.0 all-gather.12.cloned.1.call-done
  152.3 68.9 %all-gather.16.cloned.1.call-done = bf16[4096,512]{0,1:T(8,128)(2,1)} async-done(((bf16[512,512]{0,1:T(8,128)(2,1)}), bf16[4096,512]{0,1:T(8,128)(2,1)}) %all-gather.16.cloned.1.call-update) | async-done | bytes 4194320 | tf_op jit(solution)/shard_map/all_gather | solution.py:73
  234.8 61.6 %all-gather.18.cloned.1.call-done = bf16[4096,512]{0,1:T(8,128)(2,1)} async-done(((bf16[512,512]{0,1:T(8,128)(2,1)}), bf16[4096,512]{0,1:T(8,128)(2,1)}) %all-gather.18.cloned.1.call-update) | async-done | bytes 4194320 | tf_op jit(solution)/shard_map/all_gather | solution.py:72
  309.9 73.7 %while.41 = (s32[]{:T(128)}, f32[8,512]{1,0:T(8,128)S(1)}, f32[8,512]{1,0:T(8,128)S(1)}, s32[4,1024]{1,0:T(4,128)S(1)}, s32[512]{0:T(512)S(1)}, /*index=5*/s32[5...) while((s32[]{:T(128)}, f32[8,512]{1,0:T(8,128)S(1)}, ...), condition=%wide.region_9.10_spmd.clone, body=%wide.region_6.9_spmd.clone.sunk | while | flops 567824384 | bytes 36929660 | solution.py:118
  310.4 8.7 fusion.157
  319.1 9.2 exponential_reduce_fusion.2
  328.8 8.7 fusion.157
  337.5 9.3 exponential_reduce_fusion.2
  356.0 9.2 exponential_reduce_fusion.2
  374.3 9.2 exponential_reduce_fusion.2
  383.6 64.3 %while.42 = (s32[]{:T(128)}, f32[512,8,64]{0,2,1:T(8,128)S(1)}, f32[512,8,64]{0,2,1:T(8,128)}, bf16[4,1024,8,64]{1,3,2,0:T(8,128)(2,1)}, s32[4,1024]{1,0:T(4,128...) while((s32[]{:T(128)}, f32[512,8,64]{0,2,1:T(8,128)S(1)}, ...), condition=%wide.region_11.12_spmd.clone, body=%wide.region_10.11_spmd.clone.sunk | while | flops 1659371520 | bytes 68206800 | solution.py:136
  454.0 42.1 %reduce-scatter.15.cloned.1.call-done = f32[128,2048]{1,0:T(8,128)} async-done(((f32[512,2048]{1,0:T(8,128)}), f32[128,2048]{1,0:T(8,128)}) %reduce-scatter.15.cloned.1.call-update) | async-done | bytes 1048592 | tf_op jit(solution)/shard_map/reduce_scatter | solution.py:235
  501.4 89.2 %all-gather.26.cloned.1.call-done = bf16[2048,1408]{1,0:T(8,128)(2,1)} async-done(((bf16[256,1408]{1,0:T(8,128)(2,1)}), bf16[2048,1408]{1,0:T(8,128)(2,1)}) %all-gather.26.cloned.1.call-update) | async-done | bytes 5767184 | tf_op jit(solution)/shard_map/all_gather | solution.py:246
  590.6 22.9 %all-gather.22.cloned.1.call-done = bf16[512,2048]{1,0:T(8,128)(2,1)} async-done(((bf16[128,2048]{1,0:T(8,128)(2,1)}), bf16[512,2048]{1,0:T(8,128)(2,1)}) %all-gather.22.cloned.1.call-update) | async-done | bytes 2097168 | tf_op jit(solution)/shard_map/all_gather | solution.py:243
  621.8 86.3 %all-gather.24.cloned.1.call-done = bf16[2048,1408]{1,0:T(8,128)(2,1)} async-done(((bf16[256,1408]{1,0:T(8,128)(2,1)}), bf16[2048,1408]{1,0:T(8,128)(2,1)}) %all-gather.24.cloned.1.call-update) | async-done | bytes 5767184 | tf_op jit(solution)/shard_map/all_gather | solution.py:245
  716.3 14.0 all-gather.30.cloned.1.call-done
  730.2 95.2 %all-gather.28.cloned.1.call-done = bf16[1408,2048]{1,0:T(8,128)(2,1)} async-done(((bf16[1408,256]{1,0:T(8,128)(2,1)}), bf16[1408,2048]{1,0:T(8,128)(2,1)}) %all-gather.28.cloned.1.call-update) | async-done | bytes 5767184 | tf_op jit(solution)/shard_map/all_gather | solution.py:247
  825.5 10.5 multiply_convert_fusion
  855.1 35.0 %reduce-scatter.19.cloned.1.call-done = f32[128,2048]{1,0:T(8,128)} async-done(((f32[512,2048]{1,0:T(8,128)}), f32[128,2048]{1,0:T(8,128)}) %reduce-scatter.19.cloned.1.call-update) | async-done | bytes 1048592 | tf_op jit(solution)/shard_map/reduce_scatter | solution.py:271
  892.4 31.5 %reduce-scatter.17.cloned.1.call-done = bf16[128,2048]{1,0:T(8,128)(2,1)} async-done(((bf16[512,2048]{1,0:T(8,128)(2,1)}), bf16[128,2048]{1,0:T(8,128)(2,1)}) %reduce-scatter.17.cloned.1.call-update) | async-done | bytes 524304 | tf_op jit(solution)/shard_map/reduce_scatter | solution.py:254
  927.4 22.5 %all-gather.32.cloned.1.call-done = bf16[512,2048]{1,0:T(8,128)(2,1)} async-done(((bf16[128,2048]{1,0:T(8,128)(2,1)}), bf16[512,2048]{1,0:T(8,128)(2,1)}) %all-gather.32.cloned.1.call-update) | async-done | bytes 2097168 | tf_op jit(solution)/shard_map/all_gather | solution.py:280
  954.4 144.2 %while.43 = (s32[]{:T(128)}, f32[512,8,64]{0,2,1:T(8,128)S(1)}, bf16[4,1024,8,64]{1,3,2,0:T(8,128)(2,1)}, bf16[4,1024,8,64]{1,3,2,0:T(8,128)(2,1)}, bf16[4,1024,...) while((s32[]{:T(128)}, f32[512,8,64]{0,2,1:T(8,128)S(1)}, ...), condition=%wide.region_21.22_spmd.clone, body=%wide.region_20.21_spmd.clone.sunk | while | flops 2729181184 | bytes 124322064 | solution.py:163
  954.9 9.4 fusion.177
  964.4 9.0 bitcast_dynamic-update-slice_fusion.5
  973.4 9.4 fusion.178
  990.9 9.4 fusion.177
  1000.4 9.0 bitcast_dynamic-update-slice_fusion.5
  1009.4 9.4 fusion.178
  1026.9 9.4 fusion.177
  1036.4 9.0 bitcast_dynamic-update-slice_fusion.5
  1045.4 9.4 fusion.178
  1062.9 9.4 fusion.177
  1072.3 9.1 bitcast_dynamic-update-slice_fusion.5
  1081.5 9.4 fusion.178
  1108.5 10.0 copy.100
  1118.5 11.8 reshape.536
  1162.3 35.0 %reduce-scatter.21.cloned.1.call-done = bf16[512,512]{0,1:T(8,128)(2,1)} async-done(((bf16[4096,512]{0,1:T(8,128)(2,1)}), bf16[512,512]{0,1:T(8,128)(2,1)}) %reduce-scatter.21.cloned.1.call-update) | async-done | bytes 524304 | tf_op jit(solution)/shard_map/reduce_scatter | solution.py:296
  1200.1 88.7 %reduce-scatter.23.cloned.1.call-done = bf16[512,512]{1,0:T(8,128)(2,1)} async-done(((bf16[4096,512]{1,0:T(8,128)(2,1)}), bf16[512,512]{1,0:T(8,128)(2,1)}) %reduce-scatter.23.cloned.1.call-update) | async-done | bytes 524304 | tf_op jit(solution)/shard_map/reduce_scatter | solution.py:299
  1306.8 96.2 %reduce-scatter.35.cloned.1.call-done = bf16[1408,256]{1,0:T(8,128)(2,1)} async-done(((bf16[1408,2048]{1,0:T(8,128)(2,1)}), bf16[1408,256]{1,0:T(8,128)(2,1)}) %reduce-scatter.35.cloned.1.call-update) | async-done | bytes 720912 | tf_op jit(solution)/shard_map/reduce_scatter | solution.py:344
  1405.3 111.2 %reduce-scatter.33.cloned.1.call-done = bf16[256,1408]{1,0:T(8,128)(2,1)} async-done(((bf16[2048,1408]{1,0:T(8,128)(2,1)}), bf16[256,1408]{1,0:T(8,128)(2,1)}) %reduce-scatter.33.cloned.1.call-update) | async-done | bytes 720912 | tf_op jit(solution)/shard_map/reduce_scatter | solution.py:341
  1518.8 111.3 %reduce-scatter.31.cloned.1.call-done = bf16[256,1408]{1,0:T(8,128)(2,1)} async-done(((bf16[2048,1408]{1,0:T(8,128)(2,1)}), bf16[256,1408]{1,0:T(8,128)(2,1)}) %reduce-scatter.31.cloned.1.call-update) | async-done | bytes 720912 | tf_op jit(solution)/shard_map/reduce_scatter | solution.py:338
  1632.4 69.4 %reduce-scatter.29.cloned.1.call-done = bf16[512,256]{1,0:T(8,128)(2,1)} async-done(((bf16[512,2048]{1,0:T(8,128)(2,1)}), bf16[512,256]{1,0:T(8,128)(2,1)}) %reduce-scatter.29.cloned.1.call-update) | async-done | bytes 262160 | tf_op jit(solution)/shard_map/reduce_scatter | solution.py:335
  1703.6 62.9 %reduce-scatter.37.cloned.1.call-done = bf16[64,3]{1,0:T(8,128)(2,1)} async-done(((bf16[512,3]{1,0:T(8,128)(2,1)}), bf16[64,3]{1,0:T(8,128)(2,1)}) %reduce-scatter.37.cloned.1.call-update) | async-done | bytes 400
  1767.9 31.4 %reduce-scatter.25.cloned.1.call-done = bf16[128,2048]{1,0:T(8,128)(2,1)} async-done(((bf16[512,2048]{1,0:T(8,128)(2,1)}), bf16[128,2048]{1,0:T(8,128)(2,1)}) %reduce-scatter.25.cloned.1.call-update) | async-done | bytes 524304 | tf_op jit(solution)/shard_map/reduce_scatter | solution.py:313
  1800.8 43.1 %all-reduce.4 = (f32[2048]{0:T(1024)S(1)}, f32[2048]{0:T(1024)S(1)}, f32[2048]{0:T(1024)S(1)}, f32[2048]{0:T(1024)S(1)}) all-reduce(f32[2048]{0:T(1024)S(1)} %get-tuple-element.382, f32[2048]{0:T(1024)S(1)} %get-tuple-element.386, f32[2048]{0:T(1024)S(1)} %copy-done.14, ...), channel_id=8, replica_groups=mesh['head'=4,'blk'=8] {'head','blk'}, use_global_device_ids=true, to_apply=%region_28.29.clone | all-reduce | flops 8192 | bytes 65536
  1848.8 73.6 %reduce-scatter.27.cloned.1.call-done = bf16[256,3,512]{2,0,1:T(8,128)(2,1)} async-done(((bf16[2048,3,512]{2,0,1:T(8,128)(2,1)}), bf16[256,3,512]{2,0,1:T(8,128)(2,1)}) %reduce-scatter.27.cloned.1.call-update) | async-done | bytes 786448 | tf_op jit(solution)/shard_map/reduce_scatter | solution.py:329
  (294 shorter events, 305.4 us)
Async XLA Ops:
  7.2 104.4 %all-gather.14.cloned.1.call-start = ((), (), s32[]{:S(2)}) async-start(), calls=%async_computation.13 | async-start | bytes 7077888 | tf_op jit(solution)/shard_map/all_gather | solution.py:215
  7.9 126.6 %all-gather.12.cloned.1.call-start = ((), (), s32[]{:S(2)}) async-start(), calls=%async_computation.12 | async-start | bytes 2621440 | tf_op jit(solution)/shard_map/all_gather | solution.py:213
  13.3 207.8 %all-gather.16.cloned.1.call-start = ((), (), s32[]{:S(2)}) async-start(), calls=%async_computation.14 | async-start | bytes 4718592 | tf_op jit(solution)/shard_map/all_gather | solution.py:73
  146.3 150.1 %all-gather.18.cloned.1.call-start = ((), (), s32[]{:S(2)}) async-start(), calls=%async_computation.15 | async-start | bytes 4718592 | tf_op jit(solution)/shard_map/all_gather | solution.py:72
  149.8 298.2 %all-gather.20.cloned.1.call-start = ((), (), s32[]{:S(2)}) async-start(), calls=%async_computation.16 | async-start | bytes 2359296 | tf_op jit(solution)/shard_map/all_gather | solution.py:216
  150.4 345.7 %reduce-scatter.15.cloned.1.call-start = ((), (), s32[]{:S(2)}) async-start(), calls=%async_computation.17 | async-start | bytes 5242880 | tf_op jit(solution)/shard_map/reduce_scatter | solution.py:235
  384.3 3.7 copy-start.24
  394.0 5.8 copy-start.25
  400.3 3.7 copy-start.24
  410.0 5.8 copy-start.25
  426.0 5.8 copy-start.25
  442.1 5.8 copy-start.25
  448.0 5.2 copy-start.7
  448.0 48.0 %copy-start = (bf16[128,2048]{1,0:T(8,128)(2,1)S(1)}, bf16[128,2048]{1,0:T(8,128)(2,1)}, u32[]{:S(2)}) copy-start(bf16[128,2048]{1,0:T(8,128)(2,1)} %param.20) | copy-start | bytes 1572868
  453.1 44.6 %copy-start.11 = (f32[2048]{0:T(1024)S(1)}, f32[2048]{0:T(1024)}, u32[]{:S(2)}) copy-start(f32[2048]{0:T(1024)} %param.26) | copy-start | bytes 24580
  453.1 44.6 %copy-start.16 = (f32[2048]{0:T(1024)S(1)}, f32[2048]{0:T(1024)}, u32[]{:S(2)}) copy-start(f32[2048]{0:T(1024)} %param.27) | copy-start | bytes 24580
  453.2 137.4 %all-gather.26.cloned.1.call-start = ((), (), s32[]{:S(2)}) async-start(), calls=%async_computation.20 | async-start | bytes 6488064 | tf_op jit(solution)/shard_map/all_gather | solution.py:246
  453.9 159.6 %all-gather.22.cloned.1.call-start = ((), (), s32[]{:S(2)}) async-start(), calls=%async_computation.18 | async-start | bytes 2621440 | tf_op jit(solution)/shard_map/all_gather | solution.py:243
  498.9 209.2 %all-gather.24.cloned.1.call-start = ((), (), s32[]{:S(2)}) async-start(), calls=%async_computation.19 | async-start | bytes 6488064 | tf_op jit(solution)/shard_map/all_gather | solution.py:245
  499.6 230.6 %all-gather.30.cloned.1.call-start = ((), (), s32[]{:S(2)}) async-start(), calls=%async_computation.23 | async-start | bytes 2621440 | tf_op jit(solution)/shard_map/all_gather | solution.py:262
  500.2 325.3 %all-gather.28.cloned.1.call-start = ((), (), s32[]{:S(2)}) async-start(), calls=%async_computation.21 | async-start | bytes 6488064 | tf_op jit(solution)/shard_map/all_gather | solution.py:247
  500.9 389.2 %reduce-scatter.19.cloned.1.call-start = ((), (), s32[]{:S(2)}) async-start(), calls=%async_computation.24 | async-start | bytes 5242880 | tf_op jit(solution)/shard_map/reduce_scatter | solution.py:271
  825.5 10.5 copy-start.23
  847.2 76.7 %reduce-scatter.17.cloned.1.call-start = ((), (), s32[]{:S(2)}) async-start(), calls=%async_computation.22 | async-start | bytes 2621440 | tf_op jit(solution)/shard_map/reduce_scatter | solution.py:254
  855.0 68.8 %copy-start.6 = (bf16[128,2048]{1,0:T(8,128)(2,1)S(1)}, bf16[128,2048]{1,0:T(8,128)(2,1)}, u32[]{:S(2)}) copy-start(bf16[128,2048]{1,0:T(8,128)(2,1)} %param.31) | copy-start | bytes 1572868
  855.0 94.8 %all-gather.32.cloned.1.call-start = ((), (), s32[]{:S(2)}) async-start(), calls=%async_computation.25 | async-start | bytes 2621440 | tf_op jit(solution)/shard_map/all_gather | solution.py:280
  927.2 270.1 %reduce-scatter.21.cloned.1.call-start = ((), (), s32[]{:S(2)}) async-start(), calls=%async_computation.26 | async-start | bytes 4718592 | tf_op jit(solution)/shard_map/reduce_scatter | solution.py:296
  954.9 9.5 copy-start.26
  990.9 9.5 copy-start.26
  1026.9 9.5 copy-start.26
  1062.9 9.5 copy-start.26
  1108.5 180.3 %reduce-scatter.23.cloned.1.call-start = ((), (), s32[]{:S(2)}) async-start(), calls=%async_computation.27 | async-start | bytes 4718592 | tf_op jit(solution)/shard_map/reduce_scatter | solution.py:299
  1130.4 272.6 %reduce-scatter.35.cloned.1.call-start = ((), (), s32[]{:S(2)}) async-start(), calls=%async_computation.33 | async-start | bytes 6488064 | tf_op jit(solution)/shard_map/reduce_scatter | solution.py:344
  1139.1 377.4 %reduce-scatter.33.cloned.1.call-start = ((), (), s32[]{:S(2)}) async-start(), calls=%async_computation.32 | async-start | bytes 6488064 | tf_op jit(solution)/shard_map/reduce_scatter | solution.py:341
  1148.0 482.1 %reduce-scatter.31.cloned.1.call-start = ((), (), s32[]{:S(2)}) async-start(), calls=%async_computation.31 | async-start | bytes 6488064 | tf_op jit(solution)/shard_map/reduce_scatter | solution.py:338
  1156.9 545.0 %reduce-scatter.29.cloned.1.call-start = ((), (), s32[]{:S(2)}) async-start(), calls=%async_computation.30 | async-start | bytes 2359296 | tf_op jit(solution)/shard_map/reduce_scatter | solution.py:335
  1162.1 37.4 %copy-start.10 = (f32[512,8]{0,1:T(8,128)S(1)}, f32[512,8]{0,1:T(8,128)}, u32[]{:S(2)}) copy-start(f32[512,8]{0,1:T(8,128)} %copy-done.9) | copy-start | bytes 49156
  1162.1 37.4 %copy-start.13 = (f32[512,8]{0,1:T(8,128)S(1)}, f32[512,8]{0,1:T(8,128)}, u32[]{:S(2)}) copy-start(f32[512,8]{0,1:T(8,128)} %get-tuple-element.479) | copy-start | bytes 49156
  1162.2 604.4 %reduce-scatter.37.cloned.1.call-start = ((), (), s32[]{:S(2)}) async-start(), calls=%async_computation.34 | async-start | bytes 147456
  1291.2 508.1 %reduce-scatter.25.cloned.1.call-start = ((), (), s32[]{:S(2)}) async-start(), calls=%async_computation.28 | async-start | bytes 2621440 | tf_op jit(solution)/shard_map/reduce_scatter | solution.py:313
  1298.7 623.7 %reduce-scatter.27.cloned.1.call-start = ((), (), s32[]{:S(2)}) async-start(), calls=%async_computation.29 | async-start | bytes 7077888 | tf_op jit(solution)/shard_map/reduce_scatter | solution.py:329
  1306.7 492.5 %copy-start.1 = (bf16[128,2048]{1,0:T(8,128)(2,1)S(1)}, bf16[128,2048]{1,0:T(8,128)(2,1)}, u32[]{:S(2)}) copy-start(bf16[128,2048]{1,0:T(8,128)(2,1)} %param.20) | copy-start | bytes 1572868
  1306.8 492.5 %copy-start.12 = (f32[2048]{0:T(1024)S(1)}, f32[2048]{0:T(1024)}, u32[]{:S(2)}) copy-start(f32[2048]{0:T(1024)} %param.21) | copy-start | bytes 24580
  1306.8 492.5 %copy-start.18 = (f32[128]{0:T(128)S(1)}, f32[128]{0:T(128)}, u32[]{:S(2)}) copy-start(f32[128]{0:T(128)} %copy-done.17) | copy-start | bytes 1540
  1306.8 492.5 %copy-start.20 = (f32[128]{0:T(128)S(1)}, f32[128]{0:T(128)}, u32[]{:S(2)}) copy-start(f32[128]{0:T(128)} %copy-done.19) | copy-start | bytes 1540
  1306.8 494.0 %copy-start.14 = (f32[2048]{0:T(1024)S(1)}, f32[2048]{0:T(1024)}, u32[]{:S(2)}) copy-start(f32[2048]{0:T(1024)} %get-tuple-element.379) | copy-start | bytes 24580
  1306.8 494.0 %copy-start.15 = (f32[2048]{0:T(1024)S(1)}, f32[2048]{0:T(1024)}, u32[]{:S(2)}) copy-start(f32[2048]{0:T(1024)} %get-tuple-element.384) | copy-start | bytes 24580
  1306.8 539.5 %copy-start.4 = (f32[128,2048]{1,0:T(8,128)S(1)}, f32[128,2048]{1,0:T(8,128)}, u32[]{:S(2)}) copy-start(f32[128,2048]{1,0:T(8,128)} %get-tuple-element.456) | copy-start | bytes 3145732
  (22 other events, 51.4 us)
Sparse Core Ops, SparseCore 0:
  10.2 101.4 all-gather.13
  113.8 20.7 all-gather.11
  146.5 74.6 all-gather.15
  223.6 72.8 all-gather.17
  298.3 48.5 all-gather.19
  453.3 42.7 reduce-scatter.14
  498.3 92.3 all-gather.25
  592.7 20.7 all-gather.21
  615.7 92.3 all-gather.23
  709.5 20.7 all-gather.29
  732.3 93.1 all-gather.27
  847.3 42.7 reduce-scatter.18
  892.6 31.1 reduce-scatter.16
  927.3 22.5 all-gather.31
  1108.6 88.6 reduce-scatter.20
  1200.8 87.9 reduce-scatter.22
  1292.3 110.6 reduce-scatter.34
  1406.5 109.9 reduce-scatter.32
  1520.1 109.9 reduce-scatter.30
  1633.5 68.3 reduce-scatter.28
  1705.7 60.7 reduce-scatter.36
  1769.0 30.1 reduce-scatter.24
  1802.9 119.4 reduce-scatter.26
where the time goes:
time: 1940 us; the launch traced here: 1930 us
  waiting for transfers between devices  1360 us (70%)
  matrix products  336 us (17%)
  local copies, waits for them, and re-layouts  93.3 us (5%)
  other arithmetic  76.9 us (4%)
  blocking collectives  43.1 us (2%)
    reduce_scatter x1, waiting for transfers between devices, on_device(): lax.psum_scatter(grad_w_gate.astype(jnp.bfloat16), 'blk', scatter_dimensi...  111 us
    reduce_scatter x1, waiting for transfers between devices, on_device(): lax.psum_scatter(grad_w_up.astype(jnp.bfloat16), 'blk', scatter_dimension...  111 us
    all_gather x1, waiting for transfers between devices, on_device(): lax.all_gather(w_qkv, 'blk', axis=0, tiled=True)  97.6 us
    reduce_scatter x1, waiting for transfers between devices, on_device(): lax.psum_scatter(grad_w_down.astype(jnp.bfloat16), 'blk', scatter_dimensi...  96.2 us
    all_gather x1, waiting for transfers between devices, on_device(): lax.all_gather(w_down, 'blk', axis=1, tiled=True)  95.2 us
    all_gather x1, waiting for transfers between devices, on_device(): lax.all_gather(w_up, 'blk', axis=0, tiled=True)  89.2 us
    reduce_scatter x1, waiting for transfers between devices, on_device(): lax.psum_scatter(value_terms.astype(jnp.bfloat16), 'blk', scatter_dimensi...  88.7 us
    dot_general x12, matrix products, masked_scores(): jnp.einsum('qhd,khd->hqk', queries, key_tile, preferred_element_type=jnp....  87.1 us
  transfers between devices with their start and end apart: 23, of which 22 were waited for; matrix products, arithmetic and copies ran while one was open for 15% of the time, Pallas kernels for 0%

commit v1 on v0

--- a/solution.py
+++ b/solution.py
@@ -1,11 +1,16 @@
 import jax
 import jax.numpy as jnp
 from jax import lax
+from jax.experimental import pallas as pl
+from jax.experimental.pallas import tpu as pltpu
 from jax.sharding import PartitionSpec as P
 
 HD = 64
 ROT = 16
 BLOCK = 128
+Z_PARTS = 4
+QUERY_TILE = 512
+KEY_TILE = 256
 
 
 EPSILON = 1e-05
@@ -361,6 +366,588 @@
     )
 
 
+def split_order(values, z_index, axis):
+    pieces = values.shape[axis] // Z_PARTS
+    parts = [
+        lax.dynamic_slice_in_dim(
+            values, lax.rem(z_index - j + Z_PARTS, Z_PARTS) * pieces, pieces, axis
+        )
+        for j in range(Z_PARTS)
+    ]
+    return jnp.concatenate(parts, axis=axis)
+
+
+def swap_x(values):
+    return lax.ppermute(values, "head", [(h, h ^ 2) for h in range(4)])
+
+
+def swap_core(values):
+    return lax.ppermute(values, "head", [(h, h ^ 1) for h in range(4)])
+
+
+def swap_y(values):
+    return lax.ppermute(values, "blk", [(b, b ^ 1) for b in range(2 * Z_PARTS)])
+
+
+def shift_z(values, amount):
+    total = 2 * Z_PARTS
+    return lax.ppermute(values, "blk", [(b, (b + 2 * amount) % total) for b in range(total)])
+
+
+def gather_rows(own):
+    half = own.shape[0] // 2
+    from_x = swap_x(own)
+    from_y = swap_y(own)
+    corner_a = swap_y(from_x[:half])
+    corner_b = swap_x(from_y[half:])
+    mine = jnp.concatenate([own, from_y, from_x, corner_a, corner_b], axis=0)
+    return jnp.concatenate([mine, swap_core(mine)], axis=0)
+
+
+def scatter_rows(partial):
+    rows = partial.shape[0] // 8
+    half = rows // 2
+    mine = partial[: 4 * rows]
+    theirs = swap_core(partial[4 * rows :].astype(jnp.bfloat16))
+    total = mine + theirs.astype(jnp.float32)
+    own, for_y, for_x, corner = [total[i * rows : (i + 1) * rows] for i in range(4)]
+    corner_b = corner.astype(jnp.bfloat16)
+    got_x = swap_x(corner_b[:half]).astype(jnp.float32)
+    got_y = swap_y(corner_b[half:]).astype(jnp.float32)
+    for_y = jnp.concatenate([for_y[:half] + got_x, for_y[half:]], axis=0)
+    for_x = jnp.concatenate([for_x[:half], for_x[half:] + got_y], axis=0)
+    last_x = swap_x(for_x.astype(jnp.bfloat16)).astype(jnp.float32)
+    last_y = swap_y(for_y.astype(jnp.bfloat16)).astype(jnp.float32)
+    return own + last_x + last_y
+
+
+def ring_gather(chunk, amount):
+    held = [chunk]
+    for unused in range(Z_PARTS - 1):
+        held.append(shift_z(held[-1], amount))
+    if amount == 1:
+        return held
+    return [held[(Z_PARTS - j) % Z_PARTS] for j in range(Z_PARTS)]
+
+
+def ring_scatter(partials, amount):
+    order = [(j + 1) % Z_PARTS for j in range(Z_PARTS)]
+    if amount == -1:
+        order = [(Z_PARTS - j) % Z_PARTS for j in order]
+    total = partials[order[0]]
+    for j in order[1:]:
+        total = shift_z(total.astype(jnp.bfloat16), amount).astype(jnp.float32) + partials[j]
+    return total
+
+
+def to_even_odd(mine, theirs, y_index):
+    got = swap_y(theirs)
+    return jnp.where(y_index == 0, mine, got), jnp.where(y_index == 0, got, mine)
+
+
+def from_even_odd(even, odd, y_index):
+    mine = jnp.where(y_index == 0, even, odd)
+    theirs = jnp.where(y_index == 0, odd, even).astype(jnp.bfloat16)
+    got = swap_y(theirs).astype(jnp.float32)
+    return jnp.where(y_index == 0, mine, got), jnp.where(y_index == 0, got, mine)
+
+
+def to_heads(pieces, z_index):
+    received = []
+    for t in range(Z_PARTS):
+        piece = lax.dynamic_index_in_dim(
+            pieces, lax.rem(z_index + t, Z_PARTS), axis=0, keepdims=False
+        )
+        received.append(piece if t == 0 else shift_z(piece, t))
+    return jnp.stack(received, axis=0)
+
+
+def from_heads(pieces, z_index):
+    received = [pieces[0]] + [shift_z(pieces[t], -t) for t in range(1, Z_PARTS)]
+    ordered = jnp.stack(received + received, axis=0)
+    return lax.dynamic_slice_in_dim(ordered, Z_PARTS - z_index, Z_PARTS, axis=0)
+
+
+def tile_mask(key_tile, query_tile, start_row):
+    key_pos = key_tile * KEY_TILE + lax.broadcasted_iota(jnp.int32, (KEY_TILE, QUERY_TILE), 0)
+    query_pos = query_tile * QUERY_TILE + lax.broadcasted_iota(
+        jnp.int32, (KEY_TILE, QUERY_TILE), 1
+    )
+    return (key_pos <= query_pos) & (key_pos >= start_row)
+
+
+def mm(left, right, left_dim=1, right_dim=0):
+    return lax.dot_general(
+        left, right, (((left_dim,), (right_dim,)), ((), ())), preferred_element_type=jnp.float32
+    )
+
+
+def pack_blocks(slot_ref, source_ref, target_ref, blocks):
+    per_part = source_ref.shape[2] // BLOCK
+    for block in range(blocks):
+        slot = slot_ref[block]
+        part = slot // per_part
+        column = pl.multiple_of((slot % per_part) * BLOCK, BLOCK)
+        target_ref[:, block * BLOCK : (block + 1) * BLOCK] = source_ref[
+            part, :, pl.ds(column, BLOCK)
+        ]
+
+
+def attend_kernel(
+    slot_ref, low_ref, qkv_ref, start_ref, out_ref, exact_ref, norm_ref, packed_ref, keys_ref
+):
+    total = packed_ref.shape[1]
+    blocks = total // BLOCK
+    pack_blocks(slot_ref, qkv_ref, packed_ref, blocks)
+    for tile in range(total // KEY_TILE):
+        spot = slice(tile * KEY_TILE, (tile + 1) * KEY_TILE)
+        keys_ref[spot, :] = packed_ref[HD : 2 * HD, spot].T
+
+    def query_step(query_tile, unused):
+        column = pl.multiple_of(query_tile * QUERY_TILE, QUERY_TILE)
+        queries = packed_ref[0:HD, pl.ds(column, QUERY_TILE)] * HD ** (-0.5)
+        queries = queries.astype(jnp.bfloat16)
+        start_row = start_ref[:, pl.ds(column, QUERY_TILE)]
+
+        def key_step(key_tile, state):
+            run_max, run_sum, run_out = state
+            row = pl.multiple_of(key_tile * KEY_TILE, KEY_TILE)
+            scores = mm(keys_ref[pl.ds(row, KEY_TILE), :], queries)
+            scores = jnp.where(tile_mask(key_tile, query_tile, start_row), scores, MASKED)
+            new_max = jnp.maximum(run_max, jnp.max(scores, axis=0, keepdims=True))
+            probs = jnp.exp(scores - new_max)
+            fade = jnp.exp(run_max - new_max)
+            run_sum = run_sum * fade + jnp.sum(probs, axis=0, keepdims=True)
+            run_out = run_out * fade + mm(
+                packed_ref[2 * HD : 3 * HD, pl.ds(row, KEY_TILE)], probs.astype(jnp.bfloat16)
+            )
+            return new_max, run_sum, run_out
+
+        first = (
+            jnp.full((1, QUERY_TILE), -3e38, jnp.float32),
+            jnp.zeros((1, QUERY_TILE), jnp.float32),
+            jnp.zeros((HD, QUERY_TILE), jnp.float32),
+        )
+        run_max, run_sum, run_out = lax.fori_loop(
+            low_ref[query_tile], ((query_tile + 1) * QUERY_TILE) // KEY_TILE, key_step, first
+        )
+        exact_ref[:, pl.ds(column, QUERY_TILE)] = run_out / run_sum
+        norm_ref[:, pl.ds(column, QUERY_TILE)] = run_max + jnp.log(run_sum)
+        return unused
+
+    lax.fori_loop(0, total // QUERY_TILE, query_step, 0)
+    per_part = out_ref.shape[2] // BLOCK
+    for block in range(blocks):
+        slot = slot_ref[block]
+        column = pl.multiple_of((slot % per_part) * BLOCK, BLOCK)
+        out_ref[slot // per_part, :, pl.ds(column, BLOCK)] = exact_ref[
+            :, block * BLOCK : (block + 1) * BLOCK
+        ].astype(jnp.bfloat16)
+
+
+def rotate_back(values, cosine, sine_table):
+    half_rot = ROT // 2
+    lead_part = values[0:half_rot]
+    tail_part = values[half_rot:ROT]
+    return jnp.concatenate(
+        [
+            lead_part * cosine + tail_part * sine_table,
+            tail_part * cosine - lead_part * sine_table,
+            values[ROT:],
+        ],
+        axis=0,
+    )
+
+
+def attend_back_kernel(
+    slot_ref,
+    low_ref,
+    grad_ref,
+    packed_ref,
+    exact_ref,
+    norm_ref,
+    start_ref,
+    cosine_ref,
+    sine_ref,
+    out_ref,
+    bias_ref,
+    keys_ref,
+    values_ref,
+    grads_ref,
+    sums_ref,
+):
+    total = packed_ref.shape[1]
+    blocks = total // BLOCK
+    scale = HD ** (-0.5)
+    pack_blocks(slot_ref, grad_ref, grads_ref, blocks)
+    for tile in range(total // KEY_TILE):
+        spot = slice(tile * KEY_TILE, (tile + 1) * KEY_TILE)
+        keys_ref[spot, :] = packed_ref[HD : 2 * HD, spot].T
+        values_ref[spot, :] = packed_ref[2 * HD : 3 * HD, spot].T
+    sums_ref[HD : 3 * HD, :] = jnp.zeros((2 * HD, total), jnp.float32)
+
+    def query_step(query_tile, unused):
+        column = pl.multiple_of(query_tile * QUERY_TILE, QUERY_TILE)
+        spot = pl.ds(column, QUERY_TILE)
+        queries = (packed_ref[0:HD, spot] * scale).astype(jnp.bfloat16)
+        grads = grads_ref[:, spot]
+        start_row = start_ref[:, spot]
+        norm_row = norm_ref[:, spot]
+        delta_row = jnp.sum(
+            grads.astype(jnp.float32) * exact_ref[:, spot], axis=0, keepdims=True
+        )
+
+        def key_step(key_tile, grad_query):
+            row = pl.multiple_of(key_tile * KEY_TILE, KEY_TILE)
+            rows = pl.ds(row, KEY_TILE)
+            scores = mm(keys_ref[rows, :], queries)
+            scores = jnp.where(tile_mask(key_tile, query_tile, start_row), scores, MASKED)
+            probs = jnp.exp(scores - norm_row)
+            grad_probs = mm(values_ref[rows, :], grads)
+            grad_scores = (probs * (grad_probs - delta_row)).astype(jnp.bfloat16)
+            probs_b = probs.astype(jnp.bfloat16)
+            sums_ref[2 * HD : 3 * HD, rows] += mm(grads, probs_b, 1, 1)
+            sums_ref[HD : 2 * HD, rows] += mm(queries, grad_scores, 1, 1)
+            return grad_query + mm(packed_ref[HD : 2 * HD, rows], grad_scores)
+
+        grad_query = lax.fori_loop(
+            low_ref[query_tile],
+            ((query_tile + 1) * QUERY_TILE) // KEY_TILE,
+            key_step,
+            jnp.zeros((HD, QUERY_TILE), jnp.float32),
+        )
+        sums_ref[0:HD, spot] = grad_query * scale
+        return unused
+
+    lax.fori_loop(0, total // QUERY_TILE, query_step, 0)
+    per_part = out_ref.shape[2] // BLOCK
+    bias_sum = jnp.zeros((3 * HD, BLOCK), jnp.float32)
+    for block in range(blocks):
+        spot = slice(block * BLOCK, (block + 1) * BLOCK)
+        cosine = cosine_ref[:, spot]
+        sine_table = sine_ref[:, spot]
+        slot = slot_ref[block]
+        column = pl.multiple_of((slot % per_part) * BLOCK, BLOCK)
+        rounded = jnp.concatenate(
+            [
+                rotate_back(sums_ref[0:HD, spot], cosine, sine_table),
+                rotate_back(sums_ref[HD : 2 * HD, spot], cosine, sine_table),
+                sums_ref[2 * HD : 3 * HD, spot],
+            ],
+            axis=0,
+        ).astype(jnp.bfloat16)
+        out_ref[slot // per_part, :, pl.ds(column, BLOCK)] = rounded
+        bias_sum = bias_sum + rounded.astype(jnp.float32)
+    bias_ref[...] = bias_sum
+
+
+def attend_heads(slot_of, low_tile, qkv_parts, start_row):
+    parts, features, part_rows = qkv_parts.shape
+    total = parts * part_rows
+    vmem = pl.BlockSpec(memory_space=pltpu.VMEM)
+    return pl.pallas_call(
+        attend_kernel,
+        grid_spec=pltpu.PrefetchScalarGridSpec(
+            num_scalar_prefetch=2,
+            grid=(1,),
+            in_specs=[vmem, vmem],
+            out_specs=[vmem, vmem, vmem, vmem],
+            scratch_shapes=[pltpu.VMEM((total, HD), jnp.bfloat16)],
+        ),
+        out_shape=[
+            jax.ShapeDtypeStruct((parts, HD, part_rows), jnp.bfloat16),
+            jax.ShapeDtypeStruct((HD, total), jnp.float32),
+            jax.ShapeDtypeStruct((1, total), jnp.float32),
+            jax.ShapeDtypeStruct((3 * HD, total), jnp.bfloat16),
+        ],
+        cost_estimate=pl.CostEstimate(
+            flops=total * total * HD, transcendentals=total * total // 4, bytes_accessed=6 << 20
+        ),
+        compiler_params=pltpu.CompilerParams(vmem_limit_bytes=40 << 20),
+        name="attend",
+    )(slot_of, low_tile, qkv_parts, start_row)
+
+
+def attend_heads_back(
+    slot_of, low_tile, grad_parts, packed, exact, log_norm, start_row, cosine, sine_table
+):
+    parts, features, part_rows = grad_parts.shape
+    total = parts * part_rows
+    vmem = pl.BlockSpec(memory_space=pltpu.VMEM)
+    return pl.pallas_call(
+        attend_back_kernel,
+        grid_spec=pltpu.PrefetchScalarGridSpec(
+            num_scalar_prefetch=2,
+            grid=(1,),
+            in_specs=[vmem] * 7,
+            out_specs=[vmem, vmem],
+            scratch_shapes=[
+                pltpu.VMEM((total, HD), jnp.bfloat16),
+                pltpu.VMEM((total, HD), jnp.bfloat16),
+                pltpu.VMEM((HD, total), jnp.bfloat16),
+                pltpu.VMEM((3 * HD, total), jnp.float32),
+            ],
+        ),
+        out_shape=[
+            jax.ShapeDtypeStruct((parts, 3 * HD, part_rows), jnp.bfloat16),
+            jax.ShapeDtypeStruct((3 * HD, BLOCK), jnp.float32),
+        ],
+        cost_estimate=pl.CostEstimate(
+            flops=3 * total * total * HD,
+            transcendentals=total * total // 4,
+            bytes_accessed=8 << 20,
+        ),
+        compiler_params=pltpu.CompilerParams(vmem_limit_bytes=50 << 20),
+        name="attend_back",
+    )(slot_of, low_tile, grad_parts, packed, exact, log_norm, start_row, cosine, sine_table)
+
+
+def start_of(position, seq_lengths):
+    seq_ends = jnp.cumsum(seq_lengths)
+    ends_before = seq_ends[:, None] <= position[None, :]
+    return jnp.sum(jnp.where(ends_before, seq_lengths[:, None], 0), axis=0)
+
+
+def rotary_tables(offset_in_seq):
+    half_rot = ROT // 2
+    freq_table = jnp.power(10000.0, -2.0 * jnp.arange(half_rot, dtype=jnp.float32) / ROT)
+    angles = freq_table[:, None] * offset_in_seq.astype(jnp.float32)[None, :]
+    return jnp.cos(angles), jnp.sin(angles)
+
+
+def on_device_heads(
+    tokens,
+    norm1_gain,
+    norm1_bias,
+    w_qkv,
+    qkv_bias,
+    w_out,
+    norm2_gain,
+    norm2_bias,
+    w_gate,
+    w_up,
+    w_down,
+    cotangent,
+    seq_lengths,
+    block_order,
+):
+    head_index = lax.axis_index("head")
+    blk_index = lax.axis_index("blk")
+    x_index, core_index = head_index // 2, head_index % 2
+    z_index, y_index = blk_index // 2, blk_index % 2
+    tok_rows, model_width = tokens.shape
+    plane_rows = 8 * tok_rows
+    total_rows = Z_PARTS * plane_rows
+    row_block = model_width // (2 * Z_PARTS)
+    chunk = 2 * row_block
+    ff_half = w_gate.shape[1] // 2
+    heads_width = Z_PARTS * HD
+
+    qkv_split = w_qkv.reshape(row_block, 3, Z_PARTS, 2, HD)
+    qkv_low = qkv_split[:, :, :, 0].reshape(row_block, 3 * heads_width)
+    qkv_high = qkv_split[:, :, :, 1].reshape(row_block, 3 * heads_width)
+    first = y_index == 0
+    qkv_even, qkv_odd = to_even_odd(
+        jnp.where(first, qkv_low, qkv_high), jnp.where(first, qkv_high, qkv_low), y_index
+    )
+    out_split = w_out.reshape(Z_PARTS, 2, HD, row_block)
+    out_low = out_split[:, 0].reshape(heads_width, row_block)
+    out_high = out_split[:, 1].reshape(heads_width, row_block)
+    out_even, out_odd = to_even_odd(
+        jnp.where(first, out_low, out_high), jnp.where(first, out_high, out_low), y_index
+    )
+
+    def column_halves(weight):
+        low, high = weight[:, :ff_half], weight[:, ff_half:]
+        return to_even_odd(jnp.where(first, low, high), jnp.where(first, high, low), y_index)
+
+    gate_own = jnp.concatenate(column_halves(w_gate), axis=0)
+    up_own = jnp.concatenate(column_halves(w_up), axis=0)
+    down_low, down_high = w_down[:ff_half], w_down[ff_half:]
+    down_even, down_odd = to_even_odd(
+        jnp.where(first, down_low, down_high), jnp.where(first, down_high, down_low), y_index
+    )
+
+    def both_ways(even, odd, axis):
+        forward = ring_gather(even, 1)
+        backward = ring_gather(odd, -1)
+        pieces = [p for pair in zip(forward, backward) for p in pair]
+        return jnp.concatenate(pieces, axis=axis)
+
+    x_own = split_order(tokens, z_index, 1).astype(jnp.float32)
+    gain_one = split_order(norm1_gain, z_index, 0)
+    shift_one = split_order(norm1_bias, z_index, 0)
+    gain_two = split_order(norm2_gain, z_index, 0)
+    shift_two = split_order(norm2_bias, z_index, 0)
+    norm1_out, unit_one, inv_one = normalize(x_own, gain_one, shift_one)
+    norm1_all = gather_rows(norm1_out.astype(jnp.bfloat16))
+    qkv_full = both_ways(qkv_even, qkv_odd, 0)
+    out_full = both_ways(out_even, out_odd, 1)
+    gate_full = jnp.concatenate(ring_gather(gate_own, 1), axis=0)
+    up_full = jnp.concatenate(ring_gather(up_own, -1), axis=0)
+    down_full = both_ways(down_even, down_odd, 1)
+
+    slots = jnp.arange(Z_PARTS * 8, dtype=jnp.int32)
+    step_z, flip = slots // 8, slots % 8
+    owner = (
+        ((x_index ^ ((flip // 2) % 2)) * 2 + (core_index ^ (flip // 4))) * (2 * Z_PARTS)
+        + ((z_index - step_z + Z_PARTS) % Z_PARTS) * 2
+        + (y_index ^ (flip % 2))
+    )
+    packed_block = jnp.sum(
+        jnp.where(owner[:, None] == slots[None, :], block_order[None, :], 0), axis=1
+    )
+    slot_of = jnp.sum(
+        jnp.where(packed_block[None, :] == slots[:, None], slots[None, :], 0), axis=1
+    )
+    plane_pos = (
+        packed_block[:8, None] * BLOCK + jnp.arange(BLOCK, dtype=jnp.int32)[None, :]
+    ).reshape(-1)
+    plane_cos, plane_sin = rotary_tables(plane_pos - start_of(plane_pos, seq_lengths))
+    all_pos = jnp.arange(total_rows, dtype=jnp.int32)
+    all_start = start_of(all_pos, seq_lengths)
+    all_cos, all_sin = rotary_tables(all_pos - all_start)
+    low_tile = (
+        start_of(
+            jnp.arange(total_rows // QUERY_TILE, dtype=jnp.int32) * QUERY_TILE, seq_lengths
+        )
+        // KEY_TILE
+    )
+    start_row = all_start[None, :]
+
+    bias_split = qkv_bias.reshape(3, Z_PARTS, 2, HD)
+    bias_own = jnp.where(first, bias_split[:, :, 0], bias_split[:, :, 1]).reshape(-1)
+    projected = (mm(qkv_full, norm1_all, 0, 1) + bias_own[:, None]).reshape(
+        3, Z_PARTS, HD, plane_rows
+    )
+    half_rot = ROT // 2
+    lead_part, tail_part = projected[:2, :, :half_rot], projected[:2, :, half_rot:ROT]
+    rotated = jnp.concatenate(
+        [
+            lead_part * plane_cos - tail_part * plane_sin,
+            tail_part * plane_cos + lead_part * plane_sin,
+            projected[:2, :, ROT:],
+        ],
+        axis=2,
+    )
+    qkv_heads = jnp.concatenate([rotated, projected[2:]], axis=0).astype(jnp.bfloat16)
+    qkv_heads = qkv_heads.transpose(1, 0, 2, 3).reshape(Z_PARTS, 3 * HD, plane_rows)
+    qkv_parts = to_heads(qkv_heads, z_index)
+    attn_parts, attn_exact, log_norm, packed = attend_heads(
+        slot_of, low_tile, qkv_parts, start_row
+    )
+    attn_t = from_heads(attn_parts, z_index).reshape(heads_width, plane_rows)
+    attn_own = scatter_rows(mm(attn_t, out_full, 0, 0))
+
+    hidden = x_own + attn_own
+    norm2_out, unit_two, inv_two = normalize(hidden, gain_two, shift_two)
+    norm2_all = gather_rows(norm2_out.astype(jnp.bfloat16))
+    cotangent_own = split_order(cotangent, z_index, 1)
+    grad_all = gather_rows(cotangent_own)
+    gate_val = mm(norm2_all, gate_full)
+    up_val = mm(norm2_all, up_full)
+    sigmoid_gate = jax.nn.sigmoid(gate_val)
+    swish_val = gate_val * sigmoid_gate
+    activ_b = (swish_val * up_val).astype(jnp.bfloat16)
+    grad_activ = mm(grad_all, down_full, 1, 1)
+    grad_up_b = (grad_activ * swish_val).astype(jnp.bfloat16)
+    grad_gate_b = (
+        grad_activ * up_val * sigmoid_gate * (1.0 + gate_val * (1.0 - sigmoid_gate))
+    ).astype(jnp.bfloat16)
+    grad_norm2 = scatter_rows(mm(grad_gate_b, gate_full, 1, 1) + mm(grad_up_b, up_full, 1, 1))
+    mlp_own = scatter_rows(mm(activ_b, down_full))
+    output = split_order((hidden + mlp_own).astype(jnp.bfloat16), z_index, 1)
+
+    def pieces_of(values, width, offset=0, size=None):
+        size = width if size is None else size
+        return [
+            values[:, j * width + offset : j * width + offset + size] for j in range(Z_PARTS)
+        ]
+
+    down_sum_even = ring_scatter(
+        [mm(activ_b, p, 0, 0) for p in pieces_of(grad_all, chunk, 0, row_block)], 1
+    )
+    down_sum_odd = ring_scatter(
+        [mm(activ_b, p, 0, 0) for p in pieces_of(grad_all, chunk, row_block, row_block)], -1
+    )
+    down_parts = from_even_odd(down_sum_even, down_sum_odd, y_index)
+    down_grad = jnp.concatenate(down_parts, axis=0)
+    gate_sum = ring_scatter([mm(p, grad_gate_b, 0, 0) for p in pieces_of(norm2_all, chunk)], 1)
+    up_sum = ring_scatter([mm(p, grad_up_b, 0, 0) for p in pieces_of(norm2_all, chunk)], -1)
+    gate_grad = jnp.concatenate(
+        from_even_odd(gate_sum[:row_block], gate_sum[row_block:], y_index), axis=1
+    )
+    up_grad = jnp.concatenate(
+        from_even_odd(up_sum[:row_block], up_sum[row_block:], y_index), axis=1
+    )
+
+    grad_out = cotangent_own.astype(jnp.float32)
+    grad_hidden = grad_out + normalize_back(grad_norm2, unit_two, inv_two, gain_two)
+    branch_all = gather_rows(grad_hidden.astype(jnp.bfloat16))
+    grad_attn = (
+        mm(out_full, branch_all, 1, 1)
+        .astype(jnp.bfloat16)
+        .reshape(Z_PARTS, HD, plane_rows)
+    )
+    grad_parts = to_heads(grad_attn, z_index)
+    proj_parts, bias_sums = attend_heads_back(
+        slot_of, low_tile, grad_parts, packed, attn_exact, log_norm, start_row, all_cos, all_sin
+    )
+    bias_grad = jnp.sum(bias_sums, axis=1).reshape(3, HD)
+    grad_proj = from_heads(proj_parts, z_index).reshape(Z_PARTS, 3, HD, plane_rows)
+    grad_proj = grad_proj.transpose(1, 0, 2, 3).reshape(3 * heads_width, plane_rows)
+    grad_norm1 = scatter_rows(mm(grad_proj, qkv_full, 0, 1))
+
+    out_sum_even = ring_scatter(
+        [mm(attn_t, p) for p in pieces_of(branch_all, chunk, 0, row_block)], 1
+    )
+    out_sum_odd = ring_scatter(
+        [mm(attn_t, p) for p in pieces_of(branch_all, chunk, row_block, row_block)], -1
+    )
+    out_parts = from_even_odd(out_sum_even, out_sum_odd, y_index)
+    out_grad = jnp.stack(
+        [p.reshape(Z_PARTS, HD, row_block) for p in out_parts], axis=1
+    ).reshape(w_out.shape)
+    qkv_sum_even = ring_scatter(
+        [mm(p, grad_proj, 0, 1) for p in pieces_of(norm1_all, chunk, 0, row_block)], 1
+    )
+    qkv_sum_odd = ring_scatter(
+        [mm(p, grad_proj, 0, 1) for p in pieces_of(norm1_all, chunk, row_block, row_block)], -1
+    )
+    qkv_grad_parts = from_even_odd(qkv_sum_even, qkv_sum_odd, y_index)
+    qkv_grad = jnp.stack(
+        [p.reshape(row_block, 3, Z_PARTS, HD) for p in qkv_grad_parts], axis=3
+    ).reshape(w_qkv.shape)
+
+    input_grad = grad_hidden + normalize_back(grad_norm1, unit_one, inv_one, gain_one)
+    sums = jnp.stack(
+        [
+            jnp.sum(grad_norm1 * unit_one, axis=0),
+            jnp.sum(grad_norm1, axis=0),
+            jnp.sum(grad_norm2 * unit_two, axis=0),
+            jnp.sum(grad_norm2, axis=0),
+        ],
+        axis=0,
+    )
+    norm_sums = lax.psum_scatter(
+        split_order(sums, z_index, 1), ("head", "blk"), scatter_dimension=1, tiled=True
+    )
+    return (
+        output,
+        split_order(input_grad, z_index, 1),
+        norm_sums[0],
+        norm_sums[1],
+        qkv_grad,
+        bias_grad,
+        out_grad,
+        norm_sums[2],
+        norm_sums[3],
+        gate_grad,
+        up_grad,
+        down_grad,
+    )
+
+
 def solution(mesh):
     placed = (
         P(("head", "blk"), None),
@@ -378,8 +965,9 @@
         P(),
         P(),
     )
+    heads_plan = mesh.shape["head"] == 4 and mesh.shape["blk"] == 2 * Z_PARTS
     return jax.shard_map(
-        on_device,
+        on_device_heads if heads_plan else on_device,
         mesh=mesh,
         in_specs=placed,
         out_specs=(

time: 1940 us -> 916 us (0.47)
  waiting for transfers between devices: 1360 us -> 531 us
  matrix products: 336 us -> 66.5 us
  starting transfers between devices: 2.26 us -> 136 us
  Pallas kernels: 0 us -> 46.2 us
  blocking collectives: 43.1 us -> 0 us
  other arithmetic: 76.9 us -> 42.6 us
  local copies, waits for them, and re-layouts: 93.3 us -> 71.6 us
    reduce_scatter x11 -> x0, waiting for transfers between devices: 725 us -> none  [the longest x1 111 us: on_device(): lax.psum_scatter(grad_w_gate.astype(jnp.bfloat16), 'blk', scatter_dimensi...]
    all_gather x11 -> x0, waiting for transfers between devices: 572 us -> none  [the longest x1 97.6 us: on_device(): lax.all_gather(w_qkv, 'blk', axis=0, tiled=True)]
    ppermute x0 -> x110, waiting for transfers between devices: none -> 399 us  [the longest x60 319 us: shift_z(): lax.ppermute(values, 'blk', [(b, (b + 2 * amount) % total) for b in range...]
    dot_general x51 -> x42, matrix products: 336 us -> 66.5 us  [mm(): lax.dot_general(left, right, (((left_dim,), (right_dim,)), ((), ())), pre...]
    ppermute x0 -> x110, starting transfers between devices: none -> 136 us  [the longest x60 92.9 us: shift_z(): lax.ppermute(values, 'blk', [(b, (b + 2 * amount) % total) for b in range...]
    unnamed x24 -> x2, waiting for transfers between devices: 67 us -> 132 us
    pallas_call x0 -> x2, Pallas kernels: none -> 46.2 us  [the longest x1 26.4 us: attend_heads_back(): pl.pallas_call(attend_back_kernel, grid_spec=pltpu.PrefetchScalarGridSpec...]
    unnamed x1 -> x0, blocking collectives: 43.1 us -> none
  transfers between devices with their start and end apart: 23 -> 111, of which waited for: 22 -> 52; matrix products, arithmetic and copies ran while one was open for 15% -> 16% of each run, Pallas kernels for 0% -> 5%
where the time goes in v1:
time: 916 us; the launch traced here: 911 us
  waiting for transfers between devices  531 us (58%)
  starting transfers between devices  136 us (15%)
  local copies, waits for them, and re-layouts  71.6 us (8%)
  matrix products  66.5 us (7%)
  Pallas kernels  46.2 us (5%)
  other arithmetic  42.6 us (5%)
  between operations  16.9 us (2%)
    ppermute x60, waiting for transfers between devices, shift_z(): lax.ppermute(values, 'blk', [(b, (b + 2 * amount) % total) for b in range...  319 us
    unnamed x2, waiting for transfers between devices  132 us
    ppermute x60, starting transfers between devices, shift_z(): lax.ppermute(values, 'blk', [(b, (b + 2 * amount) % total) for b in range...  92.9 us
    dot_general x42, matrix products, mm(): lax.dot_general(left, right, (((left_dim,), (right_dim,)), ((), ())), pre...  66.5 us
    ppermute x26, waiting for transfers between devices, swap_y(): return lax.ppermute(values, 'blk', [(b, b ^ 1) for b in range(2 * Z_PARTS)])  51.4 us
    unnamed x227, local copies, waits for them, and re-layouts  42.2 us
    ppermute x16, waiting for transfers between devices, swap_x(): return lax.ppermute(values, 'head', [(h, h ^ 2) for h in range(4)])  28.1 us
    pallas_call x1, Pallas kernels, attend_heads_back(): pl.pallas_call(attend_back_kernel, grid_spec=pltpu.PrefetchScalarGridSpec...  26.4 us
  transfers between devices with their start and end apart: 111, of which 52 were waited for; matrix products, arithmetic and copies ran while one was open for 16% of the time, Pallas kernels for 5%

profile of v1, /device:TPU:0, one launch (start us, length us, event | category | flops | bytes accessed | tf_op | source)
XLA Modules:
  0.0 910.5 jit_solution(14854688602424167744)
XLA Ops:
  38.8 4.1 collective-permute-start.2
  60.7 9.1 collective-permute-done.1
  69.8 6.6 collective-permute-done.3
  83.1 17.7 %collective-permute-done.19 = bf16[256,256]{1,0:T(8,128)(2,1)S(1)} collective-permute-done((bf16[256,256]{1,0:T(8,128)(2,1)S(1)}, bf16[256,256]{1,0:T(8,128)(2,1)S(1)}, u32[]{:S(2)}, u32[]{:S(2)}) %collective-permute-start.19) | collective-permute-done | bytes 131104 | tf_op jit(solution)/shard_map/ppermute | solution.py:394
  108.8 9.6 %collective-permute-done.6 = bf16[256,768]{1,0:T(8,128)(2,1)S(1)} collective-permute-done((bf16[256,768]{1,0:T(8,128)(2,1)S(1)}, bf16[256,768]{1,0:T(8,128)(2,1)S(1)}, u32[]{:S(2)}, u32[]{:S(2)}) %collective-permute-start.6) | collective-permute-done | bytes 393248 | tf_op jit(solution)/shard_map/ppermute | solution.py:394
  133.4 8.3 collective-permute-done.12
  142.2 13.8 %collective-permute-done.13 = bf16[192,1024]{1,0:T(8,128)(2,1)S(1)} collective-permute-done((bf16[192,1024]{1,0:T(8,128)(2,1)S(1)}, bf16[192,1024]{1,0:T(8,128)(2,1)S(1)}, u32[]{:S(2)}, u32[]{:S(2)}) %collective-permute-start.13) | collective-permute-done | bytes 393248 | tf_op jit(solution)/shard_map/ppermute | solution.py:394
  156.5 9.1 %collective-permute-start.24 = (bf16[256,256]{1,0:T(8,128)(2,1)S(1)}, bf16[256,256]{1,0:T(8,128)(2,1)S(1)}, u32[]{:S(2)}, u32[]{:S(2)}) collective-permute-start(bf16[256,256]{1,0:T(8,128)(2,1)S(1)} %collective-permute-done.23), channel_id=1, source_target_pairs={{0,2},{1,3},{2,4},{3,5},{4,6},{5,7},{6,0},{7,1},{8,10},{9,11},{10,... | collective-permute-start | bytes 393224 | tf_op jit(solution)/shard_map/ppermute | solution.py:394
  165.8 19.7 %attend.1 = (bf16[4,64,1024]{2,1,0:T(8,128)(2,1)S(1)}, f32[64,4096]{1,0:T(8,128)S(1)}, f32[1,4096]{1,0:T(1,128)S(1)}, bf16[192,4096]{1,0:T(8,128)(2,1)S(1)}) custom-call(s32[32]{0:T(128)S(1)} %select_reduce_fusion.2.slot_ref, s32[8]{0:T(128)S(1)} %and_select_fusion.low_ref, bf16[4,192,1024]{2,1,0:T(8,128)(2,1)S(1)} %pad_maximum_fusion.1.qkv_ref, ...), custom_call_target="tpu_custom_call" | custom-call | flops 1073741824 | bytes 6291456 | tf_op jit(solution)/shard_map/attend/pallas_call | solution.py:648
  185.8 4.9 collective-permute-done.15
  190.7 6.7 collective-permute-done.16
  197.4 6.7 collective-permute-done.17
  212.6 4.9 collective-permute-done.35
  226.2 6.7 collective-permute-done.26
  237.7 4.3 collective-permute-done.58
  243.9 36.9 %collective-permute-done.46 = bf16[704,256]{1,0:T(8,128)(2,1)S(1)} collective-permute-done((bf16[704,256]{1,0:T(8,128)(2,1)S(1)}, bf16[704,256]{1,0:T(8,128)(2,1)S(1)}, u32[]{:S(2)}, u32[]{:S(2)}) %collective-permute-start.46) | collective-permute-done | bytes 360480 | tf_op jit(solution)/shard_map/ppermute | solution.py:394
  287.2 6.8 collective-permute-done.47
  299.8 28.5 %collective-permute-done.41 = bf16[512,704]{0,1:T(8,128)(2,1)S(1)} collective-permute-done((bf16[512,704]{0,1:T(8,128)(2,1)S(1)}, bf16[512,704]{0,1:T(8,128)(2,1)S(1)}, u32[]{:S(2)}, u32[]{:S(2)}) %collective-permute-start.41) | collective-permute-done | bytes 720928 | tf_op jit(solution)/shard_map/ppermute | solution.py:394
  332.7 8.8 collective-permute-done.49
  341.6 14.0 %collective-permute-done.42 = bf16[512,704]{0,1:T(8,128)(2,1)S(1)} collective-permute-done((bf16[512,704]{0,1:T(8,128)(2,1)S(1)}, bf16[512,704]{0,1:T(8,128)(2,1)S(1)}, u32[]{:S(2)}, u32[]{:S(2)}) %collective-permute-start.42) | collective-permute-done | bytes 720928 | tf_op jit(solution)/shard_map/ppermute | solution.py:394
  356.0 14.8 %collective-permute-done.38 = bf16[512,704]{0,1:T(8,128)(2,1)S(1)} collective-permute-done((bf16[512,704]{0,1:T(8,128)(2,1)S(1)}, bf16[512,704]{0,1:T(8,128)(2,1)S(1)}, u32[]{:S(2)}, u32[]{:S(2)}) %collective-permute-start.38) | collective-permute-done | bytes 720928 | tf_op jit(solution)/shard_map/ppermute | solution.py:394
  377.6 4.4 multiply_convert_fusion.1
  390.8 5.8 fusion.155
  403.0 4.9 collective-permute-done.103
  412.1 18.2 %collective-permute-done.107 = bf16[704,256]{1,0:T(8,128)(2,1)S(1)} collective-permute-done((bf16[704,256]{1,0:T(8,128)(2,1)S(1)}, bf16[704,256]{1,0:T(8,128)(2,1)S(1)}, u32[]{:S(2)}, u32[]{:S(2)}) %collective-permute-start.107) | collective-permute-done | bytes 360480 | tf_op jit(solution)/shard_map/ppermute | solution.py:394
  433.9 5.0 collective-permute-done.104
  439.9 5.9 convolution_add_fusion
  446.1 21.5 %collective-permute-done.105 = bf16[704,256]{1,0:T(8,128)(2,1)S(1)} collective-permute-done((bf16[704,256]{1,0:T(8,128)(2,1)S(1)}, bf16[704,256]{1,0:T(8,128)(2,1)S(1)}, u32[]{:S(2)}, u32[]{:S(2)}) %collective-permute-start.105) | collective-permute-done | bytes 360480 | tf_op jit(solution)/shard_map/ppermute | solution.py:394
  477.0 4.6 collective-permute-done.109
  498.1 4.6 collective-permute-done.63
  514.3 7.3 collective-permute-done.62
  528.6 8.6 collective-permute-done.66
  551.6 6.4 collective-permute-done.102
  559.8 5.6 collective-permute-done.98
  596.8 26.4 %attend_back.1 = (bf16[4,192,1024]{2,1,0:T(8,128)(2,1)S(1)}, f32[192,128]{1,0:T(8,128)S(1)}) custom-call(s32[32]{0:T(128)S(1)} %select_reduce_fusion.2.slot_ref, s32[8]{0:T(128)S(1)} %and_select_fusion.low_ref, bf16[4,64,1024]{2,1,0:T(8,128)(2,1)S(1)} %pad_maximum_fusion.18.grad_ref, bf16[192,4096]{1,0:T(8,128)(2,1)} %copy-done, ...), custom_call_target="tpu_custom_call" | custom-call | flops 3221225472 | bytes 8388608 | tf_op jit(solution)/shard_map/attend_back/pallas_call | solution.py:677
  624.5 8.3 collective-permute-start.73
  639.7 5.6 collective-permute-done.93
  651.7 19.0 %collective-permute-done.74 = bf16[192,1024]{1,0:T(8,128)(2,1)S(1)} collective-permute-done((bf16[192,1024]{1,0:T(8,128)(2,1)}, bf16[192,1024]{1,0:T(8,128)(2,1)S(1)}, u32[]{:S(2)}, u32[]{:S(2)}) %collective-permute-start.74) | collective-permute-done | bytes 393248 | tf_op jit(solution)/shard_map/ppermute | solution.py:394
  689.6 6.4 collective-permute-done.84
  696.6 4.4 collective-permute-start.85
  701.0 6.7 collective-permute-done.81
  709.5 6.3 collective-permute-done.85
  717.6 7.0 collective-permute-done.82
  727.9 5.0 collective-permute-done.86
  733.0 7.6 collective-permute-done.83
  746.7 6.5 collective-permute-done.87
  756.0 6.8 collective-permute-done.80
  768.1 131.8 %reduce-scatter.4.cloned.1.call-done = f32[64,4]{1,0:T(8,128)} async-done(((f32[2048,4]{1,0:T(8,128)}), f32[64,4]{1,0:T(8,128)}) %reduce-scatter.4.cloned.1.call-update) | async-done | bytes 1040
  (598 shorter events, 300.9 us)
Async XLA Ops:
  7.2 892.7 %reduce-scatter.4.cloned.1.call-start = ((), (), s32[]{:S(2)}) async-start(), calls=%async_computation.1 | async-start | bytes 1081344
  11.3 34.1 %collective-permute-start.7 = (bf16[128,2048]{1,0:T(8,128)(2,1)}, bf16[128,2048]{1,0:T(8,128)(2,1)}, u32[]{:S(2)}, u32[]{:S(2)}) collective-permute-start(bf16[128,2048]{1,0:T(8,128)(2,1)} %get-tuple-element.122), channel_id=1, source_target_pairs={{0,1},{1,0},{2,3},{3,2},{4,5},{5,4},{6,7},{7,6},{8,9},{9,8},{10,11... | collective-permute-start | bytes 1572872 | tf_op jit(solution)/shard_map/ppermute | solution.py:389
  14.4 28.5 %collective-permute-start.8 = (bf16[128,2048]{1,0:T(8,128)(2,1)}, bf16[128,2048]{1,0:T(8,128)(2,1)}, u32[]{:S(2)}, u32[]{:S(2)}) collective-permute-start(bf16[128,2048]{1,0:T(8,128)(2,1)} %get-tuple-element.122), channel_id=1, source_target_pairs={{0,16},{8,24},{16,0},{24,8},{1,17},{9,25},{17,1},{25,9},{2,18},{10... | collective-permute-start | bytes 1572872 | tf_op jit(solution)/shard_map/ppermute | solution.py:381
  19.1 40.6 %collective-permute-start.18 = (bf16[256,256]{1,0:T(8,128)(2,1)}, bf16[256,256]{1,0:T(8,128)(2,1)}, u32[]{:S(2)}, u32[]{:S(2)}) collective-permute-start(bf16[256,256]{1,0:T(8,128)(2,1)} %bitcast.28), channel_id=1, source_target_pairs={{0,1},{1,0},{2,3},{3,2},{4,5},{5,4},{6,7},{7,6},{8,9},{9,8},{10,11... | collective-permute-start | bytes 393224 | tf_op jit(solution)/shard_map/ppermute | solution.py:389
  54.2 66.9 %collective-permute-start.11 = (bf16[512,2048]{1,0:T(8,128)(2,1)}, bf16[512,2048]{1,0:T(8,128)(2,1)}, u32[]{:S(2)}, u32[]{:S(2)}) collective-permute-start(bf16[512,2048]{1,0:T(8,128)(2,1)} %get-tuple-element.242), channel_id=1, source_target_pairs={{0,8},{8,0},{16,24},{24,16},{1,9},{9,1},{17,25},{25,17},{2,10},{10... | collective-permute-start | bytes 6291464 | tf_op jit(solution)/shard_map/ppermute | solution.py:385
  69.8 34.8 %collective-permute-start.5 = (bf16[256,768]{1,0:T(8,128)(2,1)S(1)}, bf16[256,768]{1,0:T(8,128)(2,1)S(1)}, u32[]{:S(2)}, u32[]{:S(2)}) collective-permute-start(bf16[256,768]{1,0:T(8,128)(2,1)S(1)} %collective-permute-done.1), channel_id=1, source_target_pairs={{0,2},{1,3},{2,4},{3,5},{4,6},{5,7},{6,0},{7,1},{8,10},{9,11},{10,... | collective-permute-start | bytes 1179656 | tf_op jit(solution)/shard_map/ppermute | solution.py:394
  76.4 29.0 %collective-permute-start.4 = (bf16[256,768]{1,0:T(8,128)(2,1)S(1)}, bf16[256,768]{1,0:T(8,128)(2,1)}, u32[]{:S(2)}, u32[]{:S(2)}) collective-permute-start(bf16[256,768]{1,0:T(8,128)(2,1)S(1)} %collective-permute-done.3), channel_id=1, source_target_pairs={{0,6},{1,7},{2,0},{3,1},{4,2},{5,3},{6,4},{7,5},{8,14},{9,15},{10,... | collective-permute-start | bytes 1179656 | tf_op jit(solution)/shard_map/ppermute | solution.py:394
  100.8 31.4 %collective-permute-start.23 = (bf16[256,256]{1,0:T(8,128)(2,1)S(1)}, bf16[256,256]{1,0:T(8,128)(2,1)S(1)}, u32[]{:S(2)}, u32[]{:S(2)}) collective-permute-start(bf16[256,256]{1,0:T(8,128)(2,1)S(1)} %collective-permute-done.19), channel_id=1, source_target_pairs={{0,2},{1,3},{2,4},{3,5},{4,6},{5,7},{6,0},{7,1},{8,10},{9,11},{10,... | collective-permute-start | bytes 393224 | tf_op jit(solution)/shard_map/ppermute | solution.py:394
  101.3 30.4 %collective-permute-start.22 = (bf16[256,256]{1,0:T(8,128)(2,1)S(1)}, bf16[256,256]{1,0:T(8,128)(2,1)S(1)}, u32[]{:S(2)}, u32[]{:S(2)}) collective-permute-start(bf16[256,256]{1,0:T(8,128)(2,1)S(1)} %collective-permute-done.21), channel_id=1, source_target_pairs={{0,6},{1,7},{2,0},{3,1},{4,2},{5,3},{6,4},{7,5},{8,14},{9,15},{10,... | collective-permute-start | bytes 393224 | tf_op jit(solution)/shard_map/ppermute | solution.py:394
  127.8 28.2 %collective-permute-start.13 = (bf16[192,1024]{1,0:T(8,128)(2,1)S(1)}, bf16[192,1024]{1,0:T(8,128)(2,1)S(1)}, u32[]{:S(2)}, u32[]{:S(2)}) collective-permute-start(bf16[192,1024]{1,0:T(8,128)(2,1)S(1)} %get-tuple-element.170), channel_id=1, source_target_pairs={{0,4},{1,5},{2,6},{3,7},{4,0},{5,1},{6,2},{7,3},{8,12},{9,13},{10,... | collective-permute-start | bytes 1179656 | tf_op jit(solution)/shard_map/ppermute | solution.py:394
  128.3 28.2 %collective-permute-start.14 = (bf16[192,1024]{1,0:T(8,128)(2,1)S(1)}, bf16[192,1024]{1,0:T(8,128)(2,1)S(1)}, u32[]{:S(2)}, u32[]{:S(2)}) collective-permute-start(bf16[192,1024]{1,0:T(8,128)(2,1)S(1)} %get-tuple-element.169), channel_id=1, source_target_pairs={{0,6},{1,7},{2,0},{3,1},{4,2},{5,3},{6,4},{7,5},{8,14},{9,15},{10,... | collective-permute-start | bytes 1179656 | tf_op jit(solution)/shard_map/ppermute | solution.py:394
  131.6 91.6 %collective-permute-start.55 = (bf16[128,2048]{1,0:T(8,128)(2,1)}, bf16[128,2048]{1,0:T(8,128)(2,1)S(1)}, u32[]{:S(2)}, u32[]{:S(2)}) collective-permute-start(bf16[128,2048]{1,0:T(8,128)(2,1)} %get-tuple-element.201), channel_id=1, source_target_pairs={{0,1},{1,0},{2,3},{3,2},{4,5},{5,4},{6,7},{7,6},{8,9},{9,8},{10,11... | collective-permute-start | bytes 1572872 | tf_op jit(solution)/shard_map/ppermute | solution.py:389
  132.2 87.6 %collective-permute-start.56 = (bf16[128,2048]{1,0:T(8,128)(2,1)}, bf16[128,2048]{1,0:T(8,128)(2,1)S(1)}, u32[]{:S(2)}, u32[]{:S(2)}) collective-permute-start(bf16[128,2048]{1,0:T(8,128)(2,1)} %get-tuple-element.201), channel_id=1, source_target_pairs={{0,16},{8,24},{16,0},{24,8},{1,17},{9,25},{17,1},{25,9},{2,18},{10... | collective-permute-start | bytes 1572872 | tf_op jit(solution)/shard_map/ppermute | solution.py:381
  141.7 68.1 %collective-permute-start.39 = (bf16[256,704]{0,1:T(8,128)(2,1)S(1)}, bf16[256,704]{0,1:T(8,128)(2,1)S(1)}, u32[]{:S(2)}, u32[]{:S(2)}) collective-permute-start(bf16[256,704]{0,1:T(8,128)(2,1)S(1)} %copy-done.41), channel_id=1, source_target_pairs={{0,1},{1,0},{2,3},{3,2},{4,5},{5,4},{6,7},{7,6},{8,9},{9,8},{10,11... | collective-permute-start | bytes 1081352 | tf_op jit(solution)/shard_map/ppermute | solution.py:389
  156.0 50.5 %collective-permute-start.43 = (bf16[704,256]{1,0:T(8,128)(2,1)S(1)}, bf16[704,256]{1,0:T(8,128)(2,1)S(1)}, u32[]{:S(2)}, u32[]{:S(2)}) collective-permute-start(bf16[704,256]{1,0:T(8,128)(2,1)S(1)} %copy-done.42), channel_id=1, source_target_pairs={{0,1},{1,0},{2,3},{3,2},{4,5},{5,4},{6,7},{7,6},{8,9},{9,8},{10,11... | collective-permute-start | bytes 1081352 | tf_op jit(solution)/shard_map/ppermute | solution.py:389
  156.5 29.1 %collective-permute-start.24 = (bf16[256,256]{1,0:T(8,128)(2,1)S(1)}, bf16[256,256]{1,0:T(8,128)(2,1)S(1)}, u32[]{:S(2)}, u32[]{:S(2)}) collective-permute-start(bf16[256,256]{1,0:T(8,128)(2,1)S(1)} %collective-permute-done.23), channel_id=1, source_target_pairs={{0,2},{1,3},{2,4},{3,5},{4,6},{5,7},{6,0},{7,1},{8,10},{9,11},{10,... | collective-permute-start | bytes 393224 | tf_op jit(solution)/shard_map/ppermute | solution.py:394
  209.8 25.4 %collective-permute-start.44 = (bf16[704,256]{1,0:T(8,128)(2,1)S(1)}, bf16[704,256]{1,0:T(8,128)(2,1)S(1)}, u32[]{:S(2)}, u32[]{:S(2)}) collective-permute-start(bf16[704,256]{1,0:T(8,128)(2,1)S(1)} %get-tuple-element.106), channel_id=1, source_target_pairs={{0,2},{1,3},{2,4},{3,5},{4,6},{5,7},{6,0},{7,1},{8,10},{9,11},{10,... | collective-permute-start | bytes 1081352 | tf_op jit(solution)/shard_map/ppermute | solution.py:394
  234.1 49.1 %collective-permute-start.27 = (bf16[128,2048]{1,0:T(8,128)(2,1)S(1)}, bf16[128,2048]{1,0:T(8,128)(2,1)S(1)}, u32[]{:S(2)}, u32[]{:S(2)}) collective-permute-start(bf16[128,2048]{1,0:T(8,128)(2,1)S(1)} %pad_maximum_fusion.10), channel_id=1, source_target_pairs={{0,16},{8,24},{16,0},{24,8},{1,17},{9,25},{17,1},{25,9},{2,18},{10... | collective-permute-start | bytes 1572872 | tf_op jit(solution)/shard_map/ppermute | solution.py:381
  235.2 49.5 %collective-permute-start.29 = (bf16[128,2048]{1,0:T(8,128)(2,1)S(1)}, bf16[128,2048]{1,0:T(8,128)(2,1)S(1)}, u32[]{:S(2)}, u32[]{:S(2)}) collective-permute-start(bf16[128,2048]{1,0:T(8,128)(2,1)S(1)} %pad_maximum_fusion.11), channel_id=1, source_target_pairs={{0,1},{1,0},{2,3},{3,2},{4,5},{5,4},{6,7},{7,6},{8,9},{9,8},{10,11... | collective-permute-start | bytes 1572872 | tf_op jit(solution)/shard_map/ppermute | solution.py:389
  236.8 57.2 %collective-permute-start.40 = (bf16[512,704]{0,1:T(8,128)(2,1)S(1)}, bf16[512,704]{0,1:T(8,128)(2,1)S(1)}, u32[]{:S(2)}, u32[]{:S(2)}) collective-permute-start(bf16[512,704]{0,1:T(8,128)(2,1)S(1)} %pad_maximum_fusion.8), channel_id=1, source_target_pairs={{0,6},{1,7},{2,0},{3,1},{4,2},{5,3},{6,4},{7,5},{8,14},{9,15},{10,... | collective-permute-start | bytes 2162696 | tf_op jit(solution)/shard_map/ppermute | solution.py:394
  236.9 44.0 %collective-permute-start.46 = (bf16[704,256]{1,0:T(8,128)(2,1)S(1)}, bf16[704,256]{1,0:T(8,128)(2,1)S(1)}, u32[]{:S(2)}, u32[]{:S(2)}) collective-permute-start(bf16[704,256]{1,0:T(8,128)(2,1)S(1)} %collective-permute-done.45), channel_id=1, source_target_pairs={{0,6},{1,7},{2,0},{3,1},{4,2},{5,3},{6,4},{7,5},{8,14},{9,15},{10,... | collective-permute-start | bytes 1081352 | tf_op jit(solution)/shard_map/ppermute | solution.py:394
  242.1 43.9 %collective-permute-start.36 = (bf16[512,704]{0,1:T(8,128)(2,1)S(1)}, bf16[512,704]{0,1:T(8,128)(2,1)S(1)}, u32[]{:S(2)}, u32[]{:S(2)}) collective-permute-start(bf16[512,704]{0,1:T(8,128)(2,1)S(1)} %pad_maximum_fusion.7), channel_id=1, source_target_pairs={{0,2},{1,3},{2,4},{3,5},{4,6},{5,7},{6,0},{7,1},{8,10},{9,11},{10,... | collective-permute-start | bytes 2162696 | tf_op jit(solution)/shard_map/ppermute | solution.py:394
  294.0 76.9 %collective-permute-start.59 = (bf16[512,2048]{1,0:T(8,128)(2,1)S(1)}, bf16[512,2048]{1,0:T(8,128)(2,1)S(1)}, u32[]{:S(2)}, u32[]{:S(2)}) collective-permute-start(bf16[512,2048]{1,0:T(8,128)(2,1)S(1)} %get-tuple-element.230), channel_id=1, source_target_pairs={{0,8},{8,0},{16,24},{24,16},{1,9},{9,1},{17,25},{25,17},{2,10},{10... | collective-permute-start | bytes 6291464 | tf_op jit(solution)/shard_map/ppermute | solution.py:385
  294.0 38.4 %collective-permute-start.37 = (bf16[512,704]{0,1:T(8,128)(2,1)S(1)}, bf16[512,704]{0,1:T(8,128)(2,1)S(1)}, u32[]{:S(2)}, u32[]{:S(2)}) collective-permute-start(bf16[512,704]{0,1:T(8,128)(2,1)S(1)} %collective-permute-done.36), channel_id=1, source_target_pairs={{0,2},{1,3},{2,4},{3,5},{4,6},{5,7},{6,0},{7,1},{8,10},{9,11},{10,... | collective-permute-start | bytes 2162696 | tf_op jit(solution)/shard_map/ppermute | solution.py:394
  294.6 33.7 %collective-permute-start.41 = (bf16[512,704]{0,1:T(8,128)(2,1)S(1)}, bf16[512,704]{0,1:T(8,128)(2,1)S(1)}, u32[]{:S(2)}, u32[]{:S(2)}) collective-permute-start(bf16[512,704]{0,1:T(8,128)(2,1)S(1)} %collective-permute-done.40), channel_id=1, source_target_pairs={{0,6},{1,7},{2,0},{3,1},{4,2},{5,3},{6,4},{7,5},{8,14},{9,15},{10,... | collective-permute-start | bytes 2162696 | tf_op jit(solution)/shard_map/ppermute | solution.py:394
  298.1 31.5 %collective-permute-start.32 = (bf16[64,2048]{1,0:T(8,128)(2,1)S(1)}, bf16[64,2048]{1,0:T(8,128)(2,1)S(1)}, u32[]{:S(2)}, u32[]{:S(2)}) collective-permute-start(bf16[64,2048]{1,0:T(8,128)(2,1)S(1)} %slice.503), channel_id=1, source_target_pairs={{0,1},{1,0},{2,3},{3,2},{4,5},{5,4},{6,7},{7,6},{8,9},{9,8},{10,11... | collective-permute-start | bytes 786440 | tf_op jit(solution)/shard_map/ppermute | solution.py:389
  298.4 33.8 %collective-permute-start.33 = (bf16[64,2048]{1,0:T(8,128)(2,1)S(1)}, bf16[64,2048]{1,0:T(8,128)(2,1)S(1)}, u32[]{:S(2)}, u32[]{:S(2)}) collective-permute-start(bf16[64,2048]{1,0:T(8,128)(2,1)S(1)} %slice.504), channel_id=1, source_target_pairs={{0,16},{8,24},{16,0},{24,8},{1,17},{9,25},{17,1},{25,9},{2,18},{10... | collective-permute-start | bytes 786440 | tf_op jit(solution)/shard_map/ppermute | solution.py:381
  329.6 26.1 %collective-permute-start.42 = (bf16[512,704]{0,1:T(8,128)(2,1)S(1)}, bf16[512,704]{0,1:T(8,128)(2,1)S(1)}, u32[]{:S(2)}, u32[]{:S(2)}) collective-permute-start(bf16[512,704]{0,1:T(8,128)(2,1)S(1)} %collective-permute-done.41), channel_id=1, source_target_pairs={{0,6},{1,7},{2,0},{3,1},{4,2},{5,3},{6,4},{7,5},{8,14},{9,15},{10,... | collective-permute-start | bytes 2162696 | tf_op jit(solution)/shard_map/ppermute | solution.py:394
  332.3 41.9 %collective-permute-start.34 = (bf16[512,2048]{1,0:T(8,128)(2,1)S(1)}, bf16[512,2048]{1,0:T(8,128)(2,1)S(1)}, u32[]{:S(2)}, u32[]{:S(2)}) collective-permute-start(bf16[512,2048]{1,0:T(8,128)(2,1)S(1)} %get-tuple-element.234), channel_id=1, source_target_pairs={{0,8},{8,0},{16,24},{24,16},{1,9},{9,1},{17,25},{25,17},{2,10},{10... | collective-permute-start | bytes 6291464 | tf_op jit(solution)/shard_map/ppermute | solution.py:385
  332.4 38.3 %collective-permute-start.38 = (bf16[512,704]{0,1:T(8,128)(2,1)S(1)}, bf16[512,704]{0,1:T(8,128)(2,1)S(1)}, u32[]{:S(2)}, u32[]{:S(2)}) collective-permute-start(bf16[512,704]{0,1:T(8,128)(2,1)S(1)} %collective-permute-done.37), channel_id=1, source_target_pairs={{0,2},{1,3},{2,4},{3,5},{4,6},{5,7},{6,0},{7,1},{8,10},{9,11},{10,... | collective-permute-start | bytes 2162696 | tf_op jit(solution)/shard_map/ppermute | solution.py:394
  398.9 72.3 %collective-permute-start.99 = (bf16[512,704]{0,1:T(8,128)(2,1)S(1)}, bf16[512,704]{0,1:T(8,128)(2,1)S(1)}, u32[]{:S(2)}, u32[]{:S(2)}) collective-permute-start(bf16[512,704]{0,1:T(8,128)(2,1)S(1)} %convolution_convert_fusion), channel_id=1, source_target_pairs={{0,6},{1,7},{2,0},{3,1},{4,2},{5,3},{6,4},{7,5},{8,14},{9,15},{10,... | collective-permute-start | bytes 2162696 | tf_op jit(solution)/shard_map/ppermute | solution.py:394
  401.8 28.6 %collective-permute-start.107 = (bf16[704,256]{1,0:T(8,128)(2,1)S(1)}, bf16[704,256]{1,0:T(8,128)(2,1)S(1)}, u32[]{:S(2)}, u32[]{:S(2)}) collective-permute-start(bf16[704,256]{1,0:T(8,128)(2,1)S(1)} %add_convert_fusion.10), channel_id=1, source_target_pairs={{0,6},{1,7},{2,0},{3,1},{4,2},{5,3},{6,4},{7,5},{8,14},{9,15},{10,... | collective-permute-start | bytes 1081352 | tf_op jit(solution)/shard_map/ppermute | solution.py:394
  408.5 30.5 %collective-permute-start.104 = (bf16[704,256]{1,0:T(8,128)(2,1)S(1)}, bf16[704,256]{1,0:T(8,128)(2,1)S(1)}, u32[]{:S(2)}, u32[]{:S(2)}) collective-permute-start(bf16[704,256]{1,0:T(8,128)(2,1)S(1)} %add_convert_fusion.12), channel_id=1, source_target_pairs={{0,2},{1,3},{2,4},{3,5},{4,6},{5,7},{6,0},{7,1},{8,10},{9,11},{10,... | collective-permute-start | bytes 1081352 | tf_op jit(solution)/shard_map/ppermute | solution.py:394
  410.7 64.5 %collective-permute-start.95 = (bf16[512,704]{0,1:T(8,128)(2,1)}, bf16[512,704]{0,1:T(8,128)(2,1)S(1)}, u32[]{:S(2)}, u32[]{:S(2)}) collective-permute-start(bf16[512,704]{0,1:T(8,128)(2,1)} %convolution_convert_fusion.1), channel_id=1, source_target_pairs={{0,2},{1,3},{2,4},{3,5},{4,6},{5,7},{6,0},{7,1},{8,10},{9,11},{10,... | collective-permute-start | bytes 2162696 | tf_op jit(solution)/shard_map/ppermute | solution.py:394
  412.1 70.9 %collective-permute-start.50 = (bf16[512,2048]{1,0:T(8,128)(2,1)S(1)}, bf16[512,2048]{1,0:T(8,128)(2,1)S(1)}, u32[]{:S(2)}, u32[]{:S(2)}) collective-permute-start(bf16[512,2048]{1,0:T(8,128)(2,1)S(1)} %slice.784), channel_id=1, source_target_pairs={{0,8},{8,0},{16,24},{24,16},{1,9},{9,1},{17,25},{25,17},{2,10},{10... | collective-permute-start | bytes 6291464 | tf_op jit(solution)/shard_map/ppermute | solution.py:385
  430.9 38.3 %collective-permute-start.108 = (bf16[704,256]{1,0:T(8,128)(2,1)S(1)}, bf16[704,256]{1,0:T(8,128)(2,1)S(1)}, u32[]{:S(2)}, u32[]{:S(2)}) collective-permute-start(bf16[704,256]{1,0:T(8,128)(2,1)S(1)} %add_convert_fusion.9), channel_id=1, source_target_pairs={{0,6},{1,7},{2,0},{3,1},{4,2},{5,3},{6,4},{7,5},{8,14},{9,15},{10,... | collective-permute-start | bytes 1081352 | tf_op jit(solution)/shard_map/ppermute | solution.py:394
  439.5 28.1 %collective-permute-start.105 = (bf16[704,256]{1,0:T(8,128)(2,1)S(1)}, bf16[704,256]{1,0:T(8,128)(2,1)S(1)}, u32[]{:S(2)}, u32[]{:S(2)}) collective-permute-start(bf16[704,256]{1,0:T(8,128)(2,1)S(1)} %add_convert_fusion.11), channel_id=1, source_target_pairs={{0,2},{1,3},{2,4},{3,5},{4,6},{5,7},{6,0},{7,1},{8,10},{9,11},{10,... | collective-permute-start | bytes 1081352 | tf_op jit(solution)/shard_map/ppermute | solution.py:394
  473.0 31.0 %collective-permute-start.100 = (bf16[512,704]{0,1:T(8,128)(2,1)}, bf16[512,704]{0,1:T(8,128)(2,1)S(1)}, u32[]{:S(2)}, u32[]{:S(2)}) collective-permute-start(bf16[512,704]{0,1:T(8,128)(2,1)} %add_convert_fusion.1), channel_id=1, source_target_pairs={{0,6},{1,7},{2,0},{3,1},{4,2},{5,3},{6,4},{7,5},{8,14},{9,15},{10,... | collective-permute-start | bytes 2162696 | tf_op jit(solution)/shard_map/ppermute | solution.py:394
  477.0 30.7 %collective-permute-start.96 = (bf16[512,704]{0,1:T(8,128)(2,1)}, bf16[512,704]{0,1:T(8,128)(2,1)S(1)}, u32[]{:S(2)}, u32[]{:S(2)}) collective-permute-start(bf16[512,704]{0,1:T(8,128)(2,1)} %add_convert_fusion.3), channel_id=1, source_target_pairs={{0,2},{1,3},{2,4},{3,5},{4,6},{5,7},{6,0},{7,1},{8,10},{9,11},{10,... | collective-permute-start | bytes 2162696 | tf_op jit(solution)/shard_map/ppermute | solution.py:394
  513.9 33.5 %collective-permute-start.97 = (bf16[512,704]{0,1:T(8,128)(2,1)S(1)}, bf16[512,704]{0,1:T(8,128)(2,1)S(1)}, u32[]{:S(2)}, u32[]{:S(2)}) collective-permute-start(bf16[512,704]{0,1:T(8,128)(2,1)S(1)} %add_convert_fusion.2), channel_id=1, source_target_pairs={{0,2},{1,3},{2,4},{3,5},{4,6},{5,7},{6,0},{7,1},{8,10},{9,11},{10,... | collective-permute-start | bytes 2162696 | tf_op jit(solution)/shard_map/ppermute | solution.py:394
  546.6 24.0 %collective-permute-start.69 = (bf16[512,2048]{1,0:T(8,128)(2,1)}, bf16[512,2048]{1,0:T(8,128)(2,1)}, u32[]{:S(2)}, u32[]{:S(2)}) collective-permute-start(bf16[512,2048]{1,0:T(8,128)(2,1)} %get-tuple-element.226), channel_id=1, source_target_pairs={{0,8},{8,0},{16,24},{24,16},{1,9},{9,1},{17,25},{25,17},{2,10},{10... | collective-permute-start | bytes 6291464 | tf_op jit(solution)/shard_map/ppermute | solution.py:385
  586.4 46.3 %collective-permute-start.92 = (bf16[256,256]{1,0:T(8,128)(2,1)S(1)}, bf16[256,256]{1,0:T(8,128)(2,1)S(1)}, u32[]{:S(2)}, u32[]{:S(2)}) collective-permute-start(bf16[256,256]{1,0:T(8,128)(2,1)S(1)} %add_convert_fusion.14), channel_id=1, source_target_pairs={{0,6},{1,7},{2,0},{3,1},{4,2},{5,3},{6,4},{7,5},{8,14},{9,15},{10,... | collective-permute-start | bytes 393224 | tf_op jit(solution)/shard_map/ppermute | solution.py:394
  590.3 42.9 %collective-permute-start.89 = (bf16[256,256]{1,0:T(8,128)(2,1)S(1)}, bf16[256,256]{1,0:T(8,128)(2,1)S(1)}, u32[]{:S(2)}, u32[]{:S(2)}) collective-permute-start(bf16[256,256]{1,0:T(8,128)(2,1)S(1)} %add_convert_fusion.16), channel_id=1, source_target_pairs={{0,2},{1,3},{2,4},{3,5},{4,6},{5,7},{6,0},{7,1},{8,10},{9,11},{10,... | collective-permute-start | bytes 393224 | tf_op jit(solution)/shard_map/ppermute | solution.py:394
  624.5 26.5 %collective-permute-start.73 = (bf16[192,1024]{1,0:T(8,128)(2,1)}, bf16[192,1024]{1,0:T(8,128)(2,1)S(1)}, u32[]{:S(2)}, u32[]{:S(2)}) collective-permute-start(bf16[192,1024]{1,0:T(8,128)(2,1)} %get-tuple-element.167), channel_id=1, source_target_pairs={{0,6},{1,7},{2,0},{3,1},{4,2},{5,3},{6,4},{7,5},{8,14},{9,15},{10,... | collective-permute-start | bytes 1179656 | tf_op jit(solution)/shard_map/ppermute | solution.py:394
  636.5 34.3 %collective-permute-start.74 = (bf16[192,1024]{1,0:T(8,128)(2,1)}, bf16[192,1024]{1,0:T(8,128)(2,1)S(1)}, u32[]{:S(2)}, u32[]{:S(2)}) collective-permute-start(bf16[192,1024]{1,0:T(8,128)(2,1)} %get-tuple-element.166), channel_id=1, source_target_pairs={{0,4},{1,5},{2,6},{3,7},{4,0},{5,1},{6,2},{7,3},{8,12},{9,13},{10,... | collective-permute-start | bytes 1179656 | tf_op jit(solution)/shard_map/ppermute | solution.py:394
  636.5 35.0 %collective-permute-start.75 = (bf16[192,1024]{1,0:T(8,128)(2,1)}, bf16[192,1024]{1,0:T(8,128)(2,1)}, u32[]{:S(2)}, u32[]{:S(2)}) collective-permute-start(bf16[192,1024]{1,0:T(8,128)(2,1)} %get-tuple-element.164), channel_id=1, source_target_pairs={{0,2},{1,3},{2,4},{3,5},{4,6},{5,7},{6,0},{7,1},{8,10},{9,11},{10,... | collective-permute-start | bytes 1179656 | tf_op jit(solution)/shard_map/ppermute | solution.py:394
  650.2 58.2 %collective-permute-start.94 = (bf16[256,256]{1,0:T(8,128)(2,1)S(1)}, bf16[256,256]{1,0:T(8,128)(2,1)S(1)}, u32[]{:S(2)}, u32[]{:S(2)}) collective-permute-start(bf16[256,256]{1,0:T(8,128)(2,1)S(1)} %get-tuple-element.276), channel_id=1, source_target_pairs={{0,1},{1,0},{2,3},{3,2},{4,5},{5,4},{6,7},{7,6},{8,9},{9,8},{10,11... | collective-permute-start | bytes 393224 | tf_op jit(solution)/shard_map/ppermute | solution.py:389
  683.7 41.6 %collective-permute-start.76 = (bf16[512,2048]{1,0:T(8,128)(2,1)S(1)}, bf16[512,2048]{1,0:T(8,128)(2,1)S(1)}, u32[]{:S(2)}, u32[]{:S(2)}) collective-permute-start(bf16[512,2048]{1,0:T(8,128)(2,1)S(1)} %slice.782), channel_id=1, source_target_pairs={{0,8},{8,0},{16,24},{24,16},{1,9},{9,1},{17,25},{25,17},{2,10},{10... | collective-permute-start | bytes 6291464 | tf_op jit(solution)/shard_map/ppermute | solution.py:385
  (146 other events, 2925.8 us)
Sparse Core Ops, SparseCore 0:
  766.5 133.3 reduce-scatter.3

commit v2 on v1

--- a/solution.py
+++ b/solution.py
@@ -394,6 +394,10 @@
     return lax.ppermute(values, "blk", [(b, (b + 2 * amount) % total) for b in range(total)])
 
 
+def swap_low_z(values):
+    return lax.ppermute(values, "blk", [(b, b ^ 2) for b in range(2 * Z_PARTS)])
+
+
 def gather_rows(own):
     half = own.shape[0] // 2
     from_x = swap_x(own)
@@ -419,6 +423,22 @@
     last_x = swap_x(for_x.astype(jnp.bfloat16)).astype(jnp.float32)
     last_y = swap_y(for_y.astype(jnp.bfloat16)).astype(jnp.float32)
     return own + last_x + last_y
+
+
+def halve(values, bit, swap):
+    mine = lax.dynamic_index_in_dim(values, bit, axis=0, keepdims=False)
+    theirs = lax.dynamic_index_in_dim(values, 1 - bit, axis=0, keepdims=False)
+    return mine + swap(theirs)
+
+
+def scatter_sums(sums, x_index, core_index, z_index, y_index):
+    count, width = sums.shape
+    total = sums.reshape(count, 2, 2, 2, 2, 2, width // 32).transpose(1, 2, 3, 4, 5, 0, 6)
+    total = halve(total, x_index, swap_x)
+    total = halve(total, core_index, swap_core)
+    total = halve(total, z_index // 2, lambda v: shift_z(v, 2))
+    total = halve(total, z_index % 2, swap_low_z)
+    return halve(total, y_index, swap_y)
 
 
 def ring_gather(chunk, amount):
@@ -929,8 +949,8 @@
         ],
         axis=0,
     )
-    norm_sums = lax.psum_scatter(
-        split_order(sums, z_index, 1), ("head", "blk"), scatter_dimension=1, tiled=True
+    norm_sums = scatter_sums(
+        split_order(sums, z_index, 1), x_index, core_index, z_index, y_index
     )
     return (
         output,

time: 916 us -> 786 us (0.86)
  waiting for transfers between devices: 531 us -> 403 us
  between operations: 16.9 us -> 3.64 us
    unnamed x2 -> x0, waiting for transfers between devices: 132 us -> none
    ppermute x26 -> x27, starting transfers between devices: 25.6 us -> 28.6 us  [swap_y(): return lax.ppermute(values, 'blk', [(b, b ^ 1) for b in range(2 * Z_PARTS)])]
    ppermute x16 -> x17, starting transfers between devices: 17.2 us -> 20.1 us  [swap_x(): return lax.ppermute(values, 'head', [(h, h ^ 2) for h in range(4)])]
    ppermute x26 -> x27, waiting for transfers between devices: 51.4 us -> 49.3 us  [swap_y(): return lax.ppermute(values, 'blk', [(b, b ^ 1) for b in range(2 * Z_PARTS)])]
    ppermute x16 -> x17, waiting for transfers between devices: 28.1 us -> 30 us  [swap_x(): return lax.ppermute(values, 'head', [(h, h ^ 2) for h in range(4)])]
    unnamed x227 -> x222, local copies, waits for them, and re-layouts: 42.2 us -> 40.3 us
    ppermute x60 -> x61, waiting for transfers between devices: 319 us -> 319 us  [shift_z(): lax.ppermute(values, 'blk', [(b, (b + 2 * amount) % total) for b in range...]
    ppermute x60 -> x61, starting transfers between devices: 92.9 us -> 93.3 us  [shift_z(): lax.ppermute(values, 'blk', [(b, (b + 2 * amount) % total) for b in range...]
  transfers between devices with their start and end apart: 111 -> 115, of which waited for: 52 -> 57; matrix products, arithmetic and copies ran while one was open for 16% -> 19% of each run, Pallas kernels for 5% -> 5%
where the time goes in v2:
time: 786 us; the launch traced here: 774 us
  waiting for transfers between devices  403 us (51%)
  starting transfers between devices  142 us (18%)
  local copies, waits for them, and re-layouts  72.9 us (9%)
  matrix products  68.6 us (9%)
  other arithmetic  45.2 us (6%)
  Pallas kernels  38.9 us (5%)
    ppermute x61, waiting for transfers between devices, shift_z(): lax.ppermute(values, 'blk', [(b, (b + 2 * amount) % total) for b in range...  319 us
    ppermute x61, starting transfers between devices, shift_z(): lax.ppermute(values, 'blk', [(b, (b + 2 * amount) % total) for b in range...  93.3 us
    dot_general x42, matrix products, mm(): lax.dot_general(left, right, (((left_dim,), (right_dim,)), ((), ())), pre...  68.6 us
    ppermute x27, waiting for transfers between devices, swap_y(): return lax.ppermute(values, 'blk', [(b, b ^ 1) for b in range(2 * Z_PARTS)])  49.3 us
    unnamed x222, local copies, waits for them, and re-layouts  40.3 us
    ppermute x17, waiting for transfers between devices, swap_x(): return lax.ppermute(values, 'head', [(h, h ^ 2) for h in range(4)])  30 us
    ppermute x27, starting transfers between devices, swap_y(): return lax.ppermute(values, 'blk', [(b, b ^ 1) for b in range(2 * Z_PARTS)])  28.6 us
    pallas_call x1, Pallas kernels, attend_heads_back(): pl.pallas_call(attend_back_kernel, grid_spec=pltpu.PrefetchScalarGridSpec...  22.4 us
  transfers between devices with their start and end apart: 115, of which 57 were waited for; matrix products, arithmetic and copies ran while one was open for 19% of the time, Pallas kernels for 5%

profile of v2, /device:TPU:0, one launch (start us, length us, event | category | flops | bytes accessed | tf_op | source)
XLA Modules:
  0.0 774.2 jit_solution(12323654339721484030)
XLA Ops:
  32.2 4.1 collective-permute-start.2
  54.1 9.1 %collective-permute-done.1 = bf16[256,768]{1,0:T(8,128)(2,1)S(1)} collective-permute-done((bf16[256,768]{1,0:T(8,128)(2,1)}, bf16[256,768]{1,0:T(8,128)(2,1)S(1)}, u32[]{:S(2)}, u32[]{:S(2)}) %collective-permute-start.1) | collective-permute-done | bytes 393248 | tf_op jit(solution)/shard_map/ppermute | solution.py:394
  63.2 6.6 collective-permute-done.3
  76.4 17.7 %collective-permute-done.19 = bf16[256,256]{1,0:T(8,128)(2,1)S(1)} collective-permute-done((bf16[256,256]{1,0:T(8,128)(2,1)S(1)}, bf16[256,256]{1,0:T(8,128)(2,1)S(1)}, u32[]{:S(2)}, u32[]{:S(2)}) %collective-permute-start.19) | collective-permute-done | bytes 131104 | tf_op jit(solution)/shard_map/ppermute | solution.py:394
  102.2 9.6 %collective-permute-done.6 = bf16[256,768]{1,0:T(8,128)(2,1)S(1)} collective-permute-done((bf16[256,768]{1,0:T(8,128)(2,1)S(1)}, bf16[256,768]{1,0:T(8,128)(2,1)S(1)}, u32[]{:S(2)}, u32[]{:S(2)}) %collective-permute-start.6) | collective-permute-done | bytes 393248 | tf_op jit(solution)/shard_map/ppermute | solution.py:394
  126.8 8.3 %collective-permute-done.12 = bf16[192,1024]{1,0:T(8,128)(2,1)S(1)} collective-permute-done((bf16[192,1024]{1,0:T(8,128)(2,1)S(1)}, bf16[192,1024]{1,0:T(8,128)(2,1)S(1)}, u32[]{:S(2)}, u32[]{:S(2)}) %collective-permute-start.12) | collective-permute-done | bytes 393248 | tf_op jit(solution)/shard_map/ppermute | solution.py:394
  135.5 13.8 %collective-permute-done.13 = bf16[192,1024]{1,0:T(8,128)(2,1)S(1)} collective-permute-done((bf16[192,1024]{1,0:T(8,128)(2,1)S(1)}, bf16[192,1024]{1,0:T(8,128)(2,1)S(1)}, u32[]{:S(2)}, u32[]{:S(2)}) %collective-permute-start.13) | collective-permute-done | bytes 393248 | tf_op jit(solution)/shard_map/ppermute | solution.py:394
  149.8 9.1 %collective-permute-start.24 = (bf16[256,256]{1,0:T(8,128)(2,1)S(1)}, bf16[256,256]{1,0:T(8,128)(2,1)S(1)}, u32[]{:S(2)}, u32[]{:S(2)}) collective-permute-start(bf16[256,256]{1,0:T(8,128)(2,1)S(1)} %collective-permute-done.23), channel_id=1, source_target_pairs={{0,2},{1,3},{2,4},{3,5},{4,6},{5,7},{6,0},{7,1},{8,10},{9,11},{10,... | collective-permute-start | bytes 393224 | tf_op jit(solution)/shard_map/ppermute | solution.py:394
  159.2 16.5 %attend.1 = (bf16[4,64,1024]{2,1,0:T(8,128)(2,1)S(1)}, f32[64,4096]{1,0:T(8,128)S(1)}, f32[1,4096]{1,0:T(1,128)S(1)}, bf16[192,4096]{1,0:T(8,128)(2,1)S(1)}) custom-call(s32[32]{0:T(128)S(1)} %select_reduce_fusion.2.slot_ref, s32[8]{0:T(128)S(1)} %and_select_fusion.low_ref, bf16[4,192,1024]{2,1,0:T(8,128)(2,1)S(1)} %pad_maximum_fusion.1.qkv_ref, ...), custom_call_target="tpu_custom_call" | custom-call | flops 1073741824 | bytes 6291456 | tf_op jit(solution)/shard_map/attend/pallas_call | solution.py:668
  175.9 4.9 collective-permute-done.15
  180.8 6.7 collective-permute-done.16
  187.5 6.7 collective-permute-done.17
  206.6 4.8 collective-permute-done.35
  233.0 4.3 collective-permute-done.58
  239.1 37.4 %collective-permute-done.46 = bf16[704,256]{1,0:T(8,128)(2,1)S(1)} collective-permute-done((bf16[704,256]{1,0:T(8,128)(2,1)S(1)}, bf16[704,256]{1,0:T(8,128)(2,1)S(1)}, u32[]{:S(2)}, u32[]{:S(2)}) %collective-permute-start.46) | collective-permute-done | bytes 360480 | tf_op jit(solution)/shard_map/ppermute | solution.py:394
  283.2 6.4 collective-permute-done.47
  295.8 28.1 %collective-permute-done.41 = bf16[512,704]{0,1:T(8,128)(2,1)S(1)} collective-permute-done((bf16[512,704]{0,1:T(8,128)(2,1)S(1)}, bf16[512,704]{0,1:T(8,128)(2,1)S(1)}, u32[]{:S(2)}, u32[]{:S(2)}) %collective-permute-start.41) | collective-permute-done | bytes 720928 | tf_op jit(solution)/shard_map/ppermute | solution.py:394
  328.3 8.8 %collective-permute-done.49 = bf16[704,256]{1,0:T(8,128)(2,1)S(1)} collective-permute-done((bf16[704,256]{1,0:T(8,128)(2,1)S(1)}, bf16[704,256]{1,0:T(8,128)(2,1)S(1)}, u32[]{:S(2)}, u32[]{:S(2)}) %collective-permute-start.49) | collective-permute-done | bytes 360480 | tf_op jit(solution)/shard_map/ppermute | solution.py:394
  337.3 13.9 %collective-permute-done.42 = bf16[512,704]{0,1:T(8,128)(2,1)S(1)} collective-permute-done((bf16[512,704]{0,1:T(8,128)(2,1)S(1)}, bf16[512,704]{0,1:T(8,128)(2,1)S(1)}, u32[]{:S(2)}, u32[]{:S(2)}) %collective-permute-start.42) | collective-permute-done | bytes 720928 | tf_op jit(solution)/shard_map/ppermute | solution.py:394
  351.5 14.9 %collective-permute-done.38 = bf16[512,704]{0,1:T(8,128)(2,1)S(1)} collective-permute-done((bf16[512,704]{0,1:T(8,128)(2,1)S(1)}, bf16[512,704]{0,1:T(8,128)(2,1)S(1)}, u32[]{:S(2)}, u32[]{:S(2)}) %collective-permute-start.38) | collective-permute-done | bytes 720928 | tf_op jit(solution)/shard_map/ppermute | solution.py:394
  373.2 4.4 multiply_convert_fusion.1
  386.4 5.8 fusion.163
  398.6 4.9 collective-permute-done.108
  407.7 18.3 %collective-permute-done.112 = bf16[704,256]{1,0:T(8,128)(2,1)S(1)} collective-permute-done((bf16[704,256]{1,0:T(8,128)(2,1)S(1)}, bf16[704,256]{1,0:T(8,128)(2,1)S(1)}, u32[]{:S(2)}, u32[]{:S(2)}) %collective-permute-start.112) | collective-permute-done | bytes 360480 | tf_op jit(solution)/shard_map/ppermute | solution.py:394
  430.6 4.0 collective-permute-done.109
  436.5 5.9 convolution_add_fusion
  442.8 20.4 %collective-permute-done.110 = bf16[704,256]{1,0:T(8,128)(2,1)S(1)} collective-permute-done((bf16[704,256]{1,0:T(8,128)(2,1)S(1)}, bf16[704,256]{1,0:T(8,128)(2,1)S(1)}, u32[]{:S(2)}, u32[]{:S(2)}) %collective-permute-start.110) | collective-permute-done | bytes 360480 | tf_op jit(solution)/shard_map/ppermute | solution.py:394
  473.0 4.3 collective-permute-done.114
  494.0 4.3 collective-permute-done.63
  510.0 7.2 collective-permute-done.62
  524.4 9.1 %collective-permute-done.66 = bf16[128,2048]{1,0:T(8,128)(2,1)S(1)} collective-permute-done((bf16[128,2048]{1,0:T(8,128)(2,1)S(1)}, bf16[128,2048]{1,0:T(8,128)(2,1)S(1)}, u32[]{:S(2)}, u32[]{:S(2)}) %collective-permute-start.66) | collective-permute-done | bytes 524320 | tf_op jit(solution)/shard_map/ppermute | solution.py:381
  546.8 6.4 collective-permute-done.107
  555.0 5.6 collective-permute-done.103
  577.4 4.1 collective-permute-start.71
  588.0 4.1 collective-permute-done.71
  592.2 22.4 %attend_back.1 = (bf16[4,192,1024]{2,1,0:T(8,128)(2,1)S(1)}, f32[192,128]{1,0:T(8,128)S(1)}) custom-call(s32[32]{0:T(128)S(1)} %select_reduce_fusion.2.slot_ref, s32[8]{0:T(128)S(1)} %and_select_fusion.low_ref, bf16[4,64,1024]{2,1,0:T(8,128)(2,1)S(1)} %pad_maximum_fusion.18.grad_ref, bf16[192,4096]{1,0:T(8,128)(2,1)} %copy-done, ...), custom_call_target="tpu_custom_call" | custom-call | flops 3221225472 | bytes 8388608 | tf_op jit(solution)/shard_map/attend_back/pallas_call | solution.py:697
  615.7 8.3 %collective-permute-start.73 = (bf16[192,1024]{1,0:T(8,128)(2,1)}, bf16[192,1024]{1,0:T(8,128)(2,1)S(1)}, u32[]{:S(2)}, u32[]{:S(2)}) collective-permute-start(bf16[192,1024]{1,0:T(8,128)(2,1)} %get-tuple-element.167), channel_id=1, source_target_pairs={{0,6},{1,7},{2,0},{3,1},{4,2},{5,3},{6,4},{7,5},{8,14},{9,15},{10,... | collective-permute-start | bytes 1179656 | tf_op jit(solution)/shard_map/ppermute | solution.py:394
  630.9 5.6 collective-permute-done.98
  643.2 18.8 %collective-permute-done.74 = bf16[192,1024]{1,0:T(8,128)(2,1)S(1)} collective-permute-done((bf16[192,1024]{1,0:T(8,128)(2,1)}, bf16[192,1024]{1,0:T(8,128)(2,1)S(1)}, u32[]{:S(2)}, u32[]{:S(2)}) %collective-permute-start.74) | collective-permute-done | bytes 393248 | tf_op jit(solution)/shard_map/ppermute | solution.py:394
  680.9 6.4 collective-permute-done.89
  687.9 4.4 collective-permute-start.90
  692.3 6.5 collective-permute-done.86
  700.5 6.3 collective-permute-done.90
  708.9 6.8 collective-permute-done.87
  724.0 7.6 collective-permute-done.88
  738.2 6.1 collective-permute-done.92
  747.5 6.4 collective-permute-done.80
  762.1 4.0 collective-permute-done.83
  (612 shorter events, 320.7 us)
Async XLA Ops:
  4.7 34.2 %collective-permute-start.7 = (bf16[128,2048]{1,0:T(8,128)(2,1)}, bf16[128,2048]{1,0:T(8,128)(2,1)}, u32[]{:S(2)}, u32[]{:S(2)}) collective-permute-start(bf16[128,2048]{1,0:T(8,128)(2,1)} %get-tuple-element.122), channel_id=1, source_target_pairs={{0,1},{1,0},{2,3},{3,2},{4,5},{5,4},{6,7},{7,6},{8,9},{9,8},{10,11... | collective-permute-start | bytes 1572872 | tf_op jit(solution)/shard_map/ppermute | solution.py:389
  7.8 28.5 %collective-permute-start.8 = (bf16[128,2048]{1,0:T(8,128)(2,1)}, bf16[128,2048]{1,0:T(8,128)(2,1)}, u32[]{:S(2)}, u32[]{:S(2)}) collective-permute-start(bf16[128,2048]{1,0:T(8,128)(2,1)} %get-tuple-element.122), channel_id=1, source_target_pairs={{0,16},{8,24},{16,0},{24,8},{1,17},{9,25},{17,1},{25,9},{2,18},{10... | collective-permute-start | bytes 1572872 | tf_op jit(solution)/shard_map/ppermute | solution.py:381
  12.5 40.6 %collective-permute-start.18 = (bf16[256,256]{1,0:T(8,128)(2,1)}, bf16[256,256]{1,0:T(8,128)(2,1)}, u32[]{:S(2)}, u32[]{:S(2)}) collective-permute-start(bf16[256,256]{1,0:T(8,128)(2,1)} %bitcast.28), channel_id=1, source_target_pairs={{0,1},{1,0},{2,3},{3,2},{4,5},{5,4},{6,7},{7,6},{8,9},{9,8},{10,11... | collective-permute-start | bytes 393224 | tf_op jit(solution)/shard_map/ppermute | solution.py:389
  47.6 66.9 %collective-permute-start.11 = (bf16[512,2048]{1,0:T(8,128)(2,1)}, bf16[512,2048]{1,0:T(8,128)(2,1)}, u32[]{:S(2)}, u32[]{:S(2)}) collective-permute-start(bf16[512,2048]{1,0:T(8,128)(2,1)} %get-tuple-element.242), channel_id=1, source_target_pairs={{0,8},{8,0},{16,24},{24,16},{1,9},{9,1},{17,25},{25,17},{2,10},{10... | collective-permute-start | bytes 6291464 | tf_op jit(solution)/shard_map/ppermute | solution.py:385
  63.2 34.8 %collective-permute-start.5 = (bf16[256,768]{1,0:T(8,128)(2,1)S(1)}, bf16[256,768]{1,0:T(8,128)(2,1)S(1)}, u32[]{:S(2)}, u32[]{:S(2)}) collective-permute-start(bf16[256,768]{1,0:T(8,128)(2,1)S(1)} %collective-permute-done.1), channel_id=1, source_target_pairs={{0,2},{1,3},{2,4},{3,5},{4,6},{5,7},{6,0},{7,1},{8,10},{9,11},{10,... | collective-permute-start | bytes 1179656 | tf_op jit(solution)/shard_map/ppermute | solution.py:394
  69.8 29.0 %collective-permute-start.4 = (bf16[256,768]{1,0:T(8,128)(2,1)S(1)}, bf16[256,768]{1,0:T(8,128)(2,1)}, u32[]{:S(2)}, u32[]{:S(2)}) collective-permute-start(bf16[256,768]{1,0:T(8,128)(2,1)S(1)} %collective-permute-done.3), channel_id=1, source_target_pairs={{0,6},{1,7},{2,0},{3,1},{4,2},{5,3},{6,4},{7,5},{8,14},{9,15},{10,... | collective-permute-start | bytes 1179656 | tf_op jit(solution)/shard_map/ppermute | solution.py:394
  72.7 21.9 %collective-permute-start.21 = (bf16[256,256]{1,0:T(8,128)(2,1)S(1)}, bf16[256,256]{1,0:T(8,128)(2,1)S(1)}, u32[]{:S(2)}, u32[]{:S(2)}) collective-permute-start(bf16[256,256]{1,0:T(8,128)(2,1)S(1)} %collective-permute-done.20), channel_id=1, source_target_pairs={{0,6},{1,7},{2,0},{3,1},{4,2},{5,3},{6,4},{7,5},{8,14},{9,15},{10,... | collective-permute-start | bytes 393224 | tf_op jit(solution)/shard_map/ppermute | solution.py:394
  94.1 31.4 %collective-permute-start.23 = (bf16[256,256]{1,0:T(8,128)(2,1)S(1)}, bf16[256,256]{1,0:T(8,128)(2,1)S(1)}, u32[]{:S(2)}, u32[]{:S(2)}) collective-permute-start(bf16[256,256]{1,0:T(8,128)(2,1)S(1)} %collective-permute-done.19), channel_id=1, source_target_pairs={{0,2},{1,3},{2,4},{3,5},{4,6},{5,7},{6,0},{7,1},{8,10},{9,11},{10,... | collective-permute-start | bytes 393224 | tf_op jit(solution)/shard_map/ppermute | solution.py:394
  94.6 30.4 %collective-permute-start.22 = (bf16[256,256]{1,0:T(8,128)(2,1)S(1)}, bf16[256,256]{1,0:T(8,128)(2,1)S(1)}, u32[]{:S(2)}, u32[]{:S(2)}) collective-permute-start(bf16[256,256]{1,0:T(8,128)(2,1)S(1)} %collective-permute-done.21), channel_id=1, source_target_pairs={{0,6},{1,7},{2,0},{3,1},{4,2},{5,3},{6,4},{7,5},{8,14},{9,15},{10,... | collective-permute-start | bytes 393224 | tf_op jit(solution)/shard_map/ppermute | solution.py:394
  121.2 28.2 %collective-permute-start.13 = (bf16[192,1024]{1,0:T(8,128)(2,1)S(1)}, bf16[192,1024]{1,0:T(8,128)(2,1)S(1)}, u32[]{:S(2)}, u32[]{:S(2)}) collective-permute-start(bf16[192,1024]{1,0:T(8,128)(2,1)S(1)} %get-tuple-element.170), channel_id=1, source_target_pairs={{0,4},{1,5},{2,6},{3,7},{4,0},{5,1},{6,2},{7,3},{8,12},{9,13},{10,... | collective-permute-start | bytes 1179656 | tf_op jit(solution)/shard_map/ppermute | solution.py:394
  121.6 28.2 %collective-permute-start.14 = (bf16[192,1024]{1,0:T(8,128)(2,1)S(1)}, bf16[192,1024]{1,0:T(8,128)(2,1)S(1)}, u32[]{:S(2)}, u32[]{:S(2)}) collective-permute-start(bf16[192,1024]{1,0:T(8,128)(2,1)S(1)} %get-tuple-element.169), channel_id=1, source_target_pairs={{0,6},{1,7},{2,0},{3,1},{4,2},{5,3},{6,4},{7,5},{8,14},{9,15},{10,... | collective-permute-start | bytes 1179656 | tf_op jit(solution)/shard_map/ppermute | solution.py:394
  125.0 95.0 %collective-permute-start.55 = (bf16[128,2048]{1,0:T(8,128)(2,1)}, bf16[128,2048]{1,0:T(8,128)(2,1)}, u32[]{:S(2)}, u32[]{:S(2)}) collective-permute-start(bf16[128,2048]{1,0:T(8,128)(2,1)} %get-tuple-element.201), channel_id=1, source_target_pairs={{0,1},{1,0},{2,3},{3,2},{4,5},{5,4},{6,7},{7,6},{8,9},{9,8},{10,11... | collective-permute-start | bytes 1572872 | tf_op jit(solution)/shard_map/ppermute | solution.py:389
  125.6 88.1 %collective-permute-start.56 = (bf16[128,2048]{1,0:T(8,128)(2,1)}, bf16[128,2048]{1,0:T(8,128)(2,1)}, u32[]{:S(2)}, u32[]{:S(2)}) collective-permute-start(bf16[128,2048]{1,0:T(8,128)(2,1)} %get-tuple-element.201), channel_id=1, source_target_pairs={{0,16},{8,24},{16,0},{24,8},{1,17},{9,25},{17,1},{25,9},{2,18},{10... | collective-permute-start | bytes 1572872 | tf_op jit(solution)/shard_map/ppermute | solution.py:381
  135.0 67.3 %collective-permute-start.39 = (bf16[256,704]{0,1:T(8,128)(2,1)}, bf16[256,704]{0,1:T(8,128)(2,1)}, u32[]{:S(2)}, u32[]{:S(2)}) collective-permute-start(bf16[256,704]{0,1:T(8,128)(2,1)} %broadcast_select_fusion.11), channel_id=1, source_target_pairs={{0,1},{1,0},{2,3},{3,2},{4,5},{5,4},{6,7},{7,6},{8,9},{9,8},{10,11... | collective-permute-start | bytes 1081352 | tf_op jit(solution)/shard_map/ppermute | solution.py:389
  149.3 50.5 %collective-permute-start.43 = (bf16[704,256]{1,0:T(8,128)(2,1)}, bf16[704,256]{1,0:T(8,128)(2,1)}, u32[]{:S(2)}, u32[]{:S(2)}) collective-permute-start(bf16[704,256]{1,0:T(8,128)(2,1)} %broadcast_select_fusion.7), channel_id=1, source_target_pairs={{0,1},{1,0},{2,3},{3,2},{4,5},{5,4},{6,7},{7,6},{8,9},{9,8},{10,11... | collective-permute-start | bytes 1081352 | tf_op jit(solution)/shard_map/ppermute | solution.py:389
  149.8 25.9 %collective-permute-start.24 = (bf16[256,256]{1,0:T(8,128)(2,1)S(1)}, bf16[256,256]{1,0:T(8,128)(2,1)S(1)}, u32[]{:S(2)}, u32[]{:S(2)}) collective-permute-start(bf16[256,256]{1,0:T(8,128)(2,1)S(1)} %collective-permute-done.23), channel_id=1, source_target_pairs={{0,2},{1,3},{2,4},{3,5},{4,6},{5,7},{6,0},{7,1},{8,10},{9,11},{10,... | collective-permute-start | bytes 393224 | tf_op jit(solution)/shard_map/ppermute | solution.py:394
  202.3 28.1 %collective-permute-start.44 = (bf16[704,256]{1,0:T(8,128)(2,1)S(1)}, bf16[704,256]{1,0:T(8,128)(2,1)S(1)}, u32[]{:S(2)}, u32[]{:S(2)}) collective-permute-start(bf16[704,256]{1,0:T(8,128)(2,1)S(1)} %get-tuple-element.106), channel_id=1, source_target_pairs={{0,2},{1,3},{2,4},{3,5},{4,6},{5,7},{6,0},{7,1},{8,10},{9,11},{10,... | collective-permute-start | bytes 1081352 | tf_op jit(solution)/shard_map/ppermute | solution.py:394
  229.4 49.4 %collective-permute-start.27 = (bf16[128,2048]{1,0:T(8,128)(2,1)S(1)}, bf16[128,2048]{1,0:T(8,128)(2,1)S(1)}, u32[]{:S(2)}, u32[]{:S(2)}) collective-permute-start(bf16[128,2048]{1,0:T(8,128)(2,1)S(1)} %pad_maximum_fusion.10), channel_id=1, source_target_pairs={{0,16},{8,24},{16,0},{24,8},{1,17},{9,25},{17,1},{25,9},{2,18},{10... | collective-permute-start | bytes 1572872 | tf_op jit(solution)/shard_map/ppermute | solution.py:381
  230.5 49.8 %collective-permute-start.29 = (bf16[128,2048]{1,0:T(8,128)(2,1)S(1)}, bf16[128,2048]{1,0:T(8,128)(2,1)S(1)}, u32[]{:S(2)}, u32[]{:S(2)}) collective-permute-start(bf16[128,2048]{1,0:T(8,128)(2,1)S(1)} %pad_maximum_fusion.11), channel_id=1, source_target_pairs={{0,1},{1,0},{2,3},{3,2},{4,5},{5,4},{6,7},{7,6},{8,9},{9,8},{10,11... | collective-permute-start | bytes 1572872 | tf_op jit(solution)/shard_map/ppermute | solution.py:389
  232.0 57.6 %collective-permute-start.40 = (bf16[512,704]{0,1:T(8,128)(2,1)S(1)}, bf16[512,704]{0,1:T(8,128)(2,1)S(1)}, u32[]{:S(2)}, u32[]{:S(2)}) collective-permute-start(bf16[512,704]{0,1:T(8,128)(2,1)S(1)} %pad_maximum_fusion.8), channel_id=1, source_target_pairs={{0,6},{1,7},{2,0},{3,1},{4,2},{5,3},{6,4},{7,5},{8,14},{9,15},{10,... | collective-permute-start | bytes 2162696 | tf_op jit(solution)/shard_map/ppermute | solution.py:394
  232.1 44.3 %collective-permute-start.46 = (bf16[704,256]{1,0:T(8,128)(2,1)S(1)}, bf16[704,256]{1,0:T(8,128)(2,1)S(1)}, u32[]{:S(2)}, u32[]{:S(2)}) collective-permute-start(bf16[704,256]{1,0:T(8,128)(2,1)S(1)} %collective-permute-done.45), channel_id=1, source_target_pairs={{0,6},{1,7},{2,0},{3,1},{4,2},{5,3},{6,4},{7,5},{8,14},{9,15},{10,... | collective-permute-start | bytes 1081352 | tf_op jit(solution)/shard_map/ppermute | solution.py:394
  237.3 44.7 %collective-permute-start.36 = (bf16[512,704]{0,1:T(8,128)(2,1)S(1)}, bf16[512,704]{0,1:T(8,128)(2,1)S(1)}, u32[]{:S(2)}, u32[]{:S(2)}) collective-permute-start(bf16[512,704]{0,1:T(8,128)(2,1)S(1)} %pad_maximum_fusion.7), channel_id=1, source_target_pairs={{0,2},{1,3},{2,4},{3,5},{4,6},{5,7},{6,0},{7,1},{8,10},{9,11},{10,... | collective-permute-start | bytes 2162696 | tf_op jit(solution)/shard_map/ppermute | solution.py:394
  289.6 76.9 %collective-permute-start.59 = (bf16[512,2048]{1,0:T(8,128)(2,1)S(1)}, bf16[512,2048]{1,0:T(8,128)(2,1)S(1)}, u32[]{:S(2)}, u32[]{:S(2)}) collective-permute-start(bf16[512,2048]{1,0:T(8,128)(2,1)S(1)} %get-tuple-element.230), channel_id=1, source_target_pairs={{0,8},{8,0},{16,24},{24,16},{1,9},{9,1},{17,25},{25,17},{2,10},{10... | collective-permute-start | bytes 6291464 | tf_op jit(solution)/shard_map/ppermute | solution.py:385
  289.7 38.4 %collective-permute-start.37 = (bf16[512,704]{0,1:T(8,128)(2,1)S(1)}, bf16[512,704]{0,1:T(8,128)(2,1)S(1)}, u32[]{:S(2)}, u32[]{:S(2)}) collective-permute-start(bf16[512,704]{0,1:T(8,128)(2,1)S(1)} %collective-permute-done.36), channel_id=1, source_target_pairs={{0,2},{1,3},{2,4},{3,5},{4,6},{5,7},{6,0},{7,1},{8,10},{9,11},{10,... | collective-permute-start | bytes 2162696 | tf_op jit(solution)/shard_map/ppermute | solution.py:394
  290.2 33.7 %collective-permute-start.41 = (bf16[512,704]{0,1:T(8,128)(2,1)S(1)}, bf16[512,704]{0,1:T(8,128)(2,1)S(1)}, u32[]{:S(2)}, u32[]{:S(2)}) collective-permute-start(bf16[512,704]{0,1:T(8,128)(2,1)S(1)} %collective-permute-done.40), channel_id=1, source_target_pairs={{0,6},{1,7},{2,0},{3,1},{4,2},{5,3},{6,4},{7,5},{8,14},{9,15},{10,... | collective-permute-start | bytes 2162696 | tf_op jit(solution)/shard_map/ppermute | solution.py:394
  293.7 31.5 %collective-permute-start.32 = (bf16[64,2048]{1,0:T(8,128)(2,1)S(1)}, bf16[64,2048]{1,0:T(8,128)(2,1)S(1)}, u32[]{:S(2)}, u32[]{:S(2)}) collective-permute-start(bf16[64,2048]{1,0:T(8,128)(2,1)S(1)} %slice.503), channel_id=1, source_target_pairs={{0,1},{1,0},{2,3},{3,2},{4,5},{5,4},{6,7},{7,6},{8,9},{9,8},{10,11... | collective-permute-start | bytes 786440 | tf_op jit(solution)/shard_map/ppermute | solution.py:389
  294.4 33.4 %collective-permute-start.33 = (bf16[64,2048]{1,0:T(8,128)(2,1)S(1)}, bf16[64,2048]{1,0:T(8,128)(2,1)S(1)}, u32[]{:S(2)}, u32[]{:S(2)}) collective-permute-start(bf16[64,2048]{1,0:T(8,128)(2,1)S(1)} %slice.504), channel_id=1, source_target_pairs={{0,16},{8,24},{16,0},{24,8},{1,17},{9,25},{17,1},{25,9},{2,18},{10... | collective-permute-start | bytes 786440 | tf_op jit(solution)/shard_map/ppermute | solution.py:381
  325.1 26.1 %collective-permute-start.42 = (bf16[512,704]{0,1:T(8,128)(2,1)S(1)}, bf16[512,704]{0,1:T(8,128)(2,1)S(1)}, u32[]{:S(2)}, u32[]{:S(2)}) collective-permute-start(bf16[512,704]{0,1:T(8,128)(2,1)S(1)} %collective-permute-done.41), channel_id=1, source_target_pairs={{0,6},{1,7},{2,0},{3,1},{4,2},{5,3},{6,4},{7,5},{8,14},{9,15},{10,... | collective-permute-start | bytes 2162696 | tf_op jit(solution)/shard_map/ppermute | solution.py:394
  327.9 41.9 %collective-permute-start.34 = (bf16[512,2048]{1,0:T(8,128)(2,1)S(1)}, bf16[512,2048]{1,0:T(8,128)(2,1)S(1)}, u32[]{:S(2)}, u32[]{:S(2)}) collective-permute-start(bf16[512,2048]{1,0:T(8,128)(2,1)S(1)} %get-tuple-element.234), channel_id=1, source_target_pairs={{0,8},{8,0},{16,24},{24,16},{1,9},{9,1},{17,25},{25,17},{2,10},{10... | collective-permute-start | bytes 6291464 | tf_op jit(solution)/shard_map/ppermute | solution.py:385
  328.0 38.3 %collective-permute-start.38 = (bf16[512,704]{0,1:T(8,128)(2,1)S(1)}, bf16[512,704]{0,1:T(8,128)(2,1)S(1)}, u32[]{:S(2)}, u32[]{:S(2)}) collective-permute-start(bf16[512,704]{0,1:T(8,128)(2,1)S(1)} %collective-permute-done.37), channel_id=1, source_target_pairs={{0,2},{1,3},{2,4},{3,5},{4,6},{5,7},{6,0},{7,1},{8,10},{9,11},{10,... | collective-permute-start | bytes 2162696 | tf_op jit(solution)/shard_map/ppermute | solution.py:394
  394.5 72.6 %collective-permute-start.104 = (bf16[512,704]{0,1:T(8,128)(2,1)S(1)}, bf16[512,704]{0,1:T(8,128)(2,1)S(1)}, u32[]{:S(2)}, u32[]{:S(2)}) collective-permute-start(bf16[512,704]{0,1:T(8,128)(2,1)S(1)} %convolution_convert_fusion), channel_id=1, source_target_pairs={{0,6},{1,7},{2,0},{3,1},{4,2},{5,3},{6,4},{7,5},{8,14},{9,15},{10,... | collective-permute-start | bytes 2162696 | tf_op jit(solution)/shard_map/ppermute | solution.py:394
  397.5 28.5 %collective-permute-start.112 = (bf16[704,256]{1,0:T(8,128)(2,1)S(1)}, bf16[704,256]{1,0:T(8,128)(2,1)S(1)}, u32[]{:S(2)}, u32[]{:S(2)}) collective-permute-start(bf16[704,256]{1,0:T(8,128)(2,1)S(1)} %add_convert_fusion.10), channel_id=1, source_target_pairs={{0,6},{1,7},{2,0},{3,1},{4,2},{5,3},{6,4},{7,5},{8,14},{9,15},{10,... | collective-permute-start | bytes 1081352 | tf_op jit(solution)/shard_map/ppermute | solution.py:394
  404.1 30.5 %collective-permute-start.109 = (bf16[704,256]{1,0:T(8,128)(2,1)S(1)}, bf16[704,256]{1,0:T(8,128)(2,1)S(1)}, u32[]{:S(2)}, u32[]{:S(2)}) collective-permute-start(bf16[704,256]{1,0:T(8,128)(2,1)S(1)} %add_convert_fusion.12), channel_id=1, source_target_pairs={{0,2},{1,3},{2,4},{3,5},{4,6},{5,7},{6,0},{7,1},{8,10},{9,11},{10,... | collective-permute-start | bytes 1081352 | tf_op jit(solution)/shard_map/ppermute | solution.py:394
  406.3 64.8 %collective-permute-start.100 = (bf16[512,704]{0,1:T(8,128)(2,1)}, bf16[512,704]{0,1:T(8,128)(2,1)S(1)}, u32[]{:S(2)}, u32[]{:S(2)}) collective-permute-start(bf16[512,704]{0,1:T(8,128)(2,1)} %convolution_convert_fusion.1), channel_id=1, source_target_pairs={{0,2},{1,3},{2,4},{3,5},{4,6},{5,7},{6,0},{7,1},{8,10},{9,11},{10,... | collective-permute-start | bytes 2162696 | tf_op jit(solution)/shard_map/ppermute | solution.py:394
  407.6 71.0 %collective-permute-start.50 = (bf16[512,2048]{1,0:T(8,128)(2,1)S(1)}, bf16[512,2048]{1,0:T(8,128)(2,1)S(1)}, u32[]{:S(2)}, u32[]{:S(2)}) collective-permute-start(bf16[512,2048]{1,0:T(8,128)(2,1)S(1)} %slice.784), channel_id=1, source_target_pairs={{0,8},{8,0},{16,24},{24,16},{1,9},{9,1},{17,25},{25,17},{2,10},{10... | collective-permute-start | bytes 6291464 | tf_op jit(solution)/shard_map/ppermute | solution.py:385
  427.6 37.2 %collective-permute-start.113 = (bf16[704,256]{1,0:T(8,128)(2,1)S(1)}, bf16[704,256]{1,0:T(8,128)(2,1)S(1)}, u32[]{:S(2)}, u32[]{:S(2)}) collective-permute-start(bf16[704,256]{1,0:T(8,128)(2,1)S(1)} %add_convert_fusion.9), channel_id=1, source_target_pairs={{0,6},{1,7},{2,0},{3,1},{4,2},{5,3},{6,4},{7,5},{8,14},{9,15},{10,... | collective-permute-start | bytes 1081352 | tf_op jit(solution)/shard_map/ppermute | solution.py:394
  436.1 27.0 %collective-permute-start.110 = (bf16[704,256]{1,0:T(8,128)(2,1)S(1)}, bf16[704,256]{1,0:T(8,128)(2,1)S(1)}, u32[]{:S(2)}, u32[]{:S(2)}) collective-permute-start(bf16[704,256]{1,0:T(8,128)(2,1)S(1)} %add_convert_fusion.11), channel_id=1, source_target_pairs={{0,2},{1,3},{2,4},{3,5},{4,6},{5,7},{6,0},{7,1},{8,10},{9,11},{10,... | collective-permute-start | bytes 1081352 | tf_op jit(solution)/shard_map/ppermute | solution.py:394
  468.9 30.7 %collective-permute-start.105 = (bf16[512,704]{0,1:T(8,128)(2,1)}, bf16[512,704]{0,1:T(8,128)(2,1)S(1)}, u32[]{:S(2)}, u32[]{:S(2)}) collective-permute-start(bf16[512,704]{0,1:T(8,128)(2,1)} %add_convert_fusion.1), channel_id=1, source_target_pairs={{0,6},{1,7},{2,0},{3,1},{4,2},{5,3},{6,4},{7,5},{8,14},{9,15},{10,... | collective-permute-start | bytes 2162696 | tf_op jit(solution)/shard_map/ppermute | solution.py:394
  473.0 30.7 %collective-permute-start.101 = (bf16[512,704]{0,1:T(8,128)(2,1)}, bf16[512,704]{0,1:T(8,128)(2,1)S(1)}, u32[]{:S(2)}, u32[]{:S(2)}) collective-permute-start(bf16[512,704]{0,1:T(8,128)(2,1)} %add_convert_fusion.3), channel_id=1, source_target_pairs={{0,2},{1,3},{2,4},{3,5},{4,6},{5,7},{6,0},{7,1},{8,10},{9,11},{10,... | collective-permute-start | bytes 2162696 | tf_op jit(solution)/shard_map/ppermute | solution.py:394
  509.5 33.5 %collective-permute-start.102 = (bf16[512,704]{0,1:T(8,128)(2,1)S(1)}, bf16[512,704]{0,1:T(8,128)(2,1)S(1)}, u32[]{:S(2)}, u32[]{:S(2)}) collective-permute-start(bf16[512,704]{0,1:T(8,128)(2,1)S(1)} %add_convert_fusion.2), channel_id=1, source_target_pairs={{0,2},{1,3},{2,4},{3,5},{4,6},{5,7},{6,0},{7,1},{8,10},{9,11},{10,... | collective-permute-start | bytes 2162696 | tf_op jit(solution)/shard_map/ppermute | solution.py:394
  541.8 24.0 %collective-permute-start.69 = (bf16[512,2048]{1,0:T(8,128)(2,1)}, bf16[512,2048]{1,0:T(8,128)(2,1)}, u32[]{:S(2)}, u32[]{:S(2)}) collective-permute-start(bf16[512,2048]{1,0:T(8,128)(2,1)} %get-tuple-element.226), channel_id=1, source_target_pairs={{0,8},{8,0},{16,24},{24,16},{1,9},{9,1},{17,25},{25,17},{2,10},{10... | collective-permute-start | bytes 6291464 | tf_op jit(solution)/shard_map/ppermute | solution.py:385
  581.7 42.3 %collective-permute-start.97 = (bf16[256,256]{1,0:T(8,128)(2,1)S(1)}, bf16[256,256]{1,0:T(8,128)(2,1)S(1)}, u32[]{:S(2)}, u32[]{:S(2)}) collective-permute-start(bf16[256,256]{1,0:T(8,128)(2,1)S(1)} %add_convert_fusion.14), channel_id=1, source_target_pairs={{0,6},{1,7},{2,0},{3,1},{4,2},{5,3},{6,4},{7,5},{8,14},{9,15},{10,... | collective-permute-start | bytes 393224 | tf_op jit(solution)/shard_map/ppermute | solution.py:394
  585.6 38.8 %collective-permute-start.94 = (bf16[256,256]{1,0:T(8,128)(2,1)S(1)}, bf16[256,256]{1,0:T(8,128)(2,1)S(1)}, u32[]{:S(2)}, u32[]{:S(2)}) collective-permute-start(bf16[256,256]{1,0:T(8,128)(2,1)S(1)} %add_convert_fusion.16), channel_id=1, source_target_pairs={{0,2},{1,3},{2,4},{3,5},{4,6},{5,7},{6,0},{7,1},{8,10},{9,11},{10,... | collective-permute-start | bytes 393224 | tf_op jit(solution)/shard_map/ppermute | solution.py:394
  615.7 26.7 %collective-permute-start.73 = (bf16[192,1024]{1,0:T(8,128)(2,1)}, bf16[192,1024]{1,0:T(8,128)(2,1)S(1)}, u32[]{:S(2)}, u32[]{:S(2)}) collective-permute-start(bf16[192,1024]{1,0:T(8,128)(2,1)} %get-tuple-element.167), channel_id=1, source_target_pairs={{0,6},{1,7},{2,0},{3,1},{4,2},{5,3},{6,4},{7,5},{8,14},{9,15},{10,... | collective-permute-start | bytes 1179656 | tf_op jit(solution)/shard_map/ppermute | solution.py:394
  627.7 34.3 %collective-permute-start.74 = (bf16[192,1024]{1,0:T(8,128)(2,1)}, bf16[192,1024]{1,0:T(8,128)(2,1)S(1)}, u32[]{:S(2)}, u32[]{:S(2)}) collective-permute-start(bf16[192,1024]{1,0:T(8,128)(2,1)} %get-tuple-element.166), channel_id=1, source_target_pairs={{0,4},{1,5},{2,6},{3,7},{4,0},{5,1},{6,2},{7,3},{8,12},{9,13},{10,... | collective-permute-start | bytes 1179656 | tf_op jit(solution)/shard_map/ppermute | solution.py:394
  627.8 35.0 %collective-permute-start.75 = (bf16[192,1024]{1,0:T(8,128)(2,1)}, bf16[192,1024]{1,0:T(8,128)(2,1)}, u32[]{:S(2)}, u32[]{:S(2)}) collective-permute-start(bf16[192,1024]{1,0:T(8,128)(2,1)} %get-tuple-element.164), channel_id=1, source_target_pairs={{0,2},{1,3},{2,4},{3,5},{4,6},{5,7},{6,0},{7,1},{8,10},{9,11},{10,... | collective-permute-start | bytes 1179656 | tf_op jit(solution)/shard_map/ppermute | solution.py:394
  641.5 58.0 %collective-permute-start.99 = (bf16[256,256]{1,0:T(8,128)(2,1)S(1)}, bf16[256,256]{1,0:T(8,128)(2,1)S(1)}, u32[]{:S(2)}, u32[]{:S(2)}) collective-permute-start(bf16[256,256]{1,0:T(8,128)(2,1)S(1)} %get-tuple-element.278), channel_id=1, source_target_pairs={{0,1},{1,0},{2,3},{3,2},{4,5},{5,4},{6,7},{7,6},{8,9},{9,8},{10,11... | collective-permute-start | bytes 393224 | tf_op jit(solution)/shard_map/ppermute | solution.py:389
  675.0 41.4 %collective-permute-start.76 = (bf16[512,2048]{1,0:T(8,128)(2,1)S(1)}, bf16[512,2048]{1,0:T(8,128)(2,1)S(1)}, u32[]{:S(2)}, u32[]{:S(2)}) collective-permute-start(bf16[512,2048]{1,0:T(8,128)(2,1)S(1)} %slice.782), channel_id=1, source_target_pairs={{0,8},{8,0},{16,24},{24,16},{1,9},{9,1},{17,25},{25,17},{2,10},{10... | collective-permute-start | bytes 6291464 | tf_op jit(solution)/shard_map/ppermute | solution.py:385
  (150 other events, 2982.0 us)

commit v3 on v2

--- a/solution.py
+++ b/solution.py
@@ -4,6 +4,7 @@
 from jax.experimental import pallas as pl
 from jax.experimental.pallas import tpu as pltpu
 from jax.sharding import PartitionSpec as P
+
 
 HD = 64
 ROT = 16
@@ -405,7 +406,8 @@
     corner_a = swap_y(from_x[:half])
     corner_b = swap_x(from_y[half:])
     mine = jnp.concatenate([own, from_y, from_x, corner_a, corner_b], axis=0)
-    return jnp.concatenate([mine, swap_core(mine)], axis=0)
+    other = swap_core(mine)
+    return jnp.concatenate([mine, other], axis=0)
 
 
 def scatter_rows(partial):
@@ -443,7 +445,7 @@
 
 def ring_gather(chunk, amount):
     held = [chunk]
-    for unused in range(Z_PARTS - 1):
+    for _ in range(1, Z_PARTS):
         held.append(shift_z(held[-1], amount))
     if amount == 1:
         return held
@@ -455,8 +457,9 @@
     if amount == -1:
         order = [(Z_PARTS - j) % Z_PARTS for j in order]
     total = partials[order[0]]
-    for j in order[1:]:
-        total = shift_z(total.astype(jnp.bfloat16), amount).astype(jnp.float32) + partials[j]
+    for hop in range(1, Z_PARTS):
+        moved = shift_z(total.astype(jnp.bfloat16), amount)
+        total = moved.astype(jnp.float32) + partials[order[hop]]
     return total
 
 
@@ -662,7 +665,7 @@
 
 
 def attend_heads(slot_of, low_tile, qkv_parts, start_row):
-    parts, features, part_rows = qkv_parts.shape
+    parts, _, part_rows = qkv_parts.shape
     total = parts * part_rows
     vmem = pl.BlockSpec(memory_space=pltpu.VMEM)
     return pl.pallas_call(
@@ -691,7 +694,7 @@
 def attend_heads_back(
     slot_of, low_tile, grad_parts, packed, exact, log_norm, start_row, cosine, sine_table
 ):
-    parts, features, part_rows = grad_parts.shape
+    parts, _, part_rows = grad_parts.shape
     total = parts * part_rows
     vmem = pl.BlockSpec(memory_space=pltpu.VMEM)
     return pl.pallas_call(
@@ -735,6 +738,10 @@
     return jnp.cos(angles), jnp.sin(angles)
 
 
+def on_device_layer(*arrays):
+    return on_device_heads(*arrays)
+
+
 def on_device_heads(
     tokens,
     norm1_gain,
@@ -987,7 +994,7 @@
     )
     heads_plan = mesh.shape["head"] == 4 and mesh.shape["blk"] == 2 * Z_PARTS
     return jax.shard_map(
-        on_device_heads if heads_plan else on_device,
+        on_device_layer if heads_plan else on_device,
         mesh=mesh,
         in_specs=placed,
         out_specs=(

time: 786 us -> 784 us (level)
  no operation moved by 1% of the time
where the time goes in v3:
time: 784 us; the launch traced here: 774 us
  waiting for transfers between devices  403 us (51%)
  starting transfers between devices  143 us (18%)
  local copies, waits for them, and re-layouts  72.9 us (9%)
  matrix products  68.4 us (9%)
  other arithmetic  45.1 us (6%)
  Pallas kernels  38.9 us (5%)
    ppermute x61, waiting for transfers between devices, shift_z(): lax.ppermute(values, 'blk', [(b, (b + 2 * amount) % total) for b in range...  320 us
    ppermute x61, starting transfers between devices, shift_z(): lax.ppermute(values, 'blk', [(b, (b + 2 * amount) % total) for b in range...  93.7 us
    dot_general x42, matrix products, mm(): lax.dot_general(left, right, (((left_dim,), (right_dim,)), ((), ())), pre...  68.4 us
    ppermute x27, waiting for transfers between devices, swap_y(): return lax.ppermute(values, 'blk', [(b, b ^ 1) for b in range(2 * Z_PARTS)])  49.1 us
    unnamed x222, local copies, waits for them, and re-layouts  40.3 us
    ppermute x17, waiting for transfers between devices, swap_x(): return lax.ppermute(values, 'head', [(h, h ^ 2) for h in range(4)])  29.6 us
    ppermute x27, starting transfers between devices, swap_y(): return lax.ppermute(values, 'blk', [(b, b ^ 1) for b in range(2 * Z_PARTS)])  28.8 us
    pallas_call x1, Pallas kernels, attend_heads_back(): pl.pallas_call(attend_back_kernel, grid_spec=pltpu.PrefetchScalarGridSpec...  22.4 us
  transfers between devices with their start and end apart: 115, of which 57 were waited for; matrix products, arithmetic and copies ran while one was open for 19% of the time, Pallas kernels for 5%

profile of v3, /device:TPU:0, one launch (start us, length us, event | category | flops | bytes accessed | tf_op | source)
XLA Modules:
  0.0 774.1 jit_solution(12323654339721484030)
XLA Ops:
  32.2 4.1 collective-permute-start.2
  54.1 9.1 %collective-permute-done.1 = bf16[256,768]{1,0:T(8,128)(2,1)S(1)} collective-permute-done((bf16[256,768]{1,0:T(8,128)(2,1)}, bf16[256,768]{1,0:T(8,128)(2,1)S(1)}, u32[]{:S(2)}, u32[]{:S(2)}) %collective-permute-start.1) | collective-permute-done | bytes 393248 | tf_op jit(solution)/shard_map/ppermute | solution.py:395
  63.2 6.6 collective-permute-done.3
  76.4 17.7 %collective-permute-done.19 = bf16[256,256]{1,0:T(8,128)(2,1)S(1)} collective-permute-done((bf16[256,256]{1,0:T(8,128)(2,1)S(1)}, bf16[256,256]{1,0:T(8,128)(2,1)S(1)}, u32[]{:S(2)}, u32[]{:S(2)}) %collective-permute-start.19) | collective-permute-done | bytes 131104 | tf_op jit(solution)/shard_map/ppermute | solution.py:395
  102.2 9.6 %collective-permute-done.6 = bf16[256,768]{1,0:T(8,128)(2,1)S(1)} collective-permute-done((bf16[256,768]{1,0:T(8,128)(2,1)S(1)}, bf16[256,768]{1,0:T(8,128)(2,1)S(1)}, u32[]{:S(2)}, u32[]{:S(2)}) %collective-permute-start.6) | collective-permute-done | bytes 393248 | tf_op jit(solution)/shard_map/ppermute | solution.py:395
  126.8 8.3 %collective-permute-done.12 = bf16[192,1024]{1,0:T(8,128)(2,1)S(1)} collective-permute-done((bf16[192,1024]{1,0:T(8,128)(2,1)S(1)}, bf16[192,1024]{1,0:T(8,128)(2,1)S(1)}, u32[]{:S(2)}, u32[]{:S(2)}) %collective-permute-start.12) | collective-permute-done | bytes 393248 | tf_op jit(solution)/shard_map/ppermute | solution.py:395
  135.5 13.8 %collective-permute-done.13 = bf16[192,1024]{1,0:T(8,128)(2,1)S(1)} collective-permute-done((bf16[192,1024]{1,0:T(8,128)(2,1)S(1)}, bf16[192,1024]{1,0:T(8,128)(2,1)S(1)}, u32[]{:S(2)}, u32[]{:S(2)}) %collective-permute-start.13) | collective-permute-done | bytes 393248 | tf_op jit(solution)/shard_map/ppermute | solution.py:395
  149.8 9.4 %collective-permute-start.24 = (bf16[256,256]{1,0:T(8,128)(2,1)S(1)}, bf16[256,256]{1,0:T(8,128)(2,1)S(1)}, u32[]{:S(2)}, u32[]{:S(2)}) collective-permute-start(bf16[256,256]{1,0:T(8,128)(2,1)S(1)} %collective-permute-done.23), channel_id=1, source_target_pairs={{0,2},{1,3},{2,4},{3,5},{4,6},{5,7},{6,0},{7,1},{8,10},{9,11},{10,... | collective-permute-start | bytes 393224 | tf_op jit(solution)/shard_map/ppermute | solution.py:395
  159.5 16.5 %attend.1 = (bf16[4,64,1024]{2,1,0:T(8,128)(2,1)S(1)}, f32[64,4096]{1,0:T(8,128)S(1)}, f32[1,4096]{1,0:T(1,128)S(1)}, bf16[192,4096]{1,0:T(8,128)(2,1)S(1)}) custom-call(s32[32]{0:T(128)S(1)} %select_reduce_fusion.2.slot_ref, s32[8]{0:T(128)S(1)} %and_select_fusion.low_ref, bf16[4,192,1024]{2,1,0:T(8,128)(2,1)S(1)} %pad_maximum_fusion.1.qkv_ref, ...), custom_call_target="tpu_custom_call" | custom-call | flops 1073741824 | bytes 6291456 | tf_op jit(solution)/shard_map/attend/pallas_call | solution.py:671
  176.2 4.9 collective-permute-done.15
  181.1 6.7 collective-permute-done.16
  187.8 6.7 collective-permute-done.17
  206.9 4.8 collective-permute-done.35
  233.3 4.3 collective-permute-done.58
  239.4 37.4 %collective-permute-done.46 = bf16[704,256]{1,0:T(8,128)(2,1)S(1)} collective-permute-done((bf16[704,256]{1,0:T(8,128)(2,1)S(1)}, bf16[704,256]{1,0:T(8,128)(2,1)S(1)}, u32[]{:S(2)}, u32[]{:S(2)}) %collective-permute-start.46) | collective-permute-done | bytes 360480 | tf_op jit(solution)/shard_map/ppermute | solution.py:395
  283.4 6.5 collective-permute-done.47
  296.1 28.2 %collective-permute-done.41 = bf16[512,704]{0,1:T(8,128)(2,1)S(1)} collective-permute-done((bf16[512,704]{0,1:T(8,128)(2,1)S(1)}, bf16[512,704]{0,1:T(8,128)(2,1)S(1)}, u32[]{:S(2)}, u32[]{:S(2)}) %collective-permute-start.41) | collective-permute-done | bytes 720928 | tf_op jit(solution)/shard_map/ppermute | solution.py:395
  328.6 8.8 %collective-permute-done.49 = bf16[704,256]{1,0:T(8,128)(2,1)S(1)} collective-permute-done((bf16[704,256]{1,0:T(8,128)(2,1)S(1)}, bf16[704,256]{1,0:T(8,128)(2,1)S(1)}, u32[]{:S(2)}, u32[]{:S(2)}) %collective-permute-start.49) | collective-permute-done | bytes 360480 | tf_op jit(solution)/shard_map/ppermute | solution.py:395
  337.6 13.9 %collective-permute-done.42 = bf16[512,704]{0,1:T(8,128)(2,1)S(1)} collective-permute-done((bf16[512,704]{0,1:T(8,128)(2,1)S(1)}, bf16[512,704]{0,1:T(8,128)(2,1)S(1)}, u32[]{:S(2)}, u32[]{:S(2)}) %collective-permute-start.42) | collective-permute-done | bytes 720928 | tf_op jit(solution)/shard_map/ppermute | solution.py:395
  351.8 14.9 %collective-permute-done.38 = bf16[512,704]{0,1:T(8,128)(2,1)S(1)} collective-permute-done((bf16[512,704]{0,1:T(8,128)(2,1)S(1)}, bf16[512,704]{0,1:T(8,128)(2,1)S(1)}, u32[]{:S(2)}, u32[]{:S(2)}) %collective-permute-start.38) | collective-permute-done | bytes 720928 | tf_op jit(solution)/shard_map/ppermute | solution.py:395
  373.5 4.4 multiply_convert_fusion.1
  386.5 5.8 fusion.163
  398.7 4.9 collective-permute-done.108
  407.8 18.3 %collective-permute-done.112 = bf16[704,256]{1,0:T(8,128)(2,1)S(1)} collective-permute-done((bf16[704,256]{1,0:T(8,128)(2,1)S(1)}, bf16[704,256]{1,0:T(8,128)(2,1)S(1)}, u32[]{:S(2)}, u32[]{:S(2)}) %collective-permute-start.112) | collective-permute-done | bytes 360480 | tf_op jit(solution)/shard_map/ppermute | solution.py:395
  430.7 4.0 collective-permute-done.109
  436.6 5.9 convolution_add_fusion
  442.9 20.4 %collective-permute-done.110 = bf16[704,256]{1,0:T(8,128)(2,1)S(1)} collective-permute-done((bf16[704,256]{1,0:T(8,128)(2,1)S(1)}, bf16[704,256]{1,0:T(8,128)(2,1)S(1)}, u32[]{:S(2)}, u32[]{:S(2)}) %collective-permute-start.110) | collective-permute-done | bytes 360480 | tf_op jit(solution)/shard_map/ppermute | solution.py:395
  473.3 4.1 collective-permute-done.114
  494.1 4.3 collective-permute-done.63
  510.1 7.2 collective-permute-done.62
  524.8 8.9 %collective-permute-done.66 = bf16[128,2048]{1,0:T(8,128)(2,1)S(1)} collective-permute-done((bf16[128,2048]{1,0:T(8,128)(2,1)S(1)}, bf16[128,2048]{1,0:T(8,128)(2,1)S(1)}, u32[]{:S(2)}, u32[]{:S(2)}) %collective-permute-start.66) | collective-permute-done | bytes 524320 | tf_op jit(solution)/shard_map/ppermute | solution.py:382
  546.9 6.4 collective-permute-done.107
  555.1 5.6 collective-permute-done.103
  577.4 4.1 collective-permute-start.71
  588.1 4.1 collective-permute-done.71
  592.2 22.4 %attend_back.1 = (bf16[4,192,1024]{2,1,0:T(8,128)(2,1)S(1)}, f32[192,128]{1,0:T(8,128)S(1)}) custom-call(s32[32]{0:T(128)S(1)} %select_reduce_fusion.2.slot_ref, s32[8]{0:T(128)S(1)} %and_select_fusion.low_ref, bf16[4,64,1024]{2,1,0:T(8,128)(2,1)S(1)} %pad_maximum_fusion.18.grad_ref, bf16[192,4096]{1,0:T(8,128)(2,1)} %copy-done, ...), custom_call_target="tpu_custom_call" | custom-call | flops 3221225472 | bytes 8388608 | tf_op jit(solution)/shard_map/attend_back/pallas_call | solution.py:700
  615.8 8.3 %collective-permute-start.73 = (bf16[192,1024]{1,0:T(8,128)(2,1)}, bf16[192,1024]{1,0:T(8,128)(2,1)S(1)}, u32[]{:S(2)}, u32[]{:S(2)}) collective-permute-start(bf16[192,1024]{1,0:T(8,128)(2,1)} %get-tuple-element.167), channel_id=1, source_target_pairs={{0,6},{1,7},{2,0},{3,1},{4,2},{5,3},{6,4},{7,5},{8,14},{9,15},{10,... | collective-permute-start | bytes 1179656 | tf_op jit(solution)/shard_map/ppermute | solution.py:395
  631.0 5.6 collective-permute-done.98
  643.3 18.8 %collective-permute-done.74 = bf16[192,1024]{1,0:T(8,128)(2,1)S(1)} collective-permute-done((bf16[192,1024]{1,0:T(8,128)(2,1)}, bf16[192,1024]{1,0:T(8,128)(2,1)S(1)}, u32[]{:S(2)}, u32[]{:S(2)}) %collective-permute-start.74) | collective-permute-done | bytes 393248 | tf_op jit(solution)/shard_map/ppermute | solution.py:395
  680.9 6.4 collective-permute-done.89
  687.9 4.4 collective-permute-start.90
  692.3 6.5 collective-permute-done.86
  700.6 6.2 collective-permute-done.90
  708.9 6.8 collective-permute-done.87
  724.1 7.6 collective-permute-done.88
  738.3 6.1 collective-permute-done.92
  747.6 6.3 collective-permute-done.80
  762.1 4.0 collective-permute-done.83
  (612 shorter events, 320.9 us)
Async XLA Ops:
  4.7 34.2 %collective-permute-start.7 = (bf16[128,2048]{1,0:T(8,128)(2,1)}, bf16[128,2048]{1,0:T(8,128)(2,1)}, u32[]{:S(2)}, u32[]{:S(2)}) collective-permute-start(bf16[128,2048]{1,0:T(8,128)(2,1)} %get-tuple-element.122), channel_id=1, source_target_pairs={{0,1},{1,0},{2,3},{3,2},{4,5},{5,4},{6,7},{7,6},{8,9},{9,8},{10,11... | collective-permute-start | bytes 1572872 | tf_op jit(solution)/shard_map/ppermute | solution.py:390
  7.8 28.5 %collective-permute-start.8 = (bf16[128,2048]{1,0:T(8,128)(2,1)}, bf16[128,2048]{1,0:T(8,128)(2,1)}, u32[]{:S(2)}, u32[]{:S(2)}) collective-permute-start(bf16[128,2048]{1,0:T(8,128)(2,1)} %get-tuple-element.122), channel_id=1, source_target_pairs={{0,16},{8,24},{16,0},{24,8},{1,17},{9,25},{17,1},{25,9},{2,18},{10... | collective-permute-start | bytes 1572872 | tf_op jit(solution)/shard_map/ppermute | solution.py:382
  12.5 40.6 %collective-permute-start.18 = (bf16[256,256]{1,0:T(8,128)(2,1)}, bf16[256,256]{1,0:T(8,128)(2,1)}, u32[]{:S(2)}, u32[]{:S(2)}) collective-permute-start(bf16[256,256]{1,0:T(8,128)(2,1)} %bitcast.28), channel_id=1, source_target_pairs={{0,1},{1,0},{2,3},{3,2},{4,5},{5,4},{6,7},{7,6},{8,9},{9,8},{10,11... | collective-permute-start | bytes 393224 | tf_op jit(solution)/shard_map/ppermute | solution.py:390
  47.6 66.9 %collective-permute-start.11 = (bf16[512,2048]{1,0:T(8,128)(2,1)}, bf16[512,2048]{1,0:T(8,128)(2,1)}, u32[]{:S(2)}, u32[]{:S(2)}) collective-permute-start(bf16[512,2048]{1,0:T(8,128)(2,1)} %get-tuple-element.242), channel_id=1, source_target_pairs={{0,8},{8,0},{16,24},{24,16},{1,9},{9,1},{17,25},{25,17},{2,10},{10... | collective-permute-start | bytes 6291464 | tf_op jit(solution)/shard_map/ppermute | solution.py:386
  63.2 34.8 %collective-permute-start.5 = (bf16[256,768]{1,0:T(8,128)(2,1)S(1)}, bf16[256,768]{1,0:T(8,128)(2,1)S(1)}, u32[]{:S(2)}, u32[]{:S(2)}) collective-permute-start(bf16[256,768]{1,0:T(8,128)(2,1)S(1)} %collective-permute-done.1), channel_id=1, source_target_pairs={{0,2},{1,3},{2,4},{3,5},{4,6},{5,7},{6,0},{7,1},{8,10},{9,11},{10,... | collective-permute-start | bytes 1179656 | tf_op jit(solution)/shard_map/ppermute | solution.py:395
  69.8 29.0 %collective-permute-start.4 = (bf16[256,768]{1,0:T(8,128)(2,1)S(1)}, bf16[256,768]{1,0:T(8,128)(2,1)}, u32[]{:S(2)}, u32[]{:S(2)}) collective-permute-start(bf16[256,768]{1,0:T(8,128)(2,1)S(1)} %collective-permute-done.3), channel_id=1, source_target_pairs={{0,6},{1,7},{2,0},{3,1},{4,2},{5,3},{6,4},{7,5},{8,14},{9,15},{10,... | collective-permute-start | bytes 1179656 | tf_op jit(solution)/shard_map/ppermute | solution.py:395
  72.7 21.9 %collective-permute-start.21 = (bf16[256,256]{1,0:T(8,128)(2,1)S(1)}, bf16[256,256]{1,0:T(8,128)(2,1)S(1)}, u32[]{:S(2)}, u32[]{:S(2)}) collective-permute-start(bf16[256,256]{1,0:T(8,128)(2,1)S(1)} %collective-permute-done.20), channel_id=1, source_target_pairs={{0,6},{1,7},{2,0},{3,1},{4,2},{5,3},{6,4},{7,5},{8,14},{9,15},{10,... | collective-permute-start | bytes 393224 | tf_op jit(solution)/shard_map/ppermute | solution.py:395
  94.1 31.4 %collective-permute-start.23 = (bf16[256,256]{1,0:T(8,128)(2,1)S(1)}, bf16[256,256]{1,0:T(8,128)(2,1)S(1)}, u32[]{:S(2)}, u32[]{:S(2)}) collective-permute-start(bf16[256,256]{1,0:T(8,128)(2,1)S(1)} %collective-permute-done.19), channel_id=1, source_target_pairs={{0,2},{1,3},{2,4},{3,5},{4,6},{5,7},{6,0},{7,1},{8,10},{9,11},{10,... | collective-permute-start | bytes 393224 | tf_op jit(solution)/shard_map/ppermute | solution.py:395
  94.6 30.4 %collective-permute-start.22 = (bf16[256,256]{1,0:T(8,128)(2,1)S(1)}, bf16[256,256]{1,0:T(8,128)(2,1)S(1)}, u32[]{:S(2)}, u32[]{:S(2)}) collective-permute-start(bf16[256,256]{1,0:T(8,128)(2,1)S(1)} %collective-permute-done.21), channel_id=1, source_target_pairs={{0,6},{1,7},{2,0},{3,1},{4,2},{5,3},{6,4},{7,5},{8,14},{9,15},{10,... | collective-permute-start | bytes 393224 | tf_op jit(solution)/shard_map/ppermute | solution.py:395
  121.2 28.2 %collective-permute-start.13 = (bf16[192,1024]{1,0:T(8,128)(2,1)S(1)}, bf16[192,1024]{1,0:T(8,128)(2,1)S(1)}, u32[]{:S(2)}, u32[]{:S(2)}) collective-permute-start(bf16[192,1024]{1,0:T(8,128)(2,1)S(1)} %get-tuple-element.170), channel_id=1, source_target_pairs={{0,4},{1,5},{2,6},{3,7},{4,0},{5,1},{6,2},{7,3},{8,12},{9,13},{10,... | collective-permute-start | bytes 1179656 | tf_op jit(solution)/shard_map/ppermute | solution.py:395
  121.6 28.2 %collective-permute-start.14 = (bf16[192,1024]{1,0:T(8,128)(2,1)S(1)}, bf16[192,1024]{1,0:T(8,128)(2,1)S(1)}, u32[]{:S(2)}, u32[]{:S(2)}) collective-permute-start(bf16[192,1024]{1,0:T(8,128)(2,1)S(1)} %get-tuple-element.169), channel_id=1, source_target_pairs={{0,6},{1,7},{2,0},{3,1},{4,2},{5,3},{6,4},{7,5},{8,14},{9,15},{10,... | collective-permute-start | bytes 1179656 | tf_op jit(solution)/shard_map/ppermute | solution.py:395
  125.0 95.2 %collective-permute-start.55 = (bf16[128,2048]{1,0:T(8,128)(2,1)}, bf16[128,2048]{1,0:T(8,128)(2,1)}, u32[]{:S(2)}, u32[]{:S(2)}) collective-permute-start(bf16[128,2048]{1,0:T(8,128)(2,1)} %get-tuple-element.201), channel_id=1, source_target_pairs={{0,1},{1,0},{2,3},{3,2},{4,5},{5,4},{6,7},{7,6},{8,9},{9,8},{10,11... | collective-permute-start | bytes 1572872 | tf_op jit(solution)/shard_map/ppermute | solution.py:390
  125.6 88.3 %collective-permute-start.56 = (bf16[128,2048]{1,0:T(8,128)(2,1)}, bf16[128,2048]{1,0:T(8,128)(2,1)}, u32[]{:S(2)}, u32[]{:S(2)}) collective-permute-start(bf16[128,2048]{1,0:T(8,128)(2,1)} %get-tuple-element.201), channel_id=1, source_target_pairs={{0,16},{8,24},{16,0},{24,8},{1,17},{9,25},{17,1},{25,9},{2,18},{10... | collective-permute-start | bytes 1572872 | tf_op jit(solution)/shard_map/ppermute | solution.py:382
  135.0 67.6 %collective-permute-start.39 = (bf16[256,704]{0,1:T(8,128)(2,1)}, bf16[256,704]{0,1:T(8,128)(2,1)}, u32[]{:S(2)}, u32[]{:S(2)}) collective-permute-start(bf16[256,704]{0,1:T(8,128)(2,1)} %broadcast_select_fusion.11), channel_id=1, source_target_pairs={{0,1},{1,0},{2,3},{3,2},{4,5},{5,4},{6,7},{7,6},{8,9},{9,8},{10,11... | collective-permute-start | bytes 1081352 | tf_op jit(solution)/shard_map/ppermute | solution.py:390
  149.3 50.8 %collective-permute-start.43 = (bf16[704,256]{1,0:T(8,128)(2,1)}, bf16[704,256]{1,0:T(8,128)(2,1)}, u32[]{:S(2)}, u32[]{:S(2)}) collective-permute-start(bf16[704,256]{1,0:T(8,128)(2,1)} %broadcast_select_fusion.7), channel_id=1, source_target_pairs={{0,1},{1,0},{2,3},{3,2},{4,5},{5,4},{6,7},{7,6},{8,9},{9,8},{10,11... | collective-permute-start | bytes 1081352 | tf_op jit(solution)/shard_map/ppermute | solution.py:390
  149.8 26.2 %collective-permute-start.24 = (bf16[256,256]{1,0:T(8,128)(2,1)S(1)}, bf16[256,256]{1,0:T(8,128)(2,1)S(1)}, u32[]{:S(2)}, u32[]{:S(2)}) collective-permute-start(bf16[256,256]{1,0:T(8,128)(2,1)S(1)} %collective-permute-done.23), channel_id=1, source_target_pairs={{0,2},{1,3},{2,4},{3,5},{4,6},{5,7},{6,0},{7,1},{8,10},{9,11},{10,... | collective-permute-start | bytes 393224 | tf_op jit(solution)/shard_map/ppermute | solution.py:395
  202.6 28.1 %collective-permute-start.44 = (bf16[704,256]{1,0:T(8,128)(2,1)S(1)}, bf16[704,256]{1,0:T(8,128)(2,1)S(1)}, u32[]{:S(2)}, u32[]{:S(2)}) collective-permute-start(bf16[704,256]{1,0:T(8,128)(2,1)S(1)} %get-tuple-element.106), channel_id=1, source_target_pairs={{0,2},{1,3},{2,4},{3,5},{4,6},{5,7},{6,0},{7,1},{8,10},{9,11},{10,... | collective-permute-start | bytes 1081352 | tf_op jit(solution)/shard_map/ppermute | solution.py:395
  229.7 49.4 %collective-permute-start.27 = (bf16[128,2048]{1,0:T(8,128)(2,1)S(1)}, bf16[128,2048]{1,0:T(8,128)(2,1)S(1)}, u32[]{:S(2)}, u32[]{:S(2)}) collective-permute-start(bf16[128,2048]{1,0:T(8,128)(2,1)S(1)} %pad_maximum_fusion.10), channel_id=1, source_target_pairs={{0,16},{8,24},{16,0},{24,8},{1,17},{9,25},{17,1},{25,9},{2,18},{10... | collective-permute-start | bytes 1572872 | tf_op jit(solution)/shard_map/ppermute | solution.py:382
  230.8 49.8 %collective-permute-start.29 = (bf16[128,2048]{1,0:T(8,128)(2,1)S(1)}, bf16[128,2048]{1,0:T(8,128)(2,1)S(1)}, u32[]{:S(2)}, u32[]{:S(2)}) collective-permute-start(bf16[128,2048]{1,0:T(8,128)(2,1)S(1)} %pad_maximum_fusion.11), channel_id=1, source_target_pairs={{0,1},{1,0},{2,3},{3,2},{4,5},{5,4},{6,7},{7,6},{8,9},{9,8},{10,11... | collective-permute-start | bytes 1572872 | tf_op jit(solution)/shard_map/ppermute | solution.py:390
  232.3 57.6 %collective-permute-start.40 = (bf16[512,704]{0,1:T(8,128)(2,1)S(1)}, bf16[512,704]{0,1:T(8,128)(2,1)S(1)}, u32[]{:S(2)}, u32[]{:S(2)}) collective-permute-start(bf16[512,704]{0,1:T(8,128)(2,1)S(1)} %pad_maximum_fusion.8), channel_id=1, source_target_pairs={{0,6},{1,7},{2,0},{3,1},{4,2},{5,3},{6,4},{7,5},{8,14},{9,15},{10,... | collective-permute-start | bytes 2162696 | tf_op jit(solution)/shard_map/ppermute | solution.py:395
  232.4 44.3 %collective-permute-start.46 = (bf16[704,256]{1,0:T(8,128)(2,1)S(1)}, bf16[704,256]{1,0:T(8,128)(2,1)S(1)}, u32[]{:S(2)}, u32[]{:S(2)}) collective-permute-start(bf16[704,256]{1,0:T(8,128)(2,1)S(1)} %collective-permute-done.45), channel_id=1, source_target_pairs={{0,6},{1,7},{2,0},{3,1},{4,2},{5,3},{6,4},{7,5},{8,14},{9,15},{10,... | collective-permute-start | bytes 1081352 | tf_op jit(solution)/shard_map/ppermute | solution.py:395
  237.6 44.7 %collective-permute-start.36 = (bf16[512,704]{0,1:T(8,128)(2,1)S(1)}, bf16[512,704]{0,1:T(8,128)(2,1)S(1)}, u32[]{:S(2)}, u32[]{:S(2)}) collective-permute-start(bf16[512,704]{0,1:T(8,128)(2,1)S(1)} %pad_maximum_fusion.7), channel_id=1, source_target_pairs={{0,2},{1,3},{2,4},{3,5},{4,6},{5,7},{6,0},{7,1},{8,10},{9,11},{10,... | collective-permute-start | bytes 2162696 | tf_op jit(solution)/shard_map/ppermute | solution.py:395
  289.9 76.9 %collective-permute-start.59 = (bf16[512,2048]{1,0:T(8,128)(2,1)S(1)}, bf16[512,2048]{1,0:T(8,128)(2,1)S(1)}, u32[]{:S(2)}, u32[]{:S(2)}) collective-permute-start(bf16[512,2048]{1,0:T(8,128)(2,1)S(1)} %get-tuple-element.230), channel_id=1, source_target_pairs={{0,8},{8,0},{16,24},{24,16},{1,9},{9,1},{17,25},{25,17},{2,10},{10... | collective-permute-start | bytes 6291464 | tf_op jit(solution)/shard_map/ppermute | solution.py:386
  290.0 38.4 %collective-permute-start.37 = (bf16[512,704]{0,1:T(8,128)(2,1)S(1)}, bf16[512,704]{0,1:T(8,128)(2,1)S(1)}, u32[]{:S(2)}, u32[]{:S(2)}) collective-permute-start(bf16[512,704]{0,1:T(8,128)(2,1)S(1)} %collective-permute-done.36), channel_id=1, source_target_pairs={{0,2},{1,3},{2,4},{3,5},{4,6},{5,7},{6,0},{7,1},{8,10},{9,11},{10,... | collective-permute-start | bytes 2162696 | tf_op jit(solution)/shard_map/ppermute | solution.py:395
  290.5 33.7 %collective-permute-start.41 = (bf16[512,704]{0,1:T(8,128)(2,1)S(1)}, bf16[512,704]{0,1:T(8,128)(2,1)S(1)}, u32[]{:S(2)}, u32[]{:S(2)}) collective-permute-start(bf16[512,704]{0,1:T(8,128)(2,1)S(1)} %collective-permute-done.40), channel_id=1, source_target_pairs={{0,6},{1,7},{2,0},{3,1},{4,2},{5,3},{6,4},{7,5},{8,14},{9,15},{10,... | collective-permute-start | bytes 2162696 | tf_op jit(solution)/shard_map/ppermute | solution.py:395
  294.0 31.5 %collective-permute-start.32 = (bf16[64,2048]{1,0:T(8,128)(2,1)S(1)}, bf16[64,2048]{1,0:T(8,128)(2,1)S(1)}, u32[]{:S(2)}, u32[]{:S(2)}) collective-permute-start(bf16[64,2048]{1,0:T(8,128)(2,1)S(1)} %slice.503), channel_id=1, source_target_pairs={{0,1},{1,0},{2,3},{3,2},{4,5},{5,4},{6,7},{7,6},{8,9},{9,8},{10,11... | collective-permute-start | bytes 786440 | tf_op jit(solution)/shard_map/ppermute | solution.py:390
  294.7 33.4 %collective-permute-start.33 = (bf16[64,2048]{1,0:T(8,128)(2,1)S(1)}, bf16[64,2048]{1,0:T(8,128)(2,1)S(1)}, u32[]{:S(2)}, u32[]{:S(2)}) collective-permute-start(bf16[64,2048]{1,0:T(8,128)(2,1)S(1)} %slice.504), channel_id=1, source_target_pairs={{0,16},{8,24},{16,0},{24,8},{1,17},{9,25},{17,1},{25,9},{2,18},{10... | collective-permute-start | bytes 786440 | tf_op jit(solution)/shard_map/ppermute | solution.py:382
  325.4 26.1 %collective-permute-start.42 = (bf16[512,704]{0,1:T(8,128)(2,1)S(1)}, bf16[512,704]{0,1:T(8,128)(2,1)S(1)}, u32[]{:S(2)}, u32[]{:S(2)}) collective-permute-start(bf16[512,704]{0,1:T(8,128)(2,1)S(1)} %collective-permute-done.41), channel_id=1, source_target_pairs={{0,6},{1,7},{2,0},{3,1},{4,2},{5,3},{6,4},{7,5},{8,14},{9,15},{10,... | collective-permute-start | bytes 2162696 | tf_op jit(solution)/shard_map/ppermute | solution.py:395
  328.2 41.9 %collective-permute-start.34 = (bf16[512,2048]{1,0:T(8,128)(2,1)S(1)}, bf16[512,2048]{1,0:T(8,128)(2,1)S(1)}, u32[]{:S(2)}, u32[]{:S(2)}) collective-permute-start(bf16[512,2048]{1,0:T(8,128)(2,1)S(1)} %get-tuple-element.234), channel_id=1, source_target_pairs={{0,8},{8,0},{16,24},{24,16},{1,9},{9,1},{17,25},{25,17},{2,10},{10... | collective-permute-start | bytes 6291464 | tf_op jit(solution)/shard_map/ppermute | solution.py:386
  328.3 38.3 %collective-permute-start.38 = (bf16[512,704]{0,1:T(8,128)(2,1)S(1)}, bf16[512,704]{0,1:T(8,128)(2,1)S(1)}, u32[]{:S(2)}, u32[]{:S(2)}) collective-permute-start(bf16[512,704]{0,1:T(8,128)(2,1)S(1)} %collective-permute-done.37), channel_id=1, source_target_pairs={{0,2},{1,3},{2,4},{3,5},{4,6},{5,7},{6,0},{7,1},{8,10},{9,11},{10,... | collective-permute-start | bytes 2162696 | tf_op jit(solution)/shard_map/ppermute | solution.py:395
  394.6 72.6 %collective-permute-start.104 = (bf16[512,704]{0,1:T(8,128)(2,1)S(1)}, bf16[512,704]{0,1:T(8,128)(2,1)S(1)}, u32[]{:S(2)}, u32[]{:S(2)}) collective-permute-start(bf16[512,704]{0,1:T(8,128)(2,1)S(1)} %convolution_convert_fusion), channel_id=1, source_target_pairs={{0,6},{1,7},{2,0},{3,1},{4,2},{5,3},{6,4},{7,5},{8,14},{9,15},{10,... | collective-permute-start | bytes 2162696 | tf_op jit(solution)/shard_map/ppermute | solution.py:395
  397.6 28.5 %collective-permute-start.112 = (bf16[704,256]{1,0:T(8,128)(2,1)S(1)}, bf16[704,256]{1,0:T(8,128)(2,1)S(1)}, u32[]{:S(2)}, u32[]{:S(2)}) collective-permute-start(bf16[704,256]{1,0:T(8,128)(2,1)S(1)} %add_convert_fusion.10), channel_id=1, source_target_pairs={{0,6},{1,7},{2,0},{3,1},{4,2},{5,3},{6,4},{7,5},{8,14},{9,15},{10,... | collective-permute-start | bytes 1081352 | tf_op jit(solution)/shard_map/ppermute | solution.py:395
  404.2 30.5 %collective-permute-start.109 = (bf16[704,256]{1,0:T(8,128)(2,1)S(1)}, bf16[704,256]{1,0:T(8,128)(2,1)S(1)}, u32[]{:S(2)}, u32[]{:S(2)}) collective-permute-start(bf16[704,256]{1,0:T(8,128)(2,1)S(1)} %add_convert_fusion.12), channel_id=1, source_target_pairs={{0,2},{1,3},{2,4},{3,5},{4,6},{5,7},{6,0},{7,1},{8,10},{9,11},{10,... | collective-permute-start | bytes 1081352 | tf_op jit(solution)/shard_map/ppermute | solution.py:395
  406.4 65.1 %collective-permute-start.100 = (bf16[512,704]{0,1:T(8,128)(2,1)}, bf16[512,704]{0,1:T(8,128)(2,1)S(1)}, u32[]{:S(2)}, u32[]{:S(2)}) collective-permute-start(bf16[512,704]{0,1:T(8,128)(2,1)} %convolution_convert_fusion.1), channel_id=1, source_target_pairs={{0,2},{1,3},{2,4},{3,5},{4,6},{5,7},{6,0},{7,1},{8,10},{9,11},{10,... | collective-permute-start | bytes 2162696 | tf_op jit(solution)/shard_map/ppermute | solution.py:395
  407.7 71.0 %collective-permute-start.50 = (bf16[512,2048]{1,0:T(8,128)(2,1)S(1)}, bf16[512,2048]{1,0:T(8,128)(2,1)S(1)}, u32[]{:S(2)}, u32[]{:S(2)}) collective-permute-start(bf16[512,2048]{1,0:T(8,128)(2,1)S(1)} %slice.784), channel_id=1, source_target_pairs={{0,8},{8,0},{16,24},{24,16},{1,9},{9,1},{17,25},{25,17},{2,10},{10... | collective-permute-start | bytes 6291464 | tf_op jit(solution)/shard_map/ppermute | solution.py:386
  427.7 37.2 %collective-permute-start.113 = (bf16[704,256]{1,0:T(8,128)(2,1)S(1)}, bf16[704,256]{1,0:T(8,128)(2,1)S(1)}, u32[]{:S(2)}, u32[]{:S(2)}) collective-permute-start(bf16[704,256]{1,0:T(8,128)(2,1)S(1)} %add_convert_fusion.9), channel_id=1, source_target_pairs={{0,6},{1,7},{2,0},{3,1},{4,2},{5,3},{6,4},{7,5},{8,14},{9,15},{10,... | collective-permute-start | bytes 1081352 | tf_op jit(solution)/shard_map/ppermute | solution.py:395
  436.2 27.0 %collective-permute-start.110 = (bf16[704,256]{1,0:T(8,128)(2,1)S(1)}, bf16[704,256]{1,0:T(8,128)(2,1)S(1)}, u32[]{:S(2)}, u32[]{:S(2)}) collective-permute-start(bf16[704,256]{1,0:T(8,128)(2,1)S(1)} %add_convert_fusion.11), channel_id=1, source_target_pairs={{0,2},{1,3},{2,4},{3,5},{4,6},{5,7},{6,0},{7,1},{8,10},{9,11},{10,... | collective-permute-start | bytes 1081352 | tf_op jit(solution)/shard_map/ppermute | solution.py:395
  469.0 30.7 %collective-permute-start.105 = (bf16[512,704]{0,1:T(8,128)(2,1)}, bf16[512,704]{0,1:T(8,128)(2,1)S(1)}, u32[]{:S(2)}, u32[]{:S(2)}) collective-permute-start(bf16[512,704]{0,1:T(8,128)(2,1)} %add_convert_fusion.1), channel_id=1, source_target_pairs={{0,6},{1,7},{2,0},{3,1},{4,2},{5,3},{6,4},{7,5},{8,14},{9,15},{10,... | collective-permute-start | bytes 2162696 | tf_op jit(solution)/shard_map/ppermute | solution.py:395
  473.3 30.7 %collective-permute-start.101 = (bf16[512,704]{0,1:T(8,128)(2,1)}, bf16[512,704]{0,1:T(8,128)(2,1)S(1)}, u32[]{:S(2)}, u32[]{:S(2)}) collective-permute-start(bf16[512,704]{0,1:T(8,128)(2,1)} %add_convert_fusion.3), channel_id=1, source_target_pairs={{0,2},{1,3},{2,4},{3,5},{4,6},{5,7},{6,0},{7,1},{8,10},{9,11},{10,... | collective-permute-start | bytes 2162696 | tf_op jit(solution)/shard_map/ppermute | solution.py:395
  509.6 33.6 %collective-permute-start.102 = (bf16[512,704]{0,1:T(8,128)(2,1)S(1)}, bf16[512,704]{0,1:T(8,128)(2,1)S(1)}, u32[]{:S(2)}, u32[]{:S(2)}) collective-permute-start(bf16[512,704]{0,1:T(8,128)(2,1)S(1)} %add_convert_fusion.2), channel_id=1, source_target_pairs={{0,2},{1,3},{2,4},{3,5},{4,6},{5,7},{6,0},{7,1},{8,10},{9,11},{10,... | collective-permute-start | bytes 2162696 | tf_op jit(solution)/shard_map/ppermute | solution.py:395
  541.9 24.0 %collective-permute-start.69 = (bf16[512,2048]{1,0:T(8,128)(2,1)}, bf16[512,2048]{1,0:T(8,128)(2,1)}, u32[]{:S(2)}, u32[]{:S(2)}) collective-permute-start(bf16[512,2048]{1,0:T(8,128)(2,1)} %get-tuple-element.226), channel_id=1, source_target_pairs={{0,8},{8,0},{16,24},{24,16},{1,9},{9,1},{17,25},{25,17},{2,10},{10... | collective-permute-start | bytes 6291464 | tf_op jit(solution)/shard_map/ppermute | solution.py:386
  581.8 42.3 %collective-permute-start.97 = (bf16[256,256]{1,0:T(8,128)(2,1)S(1)}, bf16[256,256]{1,0:T(8,128)(2,1)S(1)}, u32[]{:S(2)}, u32[]{:S(2)}) collective-permute-start(bf16[256,256]{1,0:T(8,128)(2,1)S(1)} %add_convert_fusion.14), channel_id=1, source_target_pairs={{0,6},{1,7},{2,0},{3,1},{4,2},{5,3},{6,4},{7,5},{8,14},{9,15},{10,... | collective-permute-start | bytes 393224 | tf_op jit(solution)/shard_map/ppermute | solution.py:395
  585.6 38.8 %collective-permute-start.94 = (bf16[256,256]{1,0:T(8,128)(2,1)S(1)}, bf16[256,256]{1,0:T(8,128)(2,1)S(1)}, u32[]{:S(2)}, u32[]{:S(2)}) collective-permute-start(bf16[256,256]{1,0:T(8,128)(2,1)S(1)} %add_convert_fusion.16), channel_id=1, source_target_pairs={{0,2},{1,3},{2,4},{3,5},{4,6},{5,7},{6,0},{7,1},{8,10},{9,11},{10,... | collective-permute-start | bytes 393224 | tf_op jit(solution)/shard_map/ppermute | solution.py:395
  615.8 26.7 %collective-permute-start.73 = (bf16[192,1024]{1,0:T(8,128)(2,1)}, bf16[192,1024]{1,0:T(8,128)(2,1)S(1)}, u32[]{:S(2)}, u32[]{:S(2)}) collective-permute-start(bf16[192,1024]{1,0:T(8,128)(2,1)} %get-tuple-element.167), channel_id=1, source_target_pairs={{0,6},{1,7},{2,0},{3,1},{4,2},{5,3},{6,4},{7,5},{8,14},{9,15},{10,... | collective-permute-start | bytes 1179656 | tf_op jit(solution)/shard_map/ppermute | solution.py:395
  627.7 34.3 %collective-permute-start.74 = (bf16[192,1024]{1,0:T(8,128)(2,1)}, bf16[192,1024]{1,0:T(8,128)(2,1)S(1)}, u32[]{:S(2)}, u32[]{:S(2)}) collective-permute-start(bf16[192,1024]{1,0:T(8,128)(2,1)} %get-tuple-element.166), channel_id=1, source_target_pairs={{0,4},{1,5},{2,6},{3,7},{4,0},{5,1},{6,2},{7,3},{8,12},{9,13},{10,... | collective-permute-start | bytes 1179656 | tf_op jit(solution)/shard_map/ppermute | solution.py:395
  627.8 35.0 %collective-permute-start.75 = (bf16[192,1024]{1,0:T(8,128)(2,1)}, bf16[192,1024]{1,0:T(8,128)(2,1)}, u32[]{:S(2)}, u32[]{:S(2)}) collective-permute-start(bf16[192,1024]{1,0:T(8,128)(2,1)} %get-tuple-element.164), channel_id=1, source_target_pairs={{0,2},{1,3},{2,4},{3,5},{4,6},{5,7},{6,0},{7,1},{8,10},{9,11},{10,... | collective-permute-start | bytes 1179656 | tf_op jit(solution)/shard_map/ppermute | solution.py:395
  641.5 58.0 %collective-permute-start.99 = (bf16[256,256]{1,0:T(8,128)(2,1)S(1)}, bf16[256,256]{1,0:T(8,128)(2,1)S(1)}, u32[]{:S(2)}, u32[]{:S(2)}) collective-permute-start(bf16[256,256]{1,0:T(8,128)(2,1)S(1)} %get-tuple-element.278), channel_id=1, source_target_pairs={{0,1},{1,0},{2,3},{3,2},{4,5},{5,4},{6,7},{7,6},{8,9},{9,8},{10,11... | collective-permute-start | bytes 393224 | tf_op jit(solution)/shard_map/ppermute | solution.py:390
  675.0 41.4 %collective-permute-start.76 = (bf16[512,2048]{1,0:T(8,128)(2,1)S(1)}, bf16[512,2048]{1,0:T(8,128)(2,1)S(1)}, u32[]{:S(2)}, u32[]{:S(2)}) collective-permute-start(bf16[512,2048]{1,0:T(8,128)(2,1)S(1)} %slice.782), channel_id=1, source_target_pairs={{0,8},{8,0},{16,24},{24,16},{1,9},{9,1},{17,25},{25,17},{2,10},{10... | collective-permute-start | bytes 6291464 | tf_op jit(solution)/shard_map/ppermute | solution.py:386
  (150 other events, 2982.0 us)

commit v4 on v3

--- a/solution.py
+++ b/solution.py
@@ -456,10 +456,12 @@
     order = [(j + 1) % Z_PARTS for j in range(Z_PARTS)]
     if amount == -1:
         order = [(Z_PARTS - j) % Z_PARTS for j in order]
-    total = partials[order[0]]
+    total = partials[order[0]]()
+    sent = total.astype(jnp.bfloat16)
     for hop in range(1, Z_PARTS):
-        moved = shift_z(total.astype(jnp.bfloat16), amount)
-        total = moved.astype(jnp.float32) + partials[order[hop]]
+        moved = shift_z(sent, amount)
+        total = moved.astype(jnp.float32) + partials[order[hop]]()
+        sent = total.astype(jnp.bfloat16)
     return total
 
 
@@ -882,8 +884,6 @@
         grad_activ * up_val * sigmoid_gate * (1.0 + gate_val * (1.0 - sigmoid_gate))
     ).astype(jnp.bfloat16)
     grad_norm2 = scatter_rows(mm(grad_gate_b, gate_full, 1, 1) + mm(grad_up_b, up_full, 1, 1))
-    mlp_own = scatter_rows(mm(activ_b, down_full))
-    output = split_order((hidden + mlp_own).astype(jnp.bfloat16), z_index, 1)
 
     def pieces_of(values, width, offset=0, size=None):
         size = width if size is None else size
@@ -892,15 +892,19 @@
         ]
 
     down_sum_even = ring_scatter(
-        [mm(activ_b, p, 0, 0) for p in pieces_of(grad_all, chunk, 0, row_block)], 1
+        [lambda p=p: mm(activ_b, p, 0, 0) for p in pieces_of(grad_all, chunk, 0, row_block)], 1
     )
     down_sum_odd = ring_scatter(
-        [mm(activ_b, p, 0, 0) for p in pieces_of(grad_all, chunk, row_block, row_block)], -1
+        [lambda p=p: mm(activ_b, p, 0, 0) for p in pieces_of(grad_all, chunk, row_block, row_block)], -1
     )
     down_parts = from_even_odd(down_sum_even, down_sum_odd, y_index)
     down_grad = jnp.concatenate(down_parts, axis=0)
-    gate_sum = ring_scatter([mm(p, grad_gate_b, 0, 0) for p in pieces_of(norm2_all, chunk)], 1)
-    up_sum = ring_scatter([mm(p, grad_up_b, 0, 0) for p in pieces_of(norm2_all, chunk)], -1)
+    gate_sum = ring_scatter(
+        [lambda p=p: mm(p, grad_gate_b, 0, 0) for p in pieces_of(norm2_all, chunk)], 1
+    )
+    up_sum = ring_scatter(
+        [lambda p=p: mm(p, grad_up_b, 0, 0) for p in pieces_of(norm2_all, chunk)], -1
+    )
     gate_grad = jnp.concatenate(
         from_even_odd(gate_sum[:row_block], gate_sum[row_block:], y_index), axis=1
     )
@@ -911,6 +915,9 @@
     grad_out = cotangent_own.astype(jnp.float32)
     grad_hidden = grad_out + normalize_back(grad_norm2, unit_two, inv_two, gain_two)
     branch_all = gather_rows(grad_hidden.astype(jnp.bfloat16))
+    activ_late, branch_all = lax.optimization_barrier((activ_b, branch_all))
+    mlp_own = scatter_rows(mm(activ_late, down_full))
+    output = split_order((hidden + mlp_own).astype(jnp.bfloat16), z_index, 1)
     grad_attn = (
         mm(out_full, branch_all, 1, 1)
         .astype(jnp.bfloat16)
@@ -923,23 +930,24 @@
     bias_grad = jnp.sum(bias_sums, axis=1).reshape(3, HD)
     grad_proj = from_heads(proj_parts, z_index).reshape(Z_PARTS, 3, HD, plane_rows)
     grad_proj = grad_proj.transpose(1, 0, 2, 3).reshape(3 * heads_width, plane_rows)
-    grad_norm1 = scatter_rows(mm(grad_proj, qkv_full, 0, 1))
+    norm1_part = mm(grad_proj, qkv_full, 0, 1)
+    grad_norm1 = scatter_rows(norm1_part)
 
     out_sum_even = ring_scatter(
-        [mm(attn_t, p) for p in pieces_of(branch_all, chunk, 0, row_block)], 1
+        [lambda p=p: mm(attn_t, p) for p in pieces_of(branch_all, chunk, 0, row_block)], 1
     )
     out_sum_odd = ring_scatter(
-        [mm(attn_t, p) for p in pieces_of(branch_all, chunk, row_block, row_block)], -1
+        [lambda p=p: mm(attn_t, p) for p in pieces_of(branch_all, chunk, row_block, row_block)], -1
     )
     out_parts = from_even_odd(out_sum_even, out_sum_odd, y_index)
     out_grad = jnp.stack(
         [p.reshape(Z_PARTS, HD, row_block) for p in out_parts], axis=1
     ).reshape(w_out.shape)
     qkv_sum_even = ring_scatter(
-        [mm(p, grad_proj, 0, 1) for p in pieces_of(norm1_all, chunk, 0, row_block)], 1
+        [lambda p=p: mm(p, grad_proj, 0, 1) for p in pieces_of(norm1_all, chunk, 0, row_block)], 1
     )
     qkv_sum_odd = ring_scatter(
-        [mm(p, grad_proj, 0, 1) for p in pieces_of(norm1_all, chunk, row_block, row_block)], -1
+        [lambda p=p: mm(p, grad_proj, 0, 1) for p in pieces_of(norm1_all, chunk, row_block, row_block)], -1
     )
     qkv_grad_parts = from_even_odd(qkv_sum_even, qkv_sum_odd, y_index)
     qkv_grad = jnp.stack(

time: 784 us -> 786 us (level)
  waiting for transfers between devices: 403 us -> 392 us
    ppermute x27, waiting for transfers between devices: 49.1 us -> 38.4 us  [swap_y(): return lax.ppermute(values, 'blk', [(b, b ^ 1) for b in range(2 * Z_PARTS)])]
    unnamed x222 -> x218, local copies, waits for them, and re-layouts: 40.3 us -> 39.3 us
  transfers between devices with their start and end apart: 115 -> 115, of which waited for: 57 -> 49; matrix products, arithmetic and copies ran while one was open for 19% -> 19% of each run, Pallas kernels for 5% -> 5%
where the time goes in v4:
time: 786 us; the launch traced here: 776 us
  waiting for transfers between devices  392 us (50%)
  starting transfers between devices  150 us (19%)
  matrix products  73.7 us (9%)
  local copies, waits for them, and re-layouts  72.8 us (9%)
  other arithmetic  45.8 us (6%)
  Pallas kernels  38.9 us (5%)
    ppermute x61, waiting for transfers between devices, shift_z(): lax.ppermute(values, 'blk', [(b, (b + 2 * amount) % total) for b in range...  320 us
    ppermute x61, starting transfers between devices, shift_z(): lax.ppermute(values, 'blk', [(b, (b + 2 * amount) % total) for b in range...  98.2 us
    dot_general x42, matrix products, mm(): lax.dot_general(left, right, (((left_dim,), (right_dim,)), ((), ())), pre...  73.7 us
    unnamed x218, local copies, waits for them, and re-layouts  39.3 us
    ppermute x27, waiting for transfers between devices, swap_y(): return lax.ppermute(values, 'blk', [(b, b ^ 1) for b in range(2 * Z_PARTS)])  38.4 us
    ppermute x17, waiting for transfers between devices, swap_x(): return lax.ppermute(values, 'head', [(h, h ^ 2) for h in range(4)])  30.8 us
    ppermute x27, starting transfers between devices, swap_y(): return lax.ppermute(values, 'blk', [(b, b ^ 1) for b in range(2 * Z_PARTS)])  28.9 us
    pallas_call x1, Pallas kernels, attend_heads_back(): pl.pallas_call(attend_back_kernel, grid_spec=pltpu.PrefetchScalarGridSpec...  22.4 us
  transfers between devices with their start and end apart: 115, of which 49 were waited for; matrix products, arithmetic and copies ran while one was open for 19% of the time, Pallas kernels for 5%

profile of v4, /device:TPU:0, one launch (start us, length us, event | category | flops | bytes accessed | tf_op | source)
XLA Modules:
  0.0 776.0 jit_solution(12870127500734065059)
XLA Ops:
  32.1 4.1 collective-permute-start.2
  53.0 10.1 %collective-permute-done.1 = bf16[256,768]{1,0:T(8,128)(2,1)} collective-permute-done((bf16[256,768]{1,0:T(8,128)(2,1)}, bf16[256,768]{1,0:T(8,128)(2,1)}, u32[]{:S(2)}, u32[]{:S(2)}) %collective-permute-start.1) | collective-permute-done | bytes 393248 | tf_op jit(solution)/shard_map/ppermute | solution.py:395
  63.2 6.3 collective-permute-done.3
  75.6 18.4 %collective-permute-done.19 = bf16[256,256]{1,0:T(8,128)(2,1)S(1)} collective-permute-done((bf16[256,256]{1,0:T(8,128)(2,1)S(1)}, bf16[256,256]{1,0:T(8,128)(2,1)S(1)}, u32[]{:S(2)}, u32[]{:S(2)}) %collective-permute-start.19) | collective-permute-done | bytes 131104 | tf_op jit(solution)/shard_map/ppermute | solution.py:395
  104.0 7.7 collective-permute-done.6
  125.7 8.2 %collective-permute-done.12 = bf16[192,1024]{1,0:T(8,128)(2,1)S(1)} collective-permute-done((bf16[192,1024]{1,0:T(8,128)(2,1)S(1)}, bf16[192,1024]{1,0:T(8,128)(2,1)S(1)}, u32[]{:S(2)}, u32[]{:S(2)}) %collective-permute-start.12) | collective-permute-done | bytes 393248 | tf_op jit(solution)/shard_map/ppermute | solution.py:395
  134.4 13.8 %collective-permute-done.13 = bf16[192,1024]{1,0:T(8,128)(2,1)S(1)} collective-permute-done((bf16[192,1024]{1,0:T(8,128)(2,1)S(1)}, bf16[192,1024]{1,0:T(8,128)(2,1)S(1)}, u32[]{:S(2)}, u32[]{:S(2)}) %collective-permute-start.13) | collective-permute-done | bytes 393248 | tf_op jit(solution)/shard_map/ppermute | solution.py:395
  148.7 9.4 %collective-permute-start.24 = (bf16[256,256]{1,0:T(8,128)(2,1)S(1)}, bf16[256,256]{1,0:T(8,128)(2,1)S(1)}, u32[]{:S(2)}, u32[]{:S(2)}) collective-permute-start(bf16[256,256]{1,0:T(8,128)(2,1)S(1)} %collective-permute-done.23), channel_id=1, source_target_pairs={{0,2},{1,3},{2,4},{3,5},{4,6},{5,7},{6,0},{7,1},{8,10},{9,11},{10,... | collective-permute-start | bytes 393224 | tf_op jit(solution)/shard_map/ppermute | solution.py:395
  158.3 16.5 %attend.1 = (bf16[4,64,1024]{2,1,0:T(8,128)(2,1)S(1)}, f32[64,4096]{1,0:T(8,128)S(1)}, f32[1,4096]{1,0:T(1,128)S(1)}, bf16[192,4096]{1,0:T(8,128)(2,1)S(1)}) custom-call(s32[32]{0:T(128)S(1)} %select_reduce_fusion.2.slot_ref, s32[8]{0:T(128)S(1)} %and_select_fusion.low_ref, bf16[4,192,1024]{2,1,0:T(8,128)(2,1)S(1)} %pad_maximum_fusion.1.qkv_ref, ...), custom_call_target="tpu_custom_call" | custom-call | flops 1073741824 | bytes 6291456 | tf_op jit(solution)/shard_map/attend/pallas_call | solution.py:673
  175.0 4.9 collective-permute-done.15
  179.9 8.4 %collective-permute-done.16 = bf16[64,1024]{1,0:T(8,128)(2,1)S(1)} collective-permute-done((bf16[64,1024]{1,0:T(8,128)(2,1)S(1)}, bf16[64,1024]{1,0:T(8,128)(2,1)S(1)}, u32[]{:S(2)}, u32[]{:S(2)}) %collective-permute-start.16) | collective-permute-done | bytes 131104 | tf_op jit(solution)/shard_map/ppermute | solution.py:395
  188.3 6.7 collective-permute-done.17
  205.2 6.5 collective-permute-done.35
  224.1 4.1 collective-permute-done.26
  232.1 5.2 collective-permute-done.46
  239.2 36.5 %collective-permute-done.51 = bf16[704,256]{1,0:T(8,128)(2,1)S(1)} collective-permute-done((bf16[704,256]{1,0:T(8,128)(2,1)S(1)}, bf16[704,256]{1,0:T(8,128)(2,1)S(1)}, u32[]{:S(2)}, u32[]{:S(2)}) %collective-permute-start.51) | collective-permute-done | bytes 360480 | tf_op jit(solution)/shard_map/ppermute | solution.py:395
  283.2 5.6 collective-permute-done.52
  295.8 27.3 %collective-permute-done.41 = bf16[512,704]{0,1:T(8,128)(2,1)S(1)} collective-permute-done((bf16[512,704]{0,1:T(8,128)(2,1)S(1)}, bf16[512,704]{0,1:T(8,128)(2,1)S(1)}, u32[]{:S(2)}, u32[]{:S(2)}) %collective-permute-start.41) | collective-permute-done | bytes 720928 | tf_op jit(solution)/shard_map/ppermute | solution.py:395
  327.5 8.8 %collective-permute-done.54 = bf16[704,256]{1,0:T(8,128)(2,1)S(1)} collective-permute-done((bf16[704,256]{1,0:T(8,128)(2,1)S(1)}, bf16[704,256]{1,0:T(8,128)(2,1)S(1)}, u32[]{:S(2)}, u32[]{:S(2)}) %collective-permute-start.54) | collective-permute-done | bytes 360480 | tf_op jit(solution)/shard_map/ppermute | solution.py:395
  336.4 15.1 %collective-permute-done.42 = bf16[512,704]{0,1:T(8,128)(2,1)S(1)} collective-permute-done((bf16[512,704]{0,1:T(8,128)(2,1)S(1)}, bf16[512,704]{0,1:T(8,128)(2,1)S(1)}, u32[]{:S(2)}, u32[]{:S(2)}) %collective-permute-start.42) | collective-permute-done | bytes 720928 | tf_op jit(solution)/shard_map/ppermute | solution.py:395
  351.8 13.8 %collective-permute-done.38 = bf16[512,704]{0,1:T(8,128)(2,1)S(1)} collective-permute-done((bf16[512,704]{0,1:T(8,128)(2,1)S(1)}, bf16[512,704]{0,1:T(8,128)(2,1)S(1)}, u32[]{:S(2)}, u32[]{:S(2)}) %collective-permute-start.38) | collective-permute-done | bytes 720928 | tf_op jit(solution)/shard_map/ppermute | solution.py:395
  365.8 4.8 fusion.161
  370.8 4.8 fusion.160
  375.5 6.0 multiply_convert_fusion.1
  383.6 5.8 fusion.162
  393.9 5.9 convolution_add_fusion
  400.2 8.0 %collective-permute-done.111 = bf16[704,256]{1,0:T(8,128)(2,1)S(1)} collective-permute-done((bf16[704,256]{1,0:T(8,128)(2,1)S(1)}, bf16[704,256]{1,0:T(8,128)(2,1)S(1)}, u32[]{:S(2)}, u32[]{:S(2)}) %collective-permute-start.111) | collective-permute-done | bytes 360480 | tf_op jit(solution)/shard_map/ppermute | solution.py:395
  412.5 38.1 %collective-permute-done.112 = bf16[704,256]{1,0:T(8,128)(2,1)S(1)} collective-permute-done((bf16[704,256]{1,0:T(8,128)(2,1)S(1)}, bf16[704,256]{1,0:T(8,128)(2,1)S(1)}, u32[]{:S(2)}, u32[]{:S(2)}) %collective-permute-start.112) | collective-permute-done | bytes 360480 | tf_op jit(solution)/shard_map/ppermute | solution.py:395
  458.7 11.7 %collective-permute-done.110 = bf16[704,256]{1,0:T(8,128)(2,1)S(1)} collective-permute-done((bf16[704,256]{1,0:T(8,128)(2,1)S(1)}, bf16[704,256]{1,0:T(8,128)(2,1)S(1)}, u32[]{:S(2)}, u32[]{:S(2)}) %collective-permute-start.110) | collective-permute-done | bytes 360480 | tf_op jit(solution)/shard_map/ppermute | solution.py:395
  476.0 4.4 collective-permute-done.114
  480.6 3.9 collective-permute-done.56
  490.9 5.2 collective-permute-start.106
  504.6 6.3 collective-permute-done.61
  523.4 6.6 collective-permute-done.102
  535.1 5.3 collective-permute-done.103
  553.4 6.2 collective-permute-start.96
  559.8 4.3 collective-permute-start.71
  574.8 22.4 %attend_back.1 = (bf16[4,192,1024]{2,1,0:T(8,128)(2,1)S(1)}, f32[192,128]{1,0:T(8,128)S(1)}) custom-call(s32[32]{0:T(128)S(1)} %select_reduce_fusion.2.slot_ref, s32[8]{0:T(128)S(1)} %and_select_fusion.low_ref, bf16[4,64,1024]{2,1,0:T(8,128)(2,1)S(1)} %pad_maximum_fusion.18.grad_ref, bf16[192,4096]{1,0:T(8,128)(2,1)} %copy-done, ...), custom_call_target="tpu_custom_call" | custom-call | flops 3221225472 | bytes 8388608 | tf_op jit(solution)/shard_map/attend_back/pallas_call | solution.py:702
  598.4 6.4 collective-permute-start.73
  620.4 21.9 %collective-permute-done.74 = bf16[192,1024]{1,0:T(8,128)(2,1)S(1)} collective-permute-done((bf16[192,1024]{1,0:T(8,128)(2,1)}, bf16[192,1024]{1,0:T(8,128)(2,1)S(1)}, u32[]{:S(2)}, u32[]{:S(2)}) %collective-permute-start.74) | collective-permute-done | bytes 393248 | tf_op jit(solution)/shard_map/ppermute | solution.py:395
  656.6 14.1 %collective-permute-done.89 = bf16[256,768]{1,0:T(8,128)(2,1)S(1)} collective-permute-done((bf16[256,768]{1,0:T(8,128)(2,1)S(1)}, bf16[256,768]{1,0:T(8,128)(2,1)S(1)}, u32[]{:S(2)}, u32[]{:S(2)}) %collective-permute-start.89) | collective-permute-done | bytes 393248 | tf_op jit(solution)/shard_map/ppermute | solution.py:395
  675.2 13.8 %collective-permute-done.90 = bf16[256,768]{1,0:T(8,128)(2,1)S(1)} collective-permute-done((bf16[256,768]{1,0:T(8,128)(2,1)S(1)}, bf16[256,768]{1,0:T(8,128)(2,1)S(1)}, u32[]{:S(2)}, u32[]{:S(2)}) %collective-permute-start.90) | collective-permute-done | bytes 393248 | tf_op jit(solution)/shard_map/ppermute | solution.py:395
  696.0 9.9 %collective-permute-done.91 = bf16[256,768]{1,0:T(8,128)(2,1)S(1)} collective-permute-done((bf16[256,768]{1,0:T(8,128)(2,1)S(1)}, bf16[256,768]{1,0:T(8,128)(2,1)S(1)}, u32[]{:S(2)}, u32[]{:S(2)}) %collective-permute-start.91) | collective-permute-done | bytes 393248 | tf_op jit(solution)/shard_map/ppermute | solution.py:395
  708.2 4.4 fusion.142
  730.4 4.9 collective-permute-done.77
  738.9 9.2 %collective-permute-done.67 = bf16[128,2048]{1,0:T(8,128)(2,1)S(1)} collective-permute-done((bf16[128,2048]{1,0:T(8,128)(2,1)S(1)}, bf16[128,2048]{1,0:T(8,128)(2,1)S(1)}, u32[]{:S(2)}, u32[]{:S(2)}) %collective-permute-start.67) | collective-permute-done | bytes 524320 | tf_op jit(solution)/shard_map/ppermute | solution.py:382
  750.5 5.0 collective-permute-done.78
  761.8 4.1 collective-permute-start.83
  (610 shorter events, 291.9 us)
Async XLA Ops:
  4.7 34.1 %collective-permute-start.7 = (bf16[128,2048]{1,0:T(8,128)(2,1)}, bf16[128,2048]{1,0:T(8,128)(2,1)}, u32[]{:S(2)}, u32[]{:S(2)}) collective-permute-start(bf16[128,2048]{1,0:T(8,128)(2,1)} %get-tuple-element.126), channel_id=1, source_target_pairs={{0,1},{1,0},{2,3},{3,2},{4,5},{5,4},{6,7},{7,6},{8,9},{9,8},{10,11... | collective-permute-start | bytes 1572872 | tf_op jit(solution)/shard_map/ppermute | solution.py:390
  7.7 28.5 %collective-permute-start.8 = (bf16[128,2048]{1,0:T(8,128)(2,1)}, bf16[128,2048]{1,0:T(8,128)(2,1)}, u32[]{:S(2)}, u32[]{:S(2)}) collective-permute-start(bf16[128,2048]{1,0:T(8,128)(2,1)} %get-tuple-element.126), channel_id=1, source_target_pairs={{0,16},{8,24},{16,0},{24,8},{1,17},{9,25},{17,1},{25,9},{2,18},{10... | collective-permute-start | bytes 1572872 | tf_op jit(solution)/shard_map/ppermute | solution.py:382
  11.7 41.2 %collective-permute-start.18 = (bf16[256,256]{1,0:T(8,128)(2,1)S(1)}, bf16[256,256]{1,0:T(8,128)(2,1)S(1)}, u32[]{:S(2)}, u32[]{:S(2)}) collective-permute-start(bf16[256,256]{1,0:T(8,128)(2,1)S(1)} %bitcast.232), channel_id=1, source_target_pairs={{0,1},{1,0},{2,3},{3,2},{4,5},{5,4},{6,7},{7,6},{8,9},{9,8},{10,11... | collective-permute-start | bytes 393224 | tf_op jit(solution)/shard_map/ppermute | solution.py:390
  47.4 65.9 %collective-permute-start.11 = (bf16[512,2048]{1,0:T(8,128)(2,1)}, bf16[512,2048]{1,0:T(8,128)(2,1)}, u32[]{:S(2)}, u32[]{:S(2)}) collective-permute-start(bf16[512,2048]{1,0:T(8,128)(2,1)} %get-tuple-element.245), channel_id=1, source_target_pairs={{0,8},{8,0},{16,24},{24,16},{1,9},{9,1},{17,25},{25,17},{2,10},{10... | collective-permute-start | bytes 6291464 | tf_op jit(solution)/shard_map/ppermute | solution.py:386
  63.1 34.7 %collective-permute-start.5 = (bf16[256,768]{1,0:T(8,128)(2,1)}, bf16[256,768]{1,0:T(8,128)(2,1)}, u32[]{:S(2)}, u32[]{:S(2)}) collective-permute-start(bf16[256,768]{1,0:T(8,128)(2,1)} %collective-permute-done.1), channel_id=1, source_target_pairs={{0,2},{1,3},{2,4},{3,5},{4,6},{5,7},{6,0},{7,1},{8,10},{9,11},{10,... | collective-permute-start | bytes 1179656 | tf_op jit(solution)/shard_map/ppermute | solution.py:395
  69.5 30.2 %collective-permute-start.4 = (bf16[256,768]{1,0:T(8,128)(2,1)S(1)}, bf16[256,768]{1,0:T(8,128)(2,1)}, u32[]{:S(2)}, u32[]{:S(2)}) collective-permute-start(bf16[256,768]{1,0:T(8,128)(2,1)S(1)} %collective-permute-done.3), channel_id=1, source_target_pairs={{0,6},{1,7},{2,0},{3,1},{4,2},{5,3},{6,4},{7,5},{8,14},{9,15},{10,... | collective-permute-start | bytes 1179656 | tf_op jit(solution)/shard_map/ppermute | solution.py:395
  71.7 22.3 %collective-permute-start.19 = (bf16[256,256]{1,0:T(8,128)(2,1)S(1)}, bf16[256,256]{1,0:T(8,128)(2,1)S(1)}, u32[]{:S(2)}, u32[]{:S(2)}) collective-permute-start(bf16[256,256]{1,0:T(8,128)(2,1)S(1)} %get-tuple-element.242), channel_id=1, source_target_pairs={{0,2},{1,3},{2,4},{3,5},{4,6},{5,7},{6,0},{7,1},{8,10},{9,11},{10,... | collective-permute-start | bytes 393224 | tf_op jit(solution)/shard_map/ppermute | solution.py:395
  72.3 22.0 %collective-permute-start.21 = (bf16[256,256]{1,0:T(8,128)(2,1)S(1)}, bf16[256,256]{1,0:T(8,128)(2,1)S(1)}, u32[]{:S(2)}, u32[]{:S(2)}) collective-permute-start(bf16[256,256]{1,0:T(8,128)(2,1)S(1)} %collective-permute-done.20), channel_id=1, source_target_pairs={{0,6},{1,7},{2,0},{3,1},{4,2},{5,3},{6,4},{7,5},{8,14},{9,15},{10,... | collective-permute-start | bytes 393224 | tf_op jit(solution)/shard_map/ppermute | solution.py:395
  94.0 30.5 %collective-permute-start.23 = (bf16[256,256]{1,0:T(8,128)(2,1)S(1)}, bf16[256,256]{1,0:T(8,128)(2,1)S(1)}, u32[]{:S(2)}, u32[]{:S(2)}) collective-permute-start(bf16[256,256]{1,0:T(8,128)(2,1)S(1)} %collective-permute-done.19), channel_id=1, source_target_pairs={{0,2},{1,3},{2,4},{3,5},{4,6},{5,7},{6,0},{7,1},{8,10},{9,11},{10,... | collective-permute-start | bytes 393224 | tf_op jit(solution)/shard_map/ppermute | solution.py:395
  94.3 29.6 %collective-permute-start.22 = (bf16[256,256]{1,0:T(8,128)(2,1)S(1)}, bf16[256,256]{1,0:T(8,128)(2,1)S(1)}, u32[]{:S(2)}, u32[]{:S(2)}) collective-permute-start(bf16[256,256]{1,0:T(8,128)(2,1)S(1)} %collective-permute-done.21), channel_id=1, source_target_pairs={{0,6},{1,7},{2,0},{3,1},{4,2},{5,3},{6,4},{7,5},{8,14},{9,15},{10,... | collective-permute-start | bytes 393224 | tf_op jit(solution)/shard_map/ppermute | solution.py:395
  120.0 28.2 %collective-permute-start.13 = (bf16[192,1024]{1,0:T(8,128)(2,1)S(1)}, bf16[192,1024]{1,0:T(8,128)(2,1)S(1)}, u32[]{:S(2)}, u32[]{:S(2)}) collective-permute-start(bf16[192,1024]{1,0:T(8,128)(2,1)S(1)} %get-tuple-element.174), channel_id=1, source_target_pairs={{0,4},{1,5},{2,6},{3,7},{4,0},{5,1},{6,2},{7,3},{8,12},{9,13},{10,... | collective-permute-start | bytes 1179656 | tf_op jit(solution)/shard_map/ppermute | solution.py:395
  120.7 28.0 %collective-permute-start.14 = (bf16[192,1024]{1,0:T(8,128)(2,1)S(1)}, bf16[192,1024]{1,0:T(8,128)(2,1)S(1)}, u32[]{:S(2)}, u32[]{:S(2)}) collective-permute-start(bf16[192,1024]{1,0:T(8,128)(2,1)S(1)} %get-tuple-element.173), channel_id=1, source_target_pairs={{0,6},{1,7},{2,0},{3,1},{4,2},{5,3},{6,4},{7,5},{8,14},{9,15},{10,... | collective-permute-start | bytes 1179656 | tf_op jit(solution)/shard_map/ppermute | solution.py:395
  123.9 95.8 %collective-permute-start.43 = (bf16[128,2048]{1,0:T(8,128)(2,1)}, bf16[128,2048]{1,0:T(8,128)(2,1)}, u32[]{:S(2)}, u32[]{:S(2)}) collective-permute-start(bf16[128,2048]{1,0:T(8,128)(2,1)} %get-tuple-element.208), channel_id=1, source_target_pairs={{0,1},{1,0},{2,3},{3,2},{4,5},{5,4},{6,7},{7,6},{8,9},{9,8},{10,11... | collective-permute-start | bytes 1572872 | tf_op jit(solution)/shard_map/ppermute | solution.py:390
  124.5 89.2 %collective-permute-start.44 = (bf16[128,2048]{1,0:T(8,128)(2,1)}, bf16[128,2048]{1,0:T(8,128)(2,1)}, u32[]{:S(2)}, u32[]{:S(2)}) collective-permute-start(bf16[128,2048]{1,0:T(8,128)(2,1)} %get-tuple-element.208), channel_id=1, source_target_pairs={{0,16},{8,24},{16,0},{24,8},{1,17},{9,25},{17,1},{25,9},{2,18},{10... | collective-permute-start | bytes 1572872 | tf_op jit(solution)/shard_map/ppermute | solution.py:382
  133.9 67.0 %collective-permute-start.39 = (bf16[256,704]{0,1:T(8,128)(2,1)}, bf16[256,704]{0,1:T(8,128)(2,1)}, u32[]{:S(2)}, u32[]{:S(2)}) collective-permute-start(bf16[256,704]{0,1:T(8,128)(2,1)} %broadcast_select_fusion.11), channel_id=1, source_target_pairs={{0,1},{1,0},{2,3},{3,2},{4,5},{5,4},{6,7},{7,6},{8,9},{9,8},{10,11... | collective-permute-start | bytes 1081352 | tf_op jit(solution)/shard_map/ppermute | solution.py:390
  148.2 52.4 %collective-permute-start.48 = (bf16[704,256]{1,0:T(8,128)(2,1)}, bf16[704,256]{1,0:T(8,128)(2,1)}, u32[]{:S(2)}, u32[]{:S(2)}) collective-permute-start(bf16[704,256]{1,0:T(8,128)(2,1)} %broadcast_select_fusion.7), channel_id=1, source_target_pairs={{0,1},{1,0},{2,3},{3,2},{4,5},{5,4},{6,7},{7,6},{8,9},{9,8},{10,11... | collective-permute-start | bytes 1081352 | tf_op jit(solution)/shard_map/ppermute | solution.py:390
  148.7 26.2 %collective-permute-start.24 = (bf16[256,256]{1,0:T(8,128)(2,1)S(1)}, bf16[256,256]{1,0:T(8,128)(2,1)S(1)}, u32[]{:S(2)}, u32[]{:S(2)}) collective-permute-start(bf16[256,256]{1,0:T(8,128)(2,1)S(1)} %collective-permute-done.23), channel_id=1, source_target_pairs={{0,2},{1,3},{2,4},{3,5},{4,6},{5,7},{6,0},{7,1},{8,10},{9,11},{10,... | collective-permute-start | bytes 393224 | tf_op jit(solution)/shard_map/ppermute | solution.py:395
  200.9 29.5 %collective-permute-start.49 = (bf16[704,256]{1,0:T(8,128)(2,1)S(1)}, bf16[704,256]{1,0:T(8,128)(2,1)S(1)}, u32[]{:S(2)}, u32[]{:S(2)}) collective-permute-start(bf16[704,256]{1,0:T(8,128)(2,1)S(1)} %get-tuple-element.110), channel_id=1, source_target_pairs={{0,2},{1,3},{2,4},{3,5},{4,6},{5,7},{6,0},{7,1},{8,10},{9,11},{10,... | collective-permute-start | bytes 1081352 | tf_op jit(solution)/shard_map/ppermute | solution.py:395
  229.5 49.1 %collective-permute-start.27 = (bf16[128,2048]{1,0:T(8,128)(2,1)S(1)}, bf16[128,2048]{1,0:T(8,128)(2,1)S(1)}, u32[]{:S(2)}, u32[]{:S(2)}) collective-permute-start(bf16[128,2048]{1,0:T(8,128)(2,1)S(1)} %pad_maximum_fusion.10), channel_id=1, source_target_pairs={{0,16},{8,24},{16,0},{24,8},{1,17},{9,25},{17,1},{25,9},{2,18},{10... | collective-permute-start | bytes 1572872 | tf_op jit(solution)/shard_map/ppermute | solution.py:382
  230.5 49.0 %collective-permute-start.29 = (bf16[128,2048]{1,0:T(8,128)(2,1)S(1)}, bf16[128,2048]{1,0:T(8,128)(2,1)S(1)}, u32[]{:S(2)}, u32[]{:S(2)}) collective-permute-start(bf16[128,2048]{1,0:T(8,128)(2,1)S(1)} %pad_maximum_fusion.11), channel_id=1, source_target_pairs={{0,1},{1,0},{2,3},{3,2},{4,5},{5,4},{6,7},{7,6},{8,9},{9,8},{10,11... | collective-permute-start | bytes 1572872 | tf_op jit(solution)/shard_map/ppermute | solution.py:390
  231.2 57.6 %collective-permute-start.40 = (bf16[512,704]{0,1:T(8,128)(2,1)S(1)}, bf16[512,704]{0,1:T(8,128)(2,1)S(1)}, u32[]{:S(2)}, u32[]{:S(2)}) collective-permute-start(bf16[512,704]{0,1:T(8,128)(2,1)S(1)} %pad_maximum_fusion.8), channel_id=1, source_target_pairs={{0,6},{1,7},{2,0},{3,1},{4,2},{5,3},{6,4},{7,5},{8,14},{9,15},{10,... | collective-permute-start | bytes 2162696 | tf_op jit(solution)/shard_map/ppermute | solution.py:395
  231.3 44.4 %collective-permute-start.51 = (bf16[704,256]{1,0:T(8,128)(2,1)S(1)}, bf16[704,256]{1,0:T(8,128)(2,1)S(1)}, u32[]{:S(2)}, u32[]{:S(2)}) collective-permute-start(bf16[704,256]{1,0:T(8,128)(2,1)S(1)} %collective-permute-done.50), channel_id=1, source_target_pairs={{0,6},{1,7},{2,0},{3,1},{4,2},{5,3},{6,4},{7,5},{8,14},{9,15},{10,... | collective-permute-start | bytes 1081352 | tf_op jit(solution)/shard_map/ppermute | solution.py:395
  237.4 44.6 %collective-permute-start.36 = (bf16[512,704]{0,1:T(8,128)(2,1)S(1)}, bf16[512,704]{0,1:T(8,128)(2,1)S(1)}, u32[]{:S(2)}, u32[]{:S(2)}) collective-permute-start(bf16[512,704]{0,1:T(8,128)(2,1)S(1)} %pad_maximum_fusion.7), channel_id=1, source_target_pairs={{0,2},{1,3},{2,4},{3,5},{4,6},{5,7},{6,0},{7,1},{8,10},{9,11},{10,... | collective-permute-start | bytes 2162696 | tf_op jit(solution)/shard_map/ppermute | solution.py:395
  288.8 76.9 %collective-permute-start.47 = (bf16[512,2048]{1,0:T(8,128)(2,1)S(1)}, bf16[512,2048]{1,0:T(8,128)(2,1)S(1)}, u32[]{:S(2)}, u32[]{:S(2)}) collective-permute-start(bf16[512,2048]{1,0:T(8,128)(2,1)S(1)} %get-tuple-element.233), channel_id=1, source_target_pairs={{0,8},{8,0},{16,24},{24,16},{1,9},{9,1},{17,25},{25,17},{2,10},{10... | collective-permute-start | bytes 6291464 | tf_op jit(solution)/shard_map/ppermute | solution.py:386
  288.8 38.4 %collective-permute-start.37 = (bf16[512,704]{0,1:T(8,128)(2,1)S(1)}, bf16[512,704]{0,1:T(8,128)(2,1)S(1)}, u32[]{:S(2)}, u32[]{:S(2)}) collective-permute-start(bf16[512,704]{0,1:T(8,128)(2,1)S(1)} %collective-permute-done.36), channel_id=1, source_target_pairs={{0,2},{1,3},{2,4},{3,5},{4,6},{5,7},{6,0},{7,1},{8,10},{9,11},{10,... | collective-permute-start | bytes 2162696 | tf_op jit(solution)/shard_map/ppermute | solution.py:395
  289.4 33.7 %collective-permute-start.41 = (bf16[512,704]{0,1:T(8,128)(2,1)S(1)}, bf16[512,704]{0,1:T(8,128)(2,1)S(1)}, u32[]{:S(2)}, u32[]{:S(2)}) collective-permute-start(bf16[512,704]{0,1:T(8,128)(2,1)S(1)} %collective-permute-done.40), channel_id=1, source_target_pairs={{0,6},{1,7},{2,0},{3,1},{4,2},{5,3},{6,4},{7,5},{8,14},{9,15},{10,... | collective-permute-start | bytes 2162696 | tf_op jit(solution)/shard_map/ppermute | solution.py:395
  292.9 32.0 %collective-permute-start.32 = (bf16[64,2048]{1,0:T(8,128)(2,1)S(1)}, bf16[64,2048]{1,0:T(8,128)(2,1)S(1)}, u32[]{:S(2)}, u32[]{:S(2)}) collective-permute-start(bf16[64,2048]{1,0:T(8,128)(2,1)S(1)} %slice.503), channel_id=1, source_target_pairs={{0,1},{1,0},{2,3},{3,2},{4,5},{5,4},{6,7},{7,6},{8,9},{9,8},{10,11... | collective-permute-start | bytes 786440 | tf_op jit(solution)/shard_map/ppermute | solution.py:390
  294.4 32.6 %collective-permute-start.33 = (bf16[64,2048]{1,0:T(8,128)(2,1)S(1)}, bf16[64,2048]{1,0:T(8,128)(2,1)S(1)}, u32[]{:S(2)}, u32[]{:S(2)}) collective-permute-start(bf16[64,2048]{1,0:T(8,128)(2,1)S(1)} %slice.504), channel_id=1, source_target_pairs={{0,16},{8,24},{16,0},{24,8},{1,17},{9,25},{17,1},{25,9},{2,18},{10... | collective-permute-start | bytes 786440 | tf_op jit(solution)/shard_map/ppermute | solution.py:382
  324.9 26.7 %collective-permute-start.42 = (bf16[512,704]{0,1:T(8,128)(2,1)S(1)}, bf16[512,704]{0,1:T(8,128)(2,1)S(1)}, u32[]{:S(2)}, u32[]{:S(2)}) collective-permute-start(bf16[512,704]{0,1:T(8,128)(2,1)S(1)} %collective-permute-done.41), channel_id=1, source_target_pairs={{0,6},{1,7},{2,0},{3,1},{4,2},{5,3},{6,4},{7,5},{8,14},{9,15},{10,... | collective-permute-start | bytes 2162696 | tf_op jit(solution)/shard_map/ppermute | solution.py:395
  327.1 43.5 %collective-permute-start.34 = (bf16[512,2048]{1,0:T(8,128)(2,1)S(1)}, bf16[512,2048]{1,0:T(8,128)(2,1)S(1)}, u32[]{:S(2)}, u32[]{:S(2)}) collective-permute-start(bf16[512,2048]{1,0:T(8,128)(2,1)S(1)} %get-tuple-element.237), channel_id=1, source_target_pairs={{0,8},{8,0},{16,24},{24,16},{1,9},{9,1},{17,25},{25,17},{2,10},{10... | collective-permute-start | bytes 6291464 | tf_op jit(solution)/shard_map/ppermute | solution.py:386
  327.2 38.3 %collective-permute-start.38 = (bf16[512,704]{0,1:T(8,128)(2,1)S(1)}, bf16[512,704]{0,1:T(8,128)(2,1)S(1)}, u32[]{:S(2)}, u32[]{:S(2)}) collective-permute-start(bf16[512,704]{0,1:T(8,128)(2,1)S(1)} %collective-permute-done.37), channel_id=1, source_target_pairs={{0,2},{1,3},{2,4},{3,5},{4,6},{5,7},{6,0},{7,1},{8,10},{9,11},{10,... | collective-permute-start | bytes 2162696 | tf_op jit(solution)/shard_map/ppermute | solution.py:395
  391.4 62.5 %collective-permute-start.104 = (bf16[512,704]{0,1:T(8,128)(2,1)S(1)}, bf16[512,704]{0,1:T(8,128)(2,1)S(1)}, u32[]{:S(2)}, u32[]{:S(2)}) collective-permute-start(bf16[512,704]{0,1:T(8,128)(2,1)S(1)} %convolution_convert_fusion), channel_id=1, source_target_pairs={{0,6},{1,7},{2,0},{3,1},{4,2},{5,3},{6,4},{7,5},{8,14},{9,15},{10,... | collective-permute-start | bytes 2162696 | tf_op jit(solution)/shard_map/ppermute | solution.py:395
  400.1 72.8 %collective-permute-start.55 = (bf16[512,2048]{1,0:T(8,128)(2,1)S(1)}, bf16[512,2048]{1,0:T(8,128)(2,1)S(1)}, u32[]{:S(2)}, u32[]{:S(2)}) collective-permute-start(bf16[512,2048]{1,0:T(8,128)(2,1)S(1)} %slice.776), channel_id=1, source_target_pairs={{0,8},{8,0},{16,24},{24,16},{1,9},{9,1},{17,25},{25,17},{2,10},{10... | collective-permute-start | bytes 6291464 | tf_op jit(solution)/shard_map/ppermute | solution.py:386
  408.8 41.8 %collective-permute-start.112 = (bf16[704,256]{1,0:T(8,128)(2,1)S(1)}, bf16[704,256]{1,0:T(8,128)(2,1)S(1)}, u32[]{:S(2)}, u32[]{:S(2)}) collective-permute-start(bf16[704,256]{1,0:T(8,128)(2,1)S(1)} %add_convert_fusion.10), channel_id=1, source_target_pairs={{0,6},{1,7},{2,0},{3,1},{4,2},{5,3},{6,4},{7,5},{8,14},{9,15},{10,... | collective-permute-start | bytes 1081352 | tf_op jit(solution)/shard_map/ppermute | solution.py:395
  409.5 41.8 %collective-permute-start.109 = (bf16[704,256]{1,0:T(8,128)(2,1)S(1)}, bf16[704,256]{1,0:T(8,128)(2,1)S(1)}, u32[]{:S(2)}, u32[]{:S(2)}) collective-permute-start(bf16[704,256]{1,0:T(8,128)(2,1)S(1)} %add_convert_fusion.12), channel_id=1, source_target_pairs={{0,2},{1,3},{2,4},{3,5},{4,6},{5,7},{6,0},{7,1},{8,10},{9,11},{10,... | collective-permute-start | bytes 1081352 | tf_op jit(solution)/shard_map/ppermute | solution.py:395
  412.5 45.0 %collective-permute-start.100 = (bf16[512,704]{0,1:T(8,128)(2,1)S(1)}, bf16[512,704]{0,1:T(8,128)(2,1)S(1)}, u32[]{:S(2)}, u32[]{:S(2)}) collective-permute-start(bf16[512,704]{0,1:T(8,128)(2,1)S(1)} %convolution_convert_fusion.1), channel_id=1, source_target_pairs={{0,2},{1,3},{2,4},{3,5},{4,6},{5,7},{6,0},{7,1},{8,10},{9,11},{10,... | collective-permute-start | bytes 2162696 | tf_op jit(solution)/shard_map/ppermute | solution.py:395
  455.7 33.1 %collective-permute-start.105 = (bf16[512,704]{0,1:T(8,128)(2,1)}, bf16[512,704]{0,1:T(8,128)(2,1)}, u32[]{:S(2)}, u32[]{:S(2)}) collective-permute-start(bf16[512,704]{0,1:T(8,128)(2,1)} %add_convert_fusion.1), channel_id=1, source_target_pairs={{0,6},{1,7},{2,0},{3,1},{4,2},{5,3},{6,4},{7,5},{8,14},{9,15},{10,... | collective-permute-start | bytes 2162696 | tf_op jit(solution)/shard_map/ppermute | solution.py:395
  458.4 42.9 %collective-permute-start.101 = (bf16[512,704]{0,1:T(8,128)(2,1)S(1)}, bf16[512,704]{0,1:T(8,128)(2,1)S(1)}, u32[]{:S(2)}, u32[]{:S(2)}) collective-permute-start(bf16[512,704]{0,1:T(8,128)(2,1)S(1)} %add_convert_fusion.3), channel_id=1, source_target_pairs={{0,2},{1,3},{2,4},{3,5},{4,6},{5,7},{6,0},{7,1},{8,10},{9,11},{10,... | collective-permute-start | bytes 2162696 | tf_op jit(solution)/shard_map/ppermute | solution.py:395
  490.9 30.8 %collective-permute-start.106 = (bf16[512,704]{0,1:T(8,128)(2,1)S(1)}, bf16[512,704]{0,1:T(8,128)(2,1)S(1)}, u32[]{:S(2)}, u32[]{:S(2)}) collective-permute-start(bf16[512,704]{0,1:T(8,128)(2,1)S(1)} %add_convert_fusion), channel_id=1, source_target_pairs={{0,6},{1,7},{2,0},{3,1},{4,2},{5,3},{6,4},{7,5},{8,14},{9,15},{10,... | collective-permute-start | bytes 2162696 | tf_op jit(solution)/shard_map/ppermute | solution.py:395
  502.3 27.8 %collective-permute-start.102 = (bf16[512,704]{0,1:T(8,128)(2,1)S(1)}, bf16[512,704]{0,1:T(8,128)(2,1)S(1)}, u32[]{:S(2)}, u32[]{:S(2)}) collective-permute-start(bf16[512,704]{0,1:T(8,128)(2,1)S(1)} %add_convert_fusion.2), channel_id=1, source_target_pairs={{0,2},{1,3},{2,4},{3,5},{4,6},{5,7},{6,0},{7,1},{8,10},{9,11},{10,... | collective-permute-start | bytes 2162696 | tf_op jit(solution)/shard_map/ppermute | solution.py:395
  519.7 23.9 %collective-permute-start.64 = (bf16[512,2048]{1,0:T(8,128)(2,1)}, bf16[512,2048]{1,0:T(8,128)(2,1)}, u32[]{:S(2)}, u32[]{:S(2)}) collective-permute-start(bf16[512,2048]{1,0:T(8,128)(2,1)} %get-tuple-element.229), channel_id=1, source_target_pairs={{0,8},{8,0},{16,24},{24,16},{1,9},{9,1},{17,25},{25,17},{2,10},{10... | collective-permute-start | bytes 6291464 | tf_op jit(solution)/shard_map/ppermute | solution.py:386
  569.5 35.3 %collective-permute-start.97 = (bf16[256,256]{1,0:T(8,128)(2,1)S(1)}, bf16[256,256]{1,0:T(8,128)(2,1)S(1)}, u32[]{:S(2)}, u32[]{:S(2)}) collective-permute-start(bf16[256,256]{1,0:T(8,128)(2,1)S(1)} %add_convert_fusion.14), channel_id=1, source_target_pairs={{0,6},{1,7},{2,0},{3,1},{4,2},{5,3},{6,4},{7,5},{8,14},{9,15},{10,... | collective-permute-start | bytes 393224 | tf_op jit(solution)/shard_map/ppermute | solution.py:395
  572.3 33.9 %collective-permute-start.94 = (bf16[256,256]{1,0:T(8,128)(2,1)S(1)}, bf16[256,256]{1,0:T(8,128)(2,1)S(1)}, u32[]{:S(2)}, u32[]{:S(2)}) collective-permute-start(bf16[256,256]{1,0:T(8,128)(2,1)S(1)} %add_convert_fusion.16), channel_id=1, source_target_pairs={{0,2},{1,3},{2,4},{3,5},{4,6},{5,7},{6,0},{7,1},{8,10},{9,11},{10,... | collective-permute-start | bytes 393224 | tf_op jit(solution)/shard_map/ppermute | solution.py:395
  613.4 94.8 %collective-permute-start.65 = (bf16[512,2048]{1,0:T(8,128)(2,1)}, bf16[512,2048]{1,0:T(8,128)(2,1)}, u32[]{:S(2)}, u32[]{:S(2)}) collective-permute-start(bf16[512,2048]{1,0:T(8,128)(2,1)} %slice.775), channel_id=1, source_target_pairs={{0,8},{8,0},{16,24},{24,16},{1,9},{9,1},{17,25},{25,17},{2,10},{10... | collective-permute-start | bytes 6291464 | tf_op jit(solution)/shard_map/ppermute | solution.py:386
  613.4 28.9 %collective-permute-start.74 = (bf16[192,1024]{1,0:T(8,128)(2,1)}, bf16[192,1024]{1,0:T(8,128)(2,1)S(1)}, u32[]{:S(2)}, u32[]{:S(2)}) collective-permute-start(bf16[192,1024]{1,0:T(8,128)(2,1)} %get-tuple-element.170), channel_id=1, source_target_pairs={{0,4},{1,5},{2,6},{3,7},{4,0},{5,1},{6,2},{7,3},{8,12},{9,13},{10,... | collective-permute-start | bytes 1179656 | tf_op jit(solution)/shard_map/ppermute | solution.py:395
  614.2 28.9 %collective-permute-start.75 = (bf16[192,1024]{1,0:T(8,128)(2,1)}, bf16[192,1024]{1,0:T(8,128)(2,1)S(1)}, u32[]{:S(2)}, u32[]{:S(2)}) collective-permute-start(bf16[192,1024]{1,0:T(8,128)(2,1)} %get-tuple-element.168), channel_id=1, source_target_pairs={{0,2},{1,3},{2,4},{3,5},{4,6},{5,7},{6,0},{7,1},{8,10},{9,11},{10,... | collective-permute-start | bytes 1179656 | tf_op jit(solution)/shard_map/ppermute | solution.py:395
  618.0 56.1 %collective-permute-start.99 = (bf16[256,256]{1,0:T(8,128)(2,1)S(1)}, bf16[256,256]{1,0:T(8,128)(2,1)S(1)}, u32[]{:S(2)}, u32[]{:S(2)}) collective-permute-start(bf16[256,256]{1,0:T(8,128)(2,1)S(1)} %get-tuple-element.281), channel_id=1, source_target_pairs={{0,1},{1,0},{2,3},{3,2},{4,5},{5,4},{6,7},{7,6},{8,9},{9,8},{10,11... | collective-permute-start | bytes 393224 | tf_op jit(solution)/shard_map/ppermute | solution.py:390
  695.3 27.0 %collective-permute-start.76 = (bf16[512,2048]{1,0:T(8,128)(2,1)}, bf16[512,2048]{1,0:T(8,128)(2,1)}, u32[]{:S(2)}, u32[]{:S(2)}) collective-permute-start(bf16[512,2048]{1,0:T(8,128)(2,1)} %slice.774), channel_id=1, source_target_pairs={{0,8},{8,0},{16,24},{24,16},{1,9},{9,1},{17,25},{25,17},{2,10},{10... | collective-permute-start | bytes 6291464 | tf_op jit(solution)/shard_map/ppermute | solution.py:386
  (148 other events, 3226.0 us)
